TPU v7x, 32 devices: a whole 2x2x4 slice. The times are simulated.
32 devices in a mesh: gx: 8 (over z, y), gy: 4 (over x, core).
Axes of the slice: x: 2, y: 2, z: 4, core: 2. Of those that a mesh axis runs over, the one named last changes fastest.
Arguments:
- velocity_u: float32 [512, 16, 2048], P('gx', None, 'gy'), may hold values from -6 to 6
- wall_strain: float32 [512, 16, 2048], P('gx', None, 'gy'), may hold values from -6 to 6
- damping: float32 [16, 2048], P(None, 'gy'), may hold values from 0.88 to 1
Outputs:
- second_deriv: float32 [512, 16, 2048], P('gx', None, 'gy')
- cosine_coeffs: float32 [512, 16, 2048], P('gx', None, 'gy')
- pressure: float32 [512, 16, 2048], P('gx', None, 'gy')
All inputs are finite; a program needn't handle non-finite values.
Results may differ from a plain program's by a relative error of at most 0.0003.
Values sent between devices are 32-bit elements; how exact they have to be, the bound alone decides.
No kernel may reach another device: no remote copies, remote signals or barrier semaphores. Data moves between devices by JAX's collectives and lax.ppermute only.
A program may use at most 128 MiB of HBM per device.

v0:
```python
import functools
import math

import jax
import jax.numpy as jnp
from jax import lax
from jax.experimental import pallas as pl
from jax.experimental.pallas import tpu as pltpu
from jax.sharding import PartitionSpec as P


LANES = 128
REACH = 3
F32 = jnp.float32
BF16 = jnp.bfloat16
MIB = 1024 * 1024


def params(limit=16 * MIB):
    return pltpu.CompilerParams(vmem_limit_bytes=limit)


def vmem(count):
    return [pl.BlockSpec(memory_space=pltpu.VMEM)] * count


def smem(count):
    return [pl.BlockSpec(memory_space=pltpu.SMEM)] * count


def hbm(count):
    return [pl.BlockSpec(memory_space=pltpu.HBM)] * count


def partner(x, axis, bit):
    count = lax.axis_size(axis)
    return lax.ppermute(x, axis, [(i, i ^ bit) for i in range(count)])


def chunks(sub):
    later = max(sub // 4, REACH)
    return sub - later, later


def chunk_start(block, h, sub):
    first, later = chunks(sub)
    return block * sub + (jnp.where(block == 0, later, 0) if h == 0 else jnp.where(block == 0, 0, first))


def derivatives(cell, at):
    c = [cell(at + k) for k in range(2 * REACH + 1)]
    first = 0.75 * (c[4] - c[2]) - 3.0 / 20.0 * (c[5] - c[1]) + 1.0 / 60.0 * (c[6] - c[0])
    second = (
        1.5 * (c[4] + c[2])
        - 3.0 / 20.0 * (c[5] + c[1])
        + 1.0 / 90.0 * (c[6] + c[0])
        - 49.0 / 18.0 * c[3]
    )
    return first, second


def lead_kernel(fold, idx, u_in, wall_in, damping_in, *refs):
    sends, (near, far, u, wall, damping, sems) = refs[: fold - 1], refs[fold - 1 :]
    cells = u.shape[0]
    sub = cells // fold
    size = chunks(sub)[0]
    me, row = idx[0], idx[1]
    order = list(range(fold - 1, -1, -1))
    rows = {r: pl.ds((me ^ r) * sub, sub) for r in order}
    u_copies = [pltpu.make_async_copy(u_in.at[rows[r]], u.at[rows[r]], sems.at[0, r]) for r in order]
    w_copies = {r: pltpu.make_async_copy(wall_in.at[rows[r]], wall.at[rows[r]], sems.at[1, r]) for r in order}
    d_copy = pltpu.make_async_copy(damping_in, damping, sems.at[2, 0])
    for copy in u_copies:
        copy.start()
    d_copy.start()
    for r in order:
        w_copies[r].start()
    for copy in u_copies:
        copy.wait()
    even = row % 2 == 0
    near[...] = u[pl.ds(jnp.where(even, cells - REACH, 0), REACH)]
    far[...] = u[pl.ds(jnp.where(even, 0, cells - REACH), REACH)]
    d_copy.wait()
    for r in order[:-1]:
        start = chunk_start(me ^ r, 0, sub)
        w_copies[r].wait()

        def step(j, _, r=r, start=start):
            first, _ = derivatives(lambda k: u[k], start - REACH + j)
            sends[r - 1][j] = first + wall[start + j]
            return 0

        lax.fori_loop(0, size, step, 0, unroll=2)
        sends[r - 1][size] = damping[...]
    w_copies[0].wait()


def lead(fold, idx, u, wall, damping):
    cells, planes, cols = u.shape
    size = chunks(cells // fold)[0]
    shape = lambda n: jax.ShapeDtypeStruct((n, planes, cols), F32)
    outs = [shape(size + 1)] * (fold - 1) + [shape(REACH)] * 2 + [shape(cells)] * 2
    outs += [jax.ShapeDtypeStruct((planes, cols), F32)]
    return pl.pallas_call(
        functools.partial(lead_kernel, fold),
        out_shape=outs,
        in_specs=smem(1) + hbm(3),
        out_specs=vmem(len(outs)),
        scratch_shapes=[pltpu.SemaphoreType.DMA((3, fold))],
        compiler_params=params(),
        cost_estimate=pl.CostEstimate(flops=cells * planes * cols * 6, bytes_accessed=cells * planes * cols * 6, transcendentals=0),
        name="lead",
    )(idx, u, wall, damping)


def stencil_kernel(fold, idx, u, wall, near, far, second_out, *refs):
    own, sends, (pad, second, out_sems) = refs[0], refs[1:fold], refs[fold:]
    cells = u.shape[0]
    sub = cells // fold
    sizes = chunks(sub)
    me = idx[0]
    even = idx[1] % 2 == 0
    pad[pl.ds(REACH, cells)] = u[...]
    pad[pl.ds(0, REACH)] = jnp.where(even, far[...], near[...])
    pad[pl.ds(REACH + cells, REACH)] = jnp.where(even, near[...], far[...])
    out_copies = []
    for r in range(fold - 1, -1, -1):
        block = me ^ r
        for h in (1, 0):
            start = chunk_start(block, h, sub)

            def step(j, _, r=r, h=h, start=start):
                first, second[start + j] = derivatives(lambda k: pad[k], start + j)
                if r == 0:
                    own[h * sizes[0] + j] = first + wall[start + j]
                elif h == 1:
                    sends[r - 1][j] = first + wall[start + j]
                return 0

            lax.fori_loop(0, sizes[h], step, 0, unroll=2)
        rows = pl.ds(block * sub, sub)
        copy = pltpu.make_async_copy(second.at[rows], second_out.at[rows], out_sems.at[r])
        copy.start()
        out_copies.append(copy)
    for copy in out_copies:
        copy.wait()


def stencil(fold, idx, u, wall, near, far):
    cells, planes, cols = u.shape
    sub = cells // fold
    later = chunks(sub)[1]
    shape = lambda n: jax.ShapeDtypeStruct((n, planes, cols), F32)
    outs = [shape(cells), shape(sub)] + [shape(later)] * (fold - 1)
    return pl.pallas_call(
        functools.partial(stencil_kernel, fold),
        out_shape=outs,
        in_specs=smem(1) + vmem(4),
        out_specs=hbm(1) + vmem(len(outs) - 1),
        scratch_shapes=[
            pltpu.VMEM((cells + 2 * REACH, planes, cols), F32),
            pltpu.VMEM((cells, planes, cols), F32),
            pltpu.SemaphoreType.DMA((fold,)),
        ],
        compiler_params=params(),
        cost_estimate=pl.CostEstimate(flops=cells * planes * cols * 20, bytes_accessed=cells * planes * cols * 16, transcendentals=0),
        name="stencil",
    )(idx, u, wall, near, far)


def exchange_edges(near, far):
    count = lax.axis_size("gx")
    inner = [(i, i + 1) for i in range(1, count - 1, 2)]
    far = lax.ppermute(far, "gx", inner + [(b, a) for a, b in inner])
    return partner(near, "gx", 1), far


def half_turn(phase, total):
    phase = phase - jnp.floor(phase * (1.0 / (4 * total))) * (4.0 * total)
    x = (jnp.abs(phase - 2.0 * total) - total) * (math.pi / (2.0 * total))
    s = x * x
    y = -1.0 / 39916800.0
    for coefficient in (1.0 / 362880.0, -1.0 / 5040.0, 1.0 / 120.0, -1.0 / 6.0, 1.0):
        y = y * s + coefficient
    return y * x


def table_kernel(total, cols, fold, chunk, idx, *outs):
    rows, width = outs[0].shape
    me = idx[0]
    modes = width // fold
    group = 8
    whole = lambda *shape: lambda axis: lax.broadcasted_iota(jnp.int32, shape, axis)
    base, inner, outer = whole(group, LANES), whole(chunk // group, LANES), whole(rows // chunk, LANES)
    at = outer(0) * chunk
    block = at // cols
    shifts = ((me ^ block) * cols + (at - block * cols)).astype(F32) * 2.0
    steps = (inner(0) * (2 * group)).astype(F32)
    sample = base(0).astype(F32) * 2.0 + 1.0

    def both(phase):
        return half_turn(phase, total), half_turn(phase - total, total)

    def column(c, _):
        r = c * LANES // modes
        first = (me ^ r) * modes + (c * LANES - r * modes)
        for parity in range(2):
            mode = lambda iota: (first + iota(1)).astype(F32) * 2.0 + parity
            c0, s0 = (v * math.sqrt(2.0 / total) for v in both(sample * mode(base)))
            ci, si = both(steps * mode(inner))
            co, so = both(shifts * mode(outer))
            cosine = jnp.concatenate([c0 * ci[i : i + 1] - s0 * si[i : i + 1] for i in range(chunk // group)])
            sine = jnp.concatenate([s0 * ci[i : i + 1] + c0 * si[i : i + 1] for i in range(chunk // group)])
            for i in range(rows // chunk):
                y = cosine * co[i : i + 1] - sine * so[i : i + 1]
                high = y.astype(BF16)
                place = (pl.ds(i * chunk, chunk), pl.ds(pl.multiple_of(c * LANES, LANES), LANES))
                outs[2 * parity][place] = high
                outs[2 * parity + 1][place] = (y - high.astype(F32)).astype(BF16)
        return 0

    lax.fori_loop(0, width // LANES, column, 0)


def cosine_tables(fold, idx, cols):
    total = fold * cols
    side = total // 2
    return pl.pallas_call(
        functools.partial(table_kernel, total, cols, fold, 128),
        out_shape=[jax.ShapeDtypeStruct((side, side), BF16)] * 4,
        in_specs=smem(1),
        out_specs=vmem(4),
        compiler_params=params(),
        cost_estimate=pl.CostEstimate(flops=side * side * 60, bytes_accessed=side * side * 8, transcendentals=0),
        name="table",
    )(idx)


def weight_of(d):
    t = (1.0 - d) * (1.0 + d)
    return t * jnp.sqrt(t)


def lane_pick(x, index):
    return jnp.take_along_axis(x, index, axis=1)


def transform_kernel(fold, at, sizes, cuts, last, idx, *refs):
    take = iter(refs)
    xs = [next(take) for _ in range(fold)]
    tables = [next(take) for _ in range(4)]
    if last:
        damp = next(take)
        earlier = next(take)
    else:
        own_damp = next(take)
    outs = [[next(take) for _ in pieces] for pieces in cuts]
    if last:
        ends = [next(take) for _ in range(fold)]
    else:
        damp = next(take)
        ends_all = next(take)
    parts = [next(take) for _ in range(2)]
    half = sizes[last]
    planes, cols = xs[1].shape[1:]
    lane = lax.broadcasted_iota(jnp.int32, (planes, LANES), 1)
    tiles = cols // LANES

    def fold_cell(j, _):
        for p in range(fold // 2):
            a, b = xs[p], xs[fold - 1 - p]
            for t in range(tiles):
                x = a[j + (at if p == 0 else 0), :, pl.ds(t * LANES, LANES)]
                y = b[j, :, pl.ds((tiles - 1 - t) * LANES, LANES)]
                y = lane_pick(y, LANES - 1 - lane)
                for parity in range(2):
                    v = x - y if parity else x + y
                    high = v.astype(BF16)
                    columns = pl.ds(p * cols + t * LANES, LANES)
                    place = pl.multiple_of(j * planes, planes)
                    parts[parity][pl.ds(place, planes), columns] = high
                    parts[parity][pl.ds(half * planes + place, planes), columns] = (v - high.astype(F32)).astype(BF16)
        return 0

    lax.fori_loop(0, half, fold_cell, 0)
    if not last:
        damp[0] = own_damp[...]
        for r in range(1, fold):
            damp[r] = xs[r][half]

    rows = half * planes
    modes = cols // 2
    wide = lax.broadcasted_iota(jnp.int32, (rows, LANES), 1)
    for r in range(fold):
        columns = pl.ds(r * modes, modes)
        sums = []
        for parity in range(2):
            dot = functools.partial(jnp.dot, preferred_element_type=F32)
            both = dot(parts[parity][...], tables[2 * parity][:, columns])
            rest = dot(parts[parity][:rows], tables[2 * parity + 1][:, columns])
            sums.append(both[:rows] + both[rows:] + rest)
        for t in range(tiles):
            source = slice((t // 2) * LANES, (t // 2 + 1) * LANES)
            index = wide // 2 + (t % 2) * (LANES // 2)
            even, odd = (lane_pick(s[:, source], index) for s in sums)
            tile = jnp.where(wide % 2 == 0, even, odd)
            tile = tile.reshape(half, planes, LANES)
            for out, (low, high) in zip(outs[r], cuts[r]):
                out[:, :, pl.ds(t * LANES, LANES)] = tile[low:high]

    for r in range(fold):
        for t in range(tiles):
            at_lanes = pl.ds(t * LANES, LANES)
            d = damp[r, :, at_lanes]
            w = weight_of(d)
            f = jnp.zeros_like(d)
            forward = []
            for out, (low, high) in zip(outs[r], cuts[r]):
                for j in range(high - low):
                    f = w * out[j, :, at_lanes] + d * f
                    forward.append(f)
            p = jnp.zeros_like(d)
            for j in reversed(range(half)):
                p = forward[j] + d * p
            if last:
                f0, p0 = earlier[0, r, :, at_lanes], earlier[1, r, :, at_lanes]
                f, p = merge((f, p), (f0, p0), idx[0] != 0, span(d, half), span(d, sizes[0]))
                ends[r][0, :, at_lanes] = f
                ends[r][1, :, at_lanes] = p
            else:
                ends_all[0, r, :, at_lanes] = f
                ends_all[1, r, :, at_lanes] = p


def transform(fold, idx, sub, cuts, last, xs, tables, extra):
    planes, cols = xs[0].shape[1:]
    sizes = chunks(sub)
    half = sizes[last]
    at = sizes[0] if last else 0
    side = tables[0].shape[0]
    shape = lambda *n: jax.ShapeDtypeStruct(n, F32)
    outs = [shape(high - low, planes, cols) for pieces in cuts for low, high in pieces]
    if last:
        outs += [shape(2, planes, cols)] * fold
    else:
        outs += [shape(fold, planes, cols), shape(2, fold, planes, cols)]
    rows = half * planes
    return pl.pallas_call(
        functools.partial(transform_kernel, fold, at, sizes, cuts, last),
        out_shape=outs,
        in_specs=smem(1) + vmem(len(xs) + 4 + len(extra)),
        out_specs=vmem(len(outs)),
        scratch_shapes=[pltpu.VMEM((2 * rows, side), BF16)] * 2,
        compiler_params=params(),
        cost_estimate=pl.CostEstimate(flops=12 * rows * side * side, bytes_accessed=8 * side * side, transcendentals=0),
        name="transform_b" if last else "transform_a",
    )(idx, *xs, *tables, *extra)


def span(d, cells):
    power, gain, block = None, None, (d, d)
    while cells:
        if cells % 2:
            if power is None:
                power, gain = block
            else:
                power, gain = power * block[0], gain + power * power * block[1]
        block = doubled(*block)
        cells //= 2
    return power, gain


def merge(mine, other, upper, span_mine, span_other):
    pick = lambda a, b: a if a is b else jnp.where(upper, a, b)
    f_low, f_high = jnp.where(upper, other[0], mine[0]), jnp.where(upper, mine[0], other[0])
    p_low, p_high = jnp.where(upper, other[1], mine[1]), jnp.where(upper, mine[1], other[1])
    high_power, high_gain = pick(span_mine[0], span_other[0]), pick(span_mine[1], span_other[1])
    low_power = pick(span_other[0], span_mine[0])
    return f_high + high_power * f_low, p_low + low_power * (p_high + high_gain * f_low)


def doubled(power, gain):
    return power * power, gain * (1.0 + power * power)


def stages(fold, count):
    bits = [1 << k for k in range(count.bit_length() - 1)]
    groups = [[1 << k for k in range(fold.bit_length() - 1)]]
    return groups + [bits[k : k + 2] for k in range(0, len(bits), 2)]


def peers(bits):
    offsets = [0]
    for bit in bits:
        offsets += [o ^ bit for o in offsets]
    return offsets


def combine(groups, stage, d, sub, me, row, ends, entry):
    power, gain = span(d, sub)
    start, stop, turn = None, None, None
    for k, bits in enumerate(groups[: stage + 1]):
        position = row if k else me
        if k == 1:
            start, stop, turn = jnp.ones_like(d), jnp.ones_like(d), jnp.zeros_like(d)
            if entry is None:
                entry = (jnp.zeros_like(d), jnp.zeros_like(d))
        for bit in bits:
            upper = position & bit != 0
            if k:
                if k == stage:
                    mine, other = ends[0], ends[1]
                    below, above = entry
                    below = below + jnp.where(upper, start * other[0], 0.0)
                    above = above + jnp.where(upper, turn * other[0], stop * (other[1] + gain * mine[0]))
                    entry = (below, above)
                turn = jnp.where(upper, power * turn, turn + stop * gain * power)
                start = jnp.where(upper, power * start, start)
                stop = jnp.where(upper, stop, power * stop)
            if k == stage:
                ends = [merge(ends[i], ends[i + 1], upper, (power, gain), (power, gain)) for i in range(0, len(ends), 2)]
            power, gain = doubled(power, gain)
    return ends[0], entry


def combine_tiles(groups, stage, sub, idx, damping, ends, entry, put):
    for t in range(damping.shape[1] // LANES):
        at = pl.ds(t * LANES, LANES)
        pairs = [(e[0, :, at], e[1, :, at]) for e in ends]
        entered = None if entry is None else (entry[0, :, at], entry[1, :, at])
        put(at, *combine(groups, stage, damping[:, at], sub, idx[0], idx[1], pairs, entered))


def combine_kernel(groups, stage, sub, idx, damping, *refs):
    count = 1 << len(groups[stage])
    ends, rest = refs[:count], refs[count:]
    entry = rest[0] if stage > 1 else None
    outs = rest[-2:] if stage else rest[-1:]

    def put(at, union, entered):
        outs[0][0, :, at], outs[0][1, :, at] = union
        if stage:
            outs[1][0, :, at], outs[1][1, :, at] = entered

    combine_tiles(groups, stage, sub, idx, damping, ends, entry, put)


def combined(groups, stage, sub, idx, damping, ends, entry):
    pair = jax.ShapeDtypeStruct((2,) + damping.shape, F32)
    extra = [entry] if stage > 1 else []
    outs = [pair, pair] if stage else [pair]
    return pl.pallas_call(
        functools.partial(combine_kernel, groups, stage, sub),
        out_shape=outs,
        in_specs=smem(1) + vmem(1 + len(ends) + len(extra)),
        out_specs=vmem(len(outs)),
        compiler_params=params(),
        cost_estimate=pl.CostEstimate(flops=100 * damping.size, bytes_accessed=32 * damping.size, transcendentals=0),
    )(idx, damping, *ends, *extra)


def solve_kernel(fold, groups, cuts, idx, damping, *refs):
    stage = len(groups) - 1
    count = 1 << len(groups[stage])
    ends, rest = refs[:count], refs[count:]
    if stage > 1:
        entry, rest = rest[0], rest[1:]
    else:
        entry = None
    count = sum(len(c) for part in cuts for c in part)
    pieces, rest = rest[:count], rest[count:]
    coefficients_out, pressure_out, coefficients, pressure, entered, c_sems, p_sems = rest
    cells = coefficients.shape[0]
    sub = cells // fold
    half = sub // 2
    copies = []
    for h in range(2):
        for r in range(fold):
            for low, high in cuts[h][r]:
                rows = pl.ds(chunk_start(idx[0] ^ r, h, sub) + low, high - low)
                k = len(copies)
                coefficients[rows] = pieces[k][...]
                copies.append(pltpu.make_async_copy(coefficients.at[rows], coefficients_out.at[rows], c_sems.at[k]))
                copies[k].start()

    def put(at, union, entry):
        entered[0, :, at], entered[1, :, at] = entry

    combine_tiles(groups, stage, sub, idx, damping, ends, entry, put)
    d = damping[...]
    w = weight_of(d)

    def forward(i, f):
        f = w * coefficients[i] + d * f
        pressure[i] = f
        return f

    lax.fori_loop(0, cells, forward, entered[0], unroll=4)

    p = entered[1]
    for block in reversed(range(2 * fold)):

        def backward(i, p, block=block):
            at = (block + 1) * half - 1 - i
            p = pressure[at] + d * p
            pressure[at] = p
            return p

        p = lax.fori_loop(0, half, backward, p, unroll=4)
        rows = pl.ds(block * half, half)
        copies.append(pltpu.make_async_copy(pressure.at[rows], pressure_out.at[rows], p_sems.at[block]))
        copies[-1].start()
    for copy in copies:
        copy.wait()


def solve(fold, groups, cuts, idx, damping, ends, entry, pieces, cells):
    planes, cols = damping.shape
    shape = (cells, planes, cols)
    extra = [entry] if len(groups) > 2 else []
    return pl.pallas_call(
        functools.partial(solve_kernel, fold, groups, cuts),
        out_shape=[jax.ShapeDtypeStruct(shape, F32)] * 2,
        in_specs=smem(1) + vmem(1 + len(ends) + len(extra) + len(pieces)),
        out_specs=hbm(2),
        scratch_shapes=[
            pltpu.VMEM(shape, F32),
            pltpu.VMEM(shape, F32),
            pltpu.VMEM((2, planes, cols), F32),
            pltpu.SemaphoreType.DMA((len(pieces),)),
            pltpu.SemaphoreType.DMA((2 * fold,)),
        ],
        compiler_params=params(),
        cost_estimate=pl.CostEstimate(flops=5 * cells * planes * cols, bytes_accessed=12 * cells * planes * cols, transcendentals=0),
        name="solve",
    )(idx, damping, *ends, *extra, *pieces)


def body(velocity_u, wall_strain, damping):
    cells, _, cols = velocity_u.shape
    fold = lax.axis_size("gy")
    sub = cells // fold
    me, row = lax.axis_index("gy"), lax.axis_index("gx")
    idx = jnp.stack([me, row]).astype(jnp.int32)
    order = list(range(fold - 1, 0, -1))
    *sends, near, far, u, wall, damping = lead(fold, idx, velocity_u, wall_strain, damping)
    got = {(r, 0): partner(sends[r - 1], "gy", r) for r in order}
    near, far = exchange_edges(near, far)
    second, own, *sends = stencil(fold, idx, u, wall, near, far)
    for r in order:
        got[r, 1] = partner(sends[r - 1], "gy", r)
    tables = cosine_tables(fold, idx, cols)
    cuts = pieces_of(fold, sub)
    first = transform(fold, idx, sub, cuts[0], 0, [own] + [got[r, 0] for r in range(1, fold)], tables, [damping])
    every_damping, ends_a = first[-2:]
    extra = [every_damping, ends_a]
    rest = transform(fold, idx, sub, cuts[1], 1, [own] + [got[r, 1] for r in range(1, fold)], tables, extra)
    ends_b = rest[-fold:]
    pieces = []
    for h, outs in enumerate((first, rest)):
        outs = iter(outs)
        for r in range(fold):
            for _ in range(len(cuts[h][r])):
                out = next(outs)
                pieces.append(out if r == 0 else partner(out, "gy", r))
    groups = stages(fold, lax.axis_size("gx"))
    ends = [ends_b[r] if r == 0 else partner(ends_b[r], "gy", r) for r in peers(groups[0])]
    entry = None
    for stage in range(1, len(groups)):
        mine, *entries = combined(groups, stage - 1, sub, idx, damping, ends, entry)
        entry = entries[0] if entries else None
        ends = [mine] + [partner(mine, "gx", o) for o in peers(groups[stage])[1:]]
    coefficients, pressure = solve(fold, groups, cuts, idx, damping, ends, entry, pieces, cells)
    return second, coefficients, pressure


def pieces_of(fold, sub):
    first, later = chunks(sub)
    cut = first // 2
    whole = [[(0, first)] for _ in range(fold)]
    whole[fold - 1] = [(0, cut), (cut, first)]
    return whole, [[(0, later)] for _ in range(fold)]


def solution(mesh):
    return jax.shard_map(
        body,
        mesh=mesh,
        in_specs=(P("gx", None, "gy"), P("gx", None, "gy"), P(None, "gy")),
        out_specs=(P("gx", None, "gy"), P("gx", None, "gy"), P("gx", None, "gy")),
        check_vma=False,
    )
```

profile of v0, /device:TPU:0, one launch (start us, length us, event | category | flops | bytes accessed | tf_op | source)
XLA Modules:
  0.0 74.3 jit_solution(3909547132485208739)
XLA Ops:
  0.7 1.6 %copy-done = f32[64,16,512]{2,1,0:T(8,128)S(1)} copy-done((f32[64,16,512]{2,1,0:T(8,128)S(1)}, f32[64,16,512]{2,1,0:T(8,128)}, u32[]{:S(2)}) %copy-start) | copy-done | bytes 2097176
  2.3 1.6 %copy-done.1 = f32[64,16,512]{2,1,0:T(8,128)S(1)} copy-done((f32[64,16,512]{2,1,0:T(8,128)S(1)}, f32[64,16,512]{2,1,0:T(8,128)}, u32[]{:S(2)}) %copy-start.1) | copy-done | bytes 2097176
  4.7 1.5 %lead.1 = (f32[13,16,512]{2,1,0:T(8,128)S(1)}, f32[13,16,512]{2,1,0:T(8,128)S(1)}, f32[13,16,512]{2,1,0:T(8,128)S(1)}, f32[3,16,512]{2,1,0:T(8,128)S(1)}, f32[3,...) custom-call(s32[2]{0:T(128)S(1)} %pad_add_fusion.idx, ...), custom_call_target="tpu_custom_call" | custom-call | flops 3145728 | bytes 3145728 | tf_op jit(solution)/shard_map/lead/pallas_call | solution.py:104
  6.7 2.6 %collective-permute-start.6 = (f32[13,16,512]{2,1,0:T(8,128)S(1)}, f32[13,16,512]{2,1,0:T(8,128)S(1)}, u32[]{:S(2)}, u32[]{:S(2)}) collective-permute-start(f32[13,16,512]{2,1,0:T(8,128)S(1)} %get-tuple-element.54), channel_id=1, source_target_pairs={{0,2},{1,3},{2,0},{3,1},{4,6},{5,7},{6,4},{7,5},{8,10},{9,11},{10,... | collective-permute-start | bytes 1277960 | tf_op jit(solution)/shard_map/ppermute | solution.py:37
  9.3 1.8 %collective-permute-start = (f32[3,16,512]{2,1,0:T(8,128)S(1)}, f32[3,16,512]{2,1,0:T(8,128)S(1)}, u32[]{:S(2)}, u32[]{:S(2)}) collective-permute-start(f32[3,16,512]{2,1,0:T(8,128)S(1)} %get-tuple-element.41), channel_id=1, source_target_pairs={{0,4},{4,0},{8,12},{12,8},{16,20},{20,16},{24,28},{28,24},{1,5},{5... | collective-permute-start | bytes 294920 | tf_op jit(solution)/shard_map/ppermute | solution.py:37
  11.8 3.8 %table.1 = (bf16[1024,1024]{1,0:T(8,128)(2,1)S(1)}, bf16[1024,1024]{1,0:T(8,128)(2,1)S(1)}, bf16[1024,1024]{1,0:T(8,128)(2,1)S(1)}, bf16[1024,1024]{1,0:T(8,128)(2,1)S(1)}) custom-call(s32[2]{0:T(128)S(1)} %pad_add_fusion.idx), custom_call_target="tpu_custom_call" | custom-call | flops 62914560 | bytes 8388608 | tf_op jit(solution)/shard_map/table/pallas_call | solution.py:228
  15.6 2.7 %stencil.1 = (f32[64,16,512]{2,1,0:T(8,128)}, f32[16,16,512]{2,1,0:T(8,128)S(1)}, f32[4,16,512]{2,1,0:T(8,128)S(1)}, f32[4,16,512]{2,1,0:T(8,128)S(1)}, f32[4,16,512]{2,1,0:T(8,128)S(1)}) custom-call(s32[2]{0:T(128)S(1)} %pad_add_fusion.idx, f32[64,16,512]{2,1,0:T(8,128)S(1)} %get-tuple-element.39.u, f32[64,16,512]{2,1,0:T(8,128)S(1)} %get-tuple-element.40.wall, ...), custom_call_target="tpu_custom_call" | custom-call | flops 10485760 | bytes 8388608 | tf_op jit(solution)/shard_map/stencil/pallas_call | solution.py:155
  18.5 1.5 %collective-permute-start.3 = (f32[4,16,512]{2,1,0:T(8,128)S(1)}, f32[4,16,512]{2,1,0:T(8,128)S(1)}, u32[]{:S(2)}, u32[]{:S(2)}) collective-permute-start(f32[4,16,512]{2,1,0:T(8,128)S(1)} %get-tuple-element.47), channel_id=1, source_target_pairs={{0,2},{1,3},{2,0},{3,1},{4,6},{5,7},{6,4},{7,5},{8,10},{9,11},{10,... | collective-permute-start | bytes 393224 | tf_op jit(solution)/shard_map/ppermute | solution.py:37
  20.3 8.4 %collective-permute-done.7.refs_3_ = f32[13,16,512]{2,1,0:T(8,128)S(1)} collective-permute-done((f32[13,16,512]{2,1,0:T(8,128)S(1)}, f32[13,16,512]{2,1,0:T(8,128)S(1)}, u32[]{:S(2)}, u32[]{:S(2)}) %collective-permute-start.7) | collective-permute-done | bytes 426016 | tf_op jit(solution)/shard_map/ppermute | solution.py:37
  28.6 4.9 %transform_a.1 = (f32[12,16,512]{2,1,0:T(8,128)S(1)}, f32[12,16,512]{2,1,0:T(8,128)S(1)}, f32[12,16,512]{2,1,0:T(8,128)S(1)}, f32[6,16,512]{2,1,0:T(8,128)S(1)},...) custom-call(s32[2]{0:T(128)S(1)} %pad_add_fusion.idx, ...), custom_call_target="tpu_custom_call" | custom-call | flops 2415919104 | bytes 8388608 | tf_op jit(solution)/shard_map/transform_a/pallas_call | solution.py:348
  34.2 2.9 %transform_b.1 = (f32[4,16,512]{2,1,0:T(8,128)S(1)}, f32[4,16,512]{2,1,0:T(8,128)S(1)}, f32[4,16,512]{2,1,0:T(8,128)S(1)}, f32[4,16,512]{2,1,0:T(8,128)S(1)}, f3...) custom-call(s32[2]{0:T(128)S(1)} %pad_add_fusion.idx, ...), custom_call_target="tpu_custom_call" | custom-call | flops 805306368 | bytes 8388608 | tf_op jit(solution)/shard_map/transform_b/pallas_call | solution.py:348
  37.2 1.7 %collective-permute-start.9 = (f32[2,16,512]{2,1,0:T(8,128)S(1)}, f32[2,16,512]{2,1,0:T(8,128)S(1)}, u32[]{:S(2)}, u32[]{:S(2)}) collective-permute-start(f32[2,16,512]{2,1,0:T(8,128)S(1)} %get-tuple-element.60), channel_id=1, source_target_pairs={{0,2},{1,3},{2,0},{3,1},{4,6},{5,7},{6,4},{7,5},{8,10},{9,11},{10,... | collective-permute-start | bytes 196616 | tf_op jit(solution)/shard_map/ppermute | solution.py:37
  39.0 2.6 %collective-permute-done.9.refs_2_ = f32[2,16,512]{2,1,0:T(8,128)S(1)} collective-permute-done((f32[2,16,512]{2,1,0:T(8,128)S(1)}, f32[2,16,512]{2,1,0:T(8,128)S(1)}, u32[]{:S(2)}, u32[]{:S(2)}) %collective-permute-start.9) | collective-permute-done | bytes 65568 | tf_op jit(solution)/shard_map/ppermute | solution.py:37
  41.6 1.7 %collective-permute-done.10.refs_3_ = f32[2,16,512]{2,1,0:T(8,128)S(1)} collective-permute-done((f32[2,16,512]{2,1,0:T(8,128)S(1)}, f32[2,16,512]{2,1,0:T(8,128)S(1)}, u32[]{:S(2)}, u32[]{:S(2)}) %collective-permute-start.10) | collective-permute-done | bytes 65568 | tf_op jit(solution)/shard_map/ppermute | solution.py:37
  43.9 2.6 %collective-permute-start.13 = (f32[2,16,512]{2,1,0:T(8,128)S(1)}, f32[2,16,512]{2,1,0:T(8,128)S(1)}, u32[]{:S(2)}, u32[]{:S(2)}) collective-permute-start(f32[2,16,512]{2,1,0:T(8,128)S(1)} %shard_map.58.refs_0_), channel_id=1, source_target_pairs={{0,12},{4,8},{8,4},{12,0},{16,28},{20,24},{24,20},{28,16},{1,13},{... | collective-permute-start | bytes 196616 | tf_op jit(solution)/shard_map/ppermute | solution.py:37
  47.8 1.4 %collective-permute-done.13.refs_3_ = f32[2,16,512]{2,1,0:T(8,128)S(1)} collective-permute-done((f32[2,16,512]{2,1,0:T(8,128)S(1)}, f32[2,16,512]{2,1,0:T(8,128)S(1)}, u32[]{:S(2)}, u32[]{:S(2)}) %collective-permute-start.13) | collective-permute-done | bytes 65568 | tf_op jit(solution)/shard_map/ppermute | solution.py:37
  49.9 1.7 %collective-permute-done.12.refs_2_ = f32[2,16,512]{2,1,0:T(8,128)S(1)} collective-permute-done((f32[2,16,512]{2,1,0:T(8,128)S(1)}, f32[2,16,512]{2,1,0:T(8,128)S(1)}, u32[]{:S(2)}, u32[]{:S(2)}) %collective-permute-start.12) | collective-permute-done | bytes 65568 | tf_op jit(solution)/shard_map/ppermute | solution.py:37
  52.1 3.8 %collective-permute-done.11.refs_1_ = f32[2,16,512]{2,1,0:T(8,128)S(1)} collective-permute-done((f32[2,16,512]{2,1,0:T(8,128)S(1)}, f32[2,16,512]{2,1,0:T(8,128)S(1)}, u32[]{:S(2)}, u32[]{:S(2)}) %collective-permute-start.11) | collective-permute-done | bytes 65568 | tf_op jit(solution)/shard_map/ppermute | solution.py:37
  55.9 1.7 %collective-permute-start.17 = (f32[6,16,512]{2,1,0:T(8,128)S(1)}, f32[6,16,512]{2,1,0:T(8,128)S(1)}, u32[]{:S(2)}, u32[]{:S(2)}) collective-permute-start(f32[6,16,512]{2,1,0:T(8,128)S(1)} %get-tuple-element.67), channel_id=1, source_target_pairs={{0,3},{1,2},{2,1},{3,0},{4,7},{5,6},{6,5},{7,4},{8,11},{9,10},{10,... | collective-permute-start | bytes 589832 | tf_op jit(solution)/shard_map/ppermute | solution.py:37
  57.6 3.7 %collective-permute-done.20.refs_10_ = f32[4,16,512]{2,1,0:T(8,128)S(1)} collective-permute-done((f32[4,16,512]{2,1,0:T(8,128)S(1)}, f32[4,16,512]{2,1,0:T(8,128)S(1)}, u32[]{:S(2)}, u32[]{:S(2)}) %collective-permute-start.20) | collective-permute-done | bytes 131104 | tf_op jit(solution)/shard_map/ppermute | solution.py:37
  63.2 2.6 %collective-permute-start.14 = (f32[2,16,512]{2,1,0:T(8,128)S(1)}, f32[2,16,512]{2,1,0:T(8,128)S(1)}, u32[]{:S(2)}, u32[]{:S(2)}) collective-permute-start(f32[2,16,512]{2,1,0:T(8,128)S(1)} %get-tuple-element.62.refs_0_), channel_id=1, source_target_pairs={{0,16},{4,20},{8,24},{12,28},{16,0},{20,4},{24,8},{28,12},{1,17},{... | collective-permute-start | bytes 196616 | tf_op jit(solution)/shard_map/ppermute | solution.py:37
  65.8 4.6 %collective-permute-done.14.refs_1_ = f32[2,16,512]{2,1,0:T(8,128)S(1)} collective-permute-done((f32[2,16,512]{2,1,0:T(8,128)S(1)}, f32[2,16,512]{2,1,0:T(8,128)S(1)}, u32[]{:S(2)}, u32[]{:S(2)}) %collective-permute-start.14) | collective-permute-done | bytes 65568 | tf_op jit(solution)/shard_map/ppermute | solution.py:37
  70.3 1.3 %collective-permute-done.18.refs_7_ = f32[6,16,512]{2,1,0:T(8,128)S(1)} collective-permute-done((f32[6,16,512]{2,1,0:T(8,128)S(1)}, f32[6,16,512]{2,1,0:T(8,128)S(1)}, u32[]{:S(2)}, u32[]{:S(2)}) %collective-permute-start.18) | collective-permute-done | bytes 196640 | tf_op jit(solution)/shard_map/ppermute | solution.py:37
  71.6 2.7 %solve.1 = (f32[64,16,512]{2,1,0:T(8,128)}, f32[64,16,512]{2,1,0:T(8,128)}) custom-call(s32[2]{0:T(128)S(1)} %pad_add_fusion.idx, f32[16,512]{1,0:T(8,128)S(1)} %get-tuple-element.44.refs_8_.damping, f32[2,16,512]{2,1,0:T(8,128)S(1)} %get-tuple-element.62.refs_0_, f32[2,16,512]{2,1,0:T(8,128)S(1)} %collective-permute-done.14.refs_1_, ...), custom_call_target="tpu_custom_call" | custom-call | flops 2621440 | bytes 6291456 | tf_op jit(solution)/shard_map/solve/pallas_call | solution.py:521
  (35 shorter events, 8.4 us)
Async XLA Ops:
  0.7 1.6 %copy-start = (f32[64,16,512]{2,1,0:T(8,128)S(1)}, f32[64,16,512]{2,1,0:T(8,128)}, u32[]{:S(2)}) copy-start(f32[64,16,512]{2,1,0:T(8,128)} %u_in.1) | copy-start | bytes 6291460
  2.3 1.6 %copy-start.1 = (f32[64,16,512]{2,1,0:T(8,128)S(1)}, f32[64,16,512]{2,1,0:T(8,128)}, u32[]{:S(2)}) copy-start(f32[64,16,512]{2,1,0:T(8,128)} %wall_in.1) | copy-start | bytes 6291460
  6.2 13.8 %collective-permute-start.5 = (f32[13,16,512]{2,1,0:T(8,128)S(1)}, f32[13,16,512]{2,1,0:T(8,128)S(1)}, u32[]{:S(2)}, u32[]{:S(2)}) collective-permute-start(f32[13,16,512]{2,1,0:T(8,128)S(1)} %get-tuple-element.53), channel_id=1, source_target_pairs={{0,1},{1,0},{2,3},{3,2},{4,5},{5,4},{6,7},{7,6},{8,9},{9,8},{10,11... | collective-permute-start | bytes 1277960 | tf_op jit(solution)/shard_map/ppermute | solution.py:37
  6.7 13.5 %collective-permute-start.6 = (f32[13,16,512]{2,1,0:T(8,128)S(1)}, f32[13,16,512]{2,1,0:T(8,128)S(1)}, u32[]{:S(2)}, u32[]{:S(2)}) collective-permute-start(f32[13,16,512]{2,1,0:T(8,128)S(1)} %get-tuple-element.54), channel_id=1, source_target_pairs={{0,2},{1,3},{2,0},{3,1},{4,6},{5,7},{6,4},{7,5},{8,10},{9,11},{10,... | collective-permute-start | bytes 1277960 | tf_op jit(solution)/shard_map/ppermute | solution.py:37
  9.3 19.3 %collective-permute-start.7 = (f32[13,16,512]{2,1,0:T(8,128)S(1)}, f32[13,16,512]{2,1,0:T(8,128)S(1)}, u32[]{:S(2)}, u32[]{:S(2)}) collective-permute-start(f32[13,16,512]{2,1,0:T(8,128)S(1)} %get-tuple-element.55), channel_id=1, source_target_pairs={{0,3},{1,2},{2,1},{3,0},{4,7},{5,6},{6,5},{7,4},{8,11},{9,10},{10,... | collective-permute-start | bytes 1277960 | tf_op jit(solution)/shard_map/ppermute | solution.py:37
  9.3 6.2 %collective-permute-start = (f32[3,16,512]{2,1,0:T(8,128)S(1)}, f32[3,16,512]{2,1,0:T(8,128)S(1)}, u32[]{:S(2)}, u32[]{:S(2)}) collective-permute-start(f32[3,16,512]{2,1,0:T(8,128)S(1)} %get-tuple-element.41), channel_id=1, source_target_pairs={{0,4},{4,0},{8,12},{12,8},{16,20},{20,16},{24,28},{28,24},{1,5},{5... | collective-permute-start | bytes 294920 | tf_op jit(solution)/shard_map/ppermute | solution.py:37
  11.1 4.5 %collective-permute-start.1 = (f32[3,16,512]{2,1,0:T(8,128)S(1)}, f32[3,16,512]{2,1,0:T(8,128)S(1)}, u32[]{:S(2)}, u32[]{:S(2)}) collective-permute-start(f32[3,16,512]{2,1,0:T(8,128)S(1)} %get-tuple-element.42), channel_id=1, source_target_pairs={{4,8},{12,16},{20,24},{8,4},{16,12},{24,20},{5,9},{13,17},{21,25},... | collective-permute-start | bytes 294920 | tf_op jit(solution)/shard_map/ppermute | solution.py:174
  18.3 15.2 %collective-permute-start.2 = (f32[4,16,512]{2,1,0:T(8,128)S(1)}, f32[4,16,512]{2,1,0:T(8,128)S(1)}, u32[]{:S(2)}, u32[]{:S(2)}) collective-permute-start(f32[4,16,512]{2,1,0:T(8,128)S(1)} %get-tuple-element.46), channel_id=1, source_target_pairs={{0,1},{1,0},{2,3},{3,2},{4,5},{5,4},{6,7},{7,6},{8,9},{9,8},{10,11... | collective-permute-start | bytes 393224 | tf_op jit(solution)/shard_map/ppermute | solution.py:37
  18.5 15.1 %collective-permute-start.3 = (f32[4,16,512]{2,1,0:T(8,128)S(1)}, f32[4,16,512]{2,1,0:T(8,128)S(1)}, u32[]{:S(2)}, u32[]{:S(2)}) collective-permute-start(f32[4,16,512]{2,1,0:T(8,128)S(1)} %get-tuple-element.47), channel_id=1, source_target_pairs={{0,2},{1,3},{2,0},{3,1},{4,6},{5,7},{6,4},{7,5},{8,10},{9,11},{10,... | collective-permute-start | bytes 393224 | tf_op jit(solution)/shard_map/ppermute | solution.py:37
  20.0 14.2 %collective-permute-start.4 = (f32[4,16,512]{2,1,0:T(8,128)S(1)}, f32[4,16,512]{2,1,0:T(8,128)S(1)}, u32[]{:S(2)}, u32[]{:S(2)}) collective-permute-start(f32[4,16,512]{2,1,0:T(8,128)S(1)} %get-tuple-element.48), channel_id=1, source_target_pairs={{0,3},{1,2},{2,1},{3,0},{4,7},{5,6},{6,5},{7,4},{8,11},{9,10},{10,... | collective-permute-start | bytes 393224 | tf_op jit(solution)/shard_map/ppermute | solution.py:37
  37.0 1.9 %collective-permute-start.8 = (f32[2,16,512]{2,1,0:T(8,128)S(1)}, f32[2,16,512]{2,1,0:T(8,128)S(1)}, u32[]{:S(2)}, u32[]{:S(2)}) collective-permute-start(f32[2,16,512]{2,1,0:T(8,128)S(1)} %get-tuple-element.59), channel_id=1, source_target_pairs={{0,1},{1,0},{2,3},{3,2},{4,5},{5,4},{6,7},{7,6},{8,9},{9,8},{10,11... | collective-permute-start | bytes 196616 | tf_op jit(solution)/shard_map/ppermute | solution.py:37
  37.2 4.4 %collective-permute-start.9 = (f32[2,16,512]{2,1,0:T(8,128)S(1)}, f32[2,16,512]{2,1,0:T(8,128)S(1)}, u32[]{:S(2)}, u32[]{:S(2)}) collective-permute-start(f32[2,16,512]{2,1,0:T(8,128)S(1)} %get-tuple-element.60), channel_id=1, source_target_pairs={{0,2},{1,3},{2,0},{3,1},{4,6},{5,7},{6,4},{7,5},{8,10},{9,11},{10,... | collective-permute-start | bytes 196616 | tf_op jit(solution)/shard_map/ppermute | solution.py:37
  38.9 4.3 %collective-permute-start.10 = (f32[2,16,512]{2,1,0:T(8,128)S(1)}, f32[2,16,512]{2,1,0:T(8,128)S(1)}, u32[]{:S(2)}, u32[]{:S(2)}) collective-permute-start(f32[2,16,512]{2,1,0:T(8,128)S(1)} %get-tuple-element.61), channel_id=1, source_target_pairs={{0,3},{1,2},{2,1},{3,0},{4,7},{5,6},{6,5},{7,4},{8,11},{9,10},{10,... | collective-permute-start | bytes 196616 | tf_op jit(solution)/shard_map/ppermute | solution.py:37
  43.9 5.2 %collective-permute-start.13 = (f32[2,16,512]{2,1,0:T(8,128)S(1)}, f32[2,16,512]{2,1,0:T(8,128)S(1)}, u32[]{:S(2)}, u32[]{:S(2)}) collective-permute-start(f32[2,16,512]{2,1,0:T(8,128)S(1)} %shard_map.58.refs_0_), channel_id=1, source_target_pairs={{0,12},{4,8},{8,4},{12,0},{16,28},{20,24},{24,20},{28,16},{1,13},{... | collective-permute-start | bytes 196616 | tf_op jit(solution)/shard_map/ppermute | solution.py:37
  46.5 25.1 %collective-permute-start.15 = (f32[12,16,512]{2,1,0:T(8,128)S(1)}, f32[12,16,512]{2,1,0:T(8,128)S(1)}, u32[]{:S(2)}, u32[]{:S(2)}) collective-permute-start(f32[12,16,512]{2,1,0:T(8,128)S(1)} %get-tuple-element.65), channel_id=1, source_target_pairs={{0,1},{1,0},{2,3},{3,2},{4,5},{5,4},{6,7},{7,6},{8,9},{9,8},{10,11... | collective-permute-start | bytes 1179656 | tf_op jit(solution)/shard_map/ppermute | solution.py:37
  46.5 25.1 %collective-permute-start.16 = (f32[12,16,512]{2,1,0:T(8,128)S(1)}, f32[12,16,512]{2,1,0:T(8,128)S(1)}, u32[]{:S(2)}, u32[]{:S(2)}) collective-permute-start(f32[12,16,512]{2,1,0:T(8,128)S(1)} %get-tuple-element.66), channel_id=1, source_target_pairs={{0,2},{1,3},{2,0},{3,1},{4,6},{5,7},{6,4},{7,5},{8,10},{9,11},{10,... | collective-permute-start | bytes 1179656 | tf_op jit(solution)/shard_map/ppermute | solution.py:37
  47.3 4.3 %collective-permute-start.12 = (f32[2,16,512]{2,1,0:T(8,128)S(1)}, f32[2,16,512]{2,1,0:T(8,128)S(1)}, u32[]{:S(2)}, u32[]{:S(2)}) collective-permute-start(f32[2,16,512]{2,1,0:T(8,128)S(1)} %shard_map.58.refs_0_), channel_id=1, source_target_pairs={{0,8},{4,12},{8,0},{12,4},{16,24},{20,28},{24,16},{28,20},{1,9},{5... | collective-permute-start | bytes 196616 | tf_op jit(solution)/shard_map/ppermute | solution.py:37
  47.8 8.1 %collective-permute-start.19 = (f32[4,16,512]{2,1,0:T(8,128)S(1)}, f32[4,16,512]{2,1,0:T(8,128)S(1)}, u32[]{:S(2)}, u32[]{:S(2)}) collective-permute-start(f32[4,16,512]{2,1,0:T(8,128)S(1)} %get-tuple-element.70), channel_id=1, source_target_pairs={{0,1},{1,0},{2,3},{3,2},{4,5},{5,4},{6,7},{7,6},{8,9},{9,8},{10,11... | collective-permute-start | bytes 393224 | tf_op jit(solution)/shard_map/ppermute | solution.py:37
  49.1 12.2 %collective-permute-start.20 = (f32[4,16,512]{2,1,0:T(8,128)S(1)}, f32[4,16,512]{2,1,0:T(8,128)S(1)}, u32[]{:S(2)}, u32[]{:S(2)}) collective-permute-start(f32[4,16,512]{2,1,0:T(8,128)S(1)} %get-tuple-element.71), channel_id=1, source_target_pairs={{0,2},{1,3},{2,0},{3,1},{4,6},{5,7},{6,4},{7,5},{8,10},{9,11},{10,... | collective-permute-start | bytes 393224 | tf_op jit(solution)/shard_map/ppermute | solution.py:37
  51.6 4.3 %collective-permute-start.11 = (f32[2,16,512]{2,1,0:T(8,128)S(1)}, f32[2,16,512]{2,1,0:T(8,128)S(1)}, u32[]{:S(2)}, u32[]{:S(2)}) collective-permute-start(f32[2,16,512]{2,1,0:T(8,128)S(1)} %shard_map.58.refs_0_), channel_id=1, source_target_pairs={{0,4},{4,0},{8,12},{12,8},{16,20},{20,16},{24,28},{28,24},{1,5},{5... | collective-permute-start | bytes 196616 | tf_op jit(solution)/shard_map/ppermute | solution.py:37
  55.9 7.3 %collective-permute-start.21 = (f32[4,16,512]{2,1,0:T(8,128)S(1)}, f32[4,16,512]{2,1,0:T(8,128)S(1)}, u32[]{:S(2)}, u32[]{:S(2)}) collective-permute-start(f32[4,16,512]{2,1,0:T(8,128)S(1)} %get-tuple-element.72), channel_id=1, source_target_pairs={{0,3},{1,2},{2,1},{3,0},{4,7},{5,6},{6,5},{7,4},{8,11},{9,10},{10,... | collective-permute-start | bytes 393224 | tf_op jit(solution)/shard_map/ppermute | solution.py:37
  55.9 14.5 %collective-permute-start.17 = (f32[6,16,512]{2,1,0:T(8,128)S(1)}, f32[6,16,512]{2,1,0:T(8,128)S(1)}, u32[]{:S(2)}, u32[]{:S(2)}) collective-permute-start(f32[6,16,512]{2,1,0:T(8,128)S(1)} %get-tuple-element.67), channel_id=1, source_target_pairs={{0,3},{1,2},{2,1},{3,0},{4,7},{5,6},{6,5},{7,4},{8,11},{9,10},{10,... | collective-permute-start | bytes 589832 | tf_op jit(solution)/shard_map/ppermute | solution.py:37
  61.3 10.3 %collective-permute-start.18 = (f32[6,16,512]{2,1,0:T(8,128)S(1)}, f32[6,16,512]{2,1,0:T(8,128)S(1)}, u32[]{:S(2)}, u32[]{:S(2)}) collective-permute-start(f32[6,16,512]{2,1,0:T(8,128)S(1)} %get-tuple-element.68), channel_id=1, source_target_pairs={{0,3},{1,2},{2,1},{3,0},{4,7},{5,6},{6,5},{7,4},{8,11},{9,10},{10,... | collective-permute-start | bytes 589832 | tf_op jit(solution)/shard_map/ppermute | solution.py:37
  63.2 7.2 %collective-permute-start.14 = (f32[2,16,512]{2,1,0:T(8,128)S(1)}, f32[2,16,512]{2,1,0:T(8,128)S(1)}, u32[]{:S(2)}, u32[]{:S(2)}) collective-permute-start(f32[2,16,512]{2,1,0:T(8,128)S(1)} %get-tuple-element.62.refs_0_), channel_id=1, source_target_pairs={{0,16},{4,20},{8,24},{12,28},{16,0},{20,4},{24,8},{28,12},{1,17},{... | collective-permute-start | bytes 196616 | tf_op jit(solution)/shard_map/ppermute | solution.py:37
  (1 other events, 0.8 us)
where the time goes:
time: 74.6 us; the launch traced here: 74.3 us
  waiting for transfers between devices  31 us (42%)
  Pallas kernels  19.7 us (26%)
  starting transfers between devices  18.9 us (25%)
  local copies, waits for them, and re-layouts  3.94 us (5%)
    ppermute x21, waiting for transfers between devices, partner(): return lax.ppermute(x, axis, [(i, i ^ bit) for i in range(count)])  31 us
    ppermute x21, starting transfers between devices, partner(): return lax.ppermute(x, axis, [(i, i ^ bit) for i in range(count)])  18.2 us
    pallas_call x2, Pallas kernels, transform(): pl.pallas_call(functools.partial(transform_kernel, fold, at, sizes, cuts,...  7.73 us
    unnamed x6, local copies, waits for them, and re-layouts  3.94 us
    pallas_call x1, Pallas kernels, cosine_tables(): pl.pallas_call(functools.partial(table_kernel, total, cols, fold, 128), o...  3.79 us
    pallas_call x1, Pallas kernels, stencil(): pl.pallas_call(functools.partial(stencil_kernel, fold), out_shape=outs, i...  2.73 us
    pallas_call x1, Pallas kernels, solve(): pl.pallas_call(functools.partial(solve_kernel, fold, groups, cuts), out_s...  2.71 us
    pallas_call x1, Pallas kernels, lead(): pl.pallas_call(functools.partial(lead_kernel, fold), out_shape=outs, in_s...  1.53 us
  transfers between devices with their start and end apart: 22, of which 11 were waited for; matrix products, arithmetic and copies ran while one was open for 0% of the time, Pallas kernels for 16%

commit v1 on v0

--- a/solution.py
+++ b/solution.py
@@ -38,7 +38,7 @@
 
 
 def chunks(sub):
-    later = max(sub // 4, REACH)
+    later = max(5 * sub // 16, REACH)
     return sub - later, later
 
 
@@ -59,8 +59,8 @@
     return first, second
 
 
-def lead_kernel(fold, idx, u_in, wall_in, damping_in, *refs):
-    sends, (near, far, u, wall, damping, sems) = refs[: fold - 1], refs[fold - 1 :]
+def lead_kernel(fold, idx, u_in, wall_in, *refs):
+    sends, (near, far, u, wall, sems) = refs[: fold - 1], refs[fold - 1 :]
     cells = u.shape[0]
     sub = cells // fold
     size = chunks(sub)[0]
@@ -69,18 +69,13 @@
     rows = {r: pl.ds((me ^ r) * sub, sub) for r in order}
     u_copies = [pltpu.make_async_copy(u_in.at[rows[r]], u.at[rows[r]], sems.at[0, r]) for r in order]
     w_copies = {r: pltpu.make_async_copy(wall_in.at[rows[r]], wall.at[rows[r]], sems.at[1, r]) for r in order}
-    d_copy = pltpu.make_async_copy(damping_in, damping, sems.at[2, 0])
     for copy in u_copies:
         copy.start()
-    d_copy.start()
     for r in order:
         w_copies[r].start()
     for copy in u_copies:
         copy.wait()
     even = row % 2 == 0
-    near[...] = u[pl.ds(jnp.where(even, cells - REACH, 0), REACH)]
-    far[...] = u[pl.ds(jnp.where(even, 0, cells - REACH), REACH)]
-    d_copy.wait()
     for r in order[:-1]:
         start = chunk_start(me ^ r, 0, sub)
         w_copies[r].wait()
@@ -91,26 +86,26 @@
             return 0
 
         lax.fori_loop(0, size, step, 0, unroll=2)
-        sends[r - 1][size] = damping[...]
+    near[...] = u[pl.ds(jnp.where(even, cells - REACH, 0), REACH)]
+    far[...] = u[pl.ds(jnp.where(even, 0, cells - REACH), REACH)]
     w_copies[0].wait()
 
 
-def lead(fold, idx, u, wall, damping):
+def lead(fold, idx, u, wall):
     cells, planes, cols = u.shape
     size = chunks(cells // fold)[0]
     shape = lambda n: jax.ShapeDtypeStruct((n, planes, cols), F32)
-    outs = [shape(size + 1)] * (fold - 1) + [shape(REACH)] * 2 + [shape(cells)] * 2
-    outs += [jax.ShapeDtypeStruct((planes, cols), F32)]
+    outs = [shape(size)] * (fold - 1) + [shape(REACH)] * 2 + [shape(cells)] * 2
     return pl.pallas_call(
         functools.partial(lead_kernel, fold),
         out_shape=outs,
-        in_specs=smem(1) + hbm(3),
+        in_specs=smem(1) + hbm(2),
         out_specs=vmem(len(outs)),
-        scratch_shapes=[pltpu.SemaphoreType.DMA((3, fold))],
-        compiler_params=params(),
+        scratch_shapes=[pltpu.SemaphoreType.DMA((2, fold))],
+        compiler_params=params(48 * MIB),
         cost_estimate=pl.CostEstimate(flops=cells * planes * cols * 6, bytes_accessed=cells * planes * cols * 6, transcendentals=0),
         name="lead",
-    )(idx, u, wall, damping)
+    )(idx, u, wall)
 
 
 def stencil_kernel(fold, idx, u, wall, near, far, second_out, *refs):
@@ -249,16 +244,13 @@
     take = iter(refs)
     xs = [next(take) for _ in range(fold)]
     tables = [next(take) for _ in range(4)]
+    damp = [next(take) for _ in range(fold)]
     if last:
-        damp = next(take)
         earlier = next(take)
-    else:
-        own_damp = next(take)
     outs = [[next(take) for _ in pieces] for pieces in cuts]
     if last:
         ends = [next(take) for _ in range(fold)]
     else:
-        damp = next(take)
         ends_all = next(take)
     parts = [next(take) for _ in range(2)]
     half = sizes[last]
@@ -283,10 +275,6 @@
         return 0
 
     lax.fori_loop(0, half, fold_cell, 0)
-    if not last:
-        damp[0] = own_damp[...]
-        for r in range(1, fold):
-            damp[r] = xs[r][half]
 
     rows = half * planes
     modes = cols // 2
@@ -311,7 +299,7 @@
     for r in range(fold):
         for t in range(tiles):
             at_lanes = pl.ds(t * LANES, LANES)
-            d = damp[r, :, at_lanes]
+            d = damp[r][:, at_lanes]
             w = weight_of(d)
             f = jnp.zeros_like(d)
             forward = []
@@ -343,7 +331,7 @@
     if last:
         outs += [shape(2, planes, cols)] * fold
     else:
-        outs += [shape(fold, planes, cols), shape(2, fold, planes, cols)]
+        outs += [shape(2, fold, planes, cols)]
     rows = half * planes
     return pl.pallas_call(
         functools.partial(transform_kernel, fold, at, sizes, cuts, last),
@@ -459,7 +447,42 @@
     )(idx, damping, *ends, *extra)
 
 
-def solve_kernel(fold, groups, cuts, idx, damping, *refs):
+def place(fold, cuts, me, sub):
+    return [
+        (chunk_start(me ^ r, h, sub) + low, high - low)
+        for h in range(2)
+        for r in range(fold)
+        for low, high in cuts[h][r]
+    ]
+
+
+def gather_kernel(fold, cuts, chosen, idx, *refs):
+    pieces, (gathered, out, sems) = refs[: len(chosen)], refs[len(chosen) :]
+    places = place(fold, cuts, idx[0], gathered.shape[0] // fold)
+    copies = []
+    for n, k in enumerate(chosen):
+        rows = pl.ds(*places[k])
+        gathered[rows] = pieces[n][...]
+        copies.append(pltpu.make_async_copy(gathered.at[rows], out.at[rows], sems.at[n]))
+        copies[n].start()
+    for copy in copies:
+        copy.wait()
+
+
+def gather(fold, cuts, idx, pieces, chosen, shape):
+    return pl.pallas_call(
+        functools.partial(gather_kernel, fold, cuts, chosen),
+        out_shape=[jax.ShapeDtypeStruct(shape, F32)] * 2,
+        in_specs=smem(1) + vmem(len(chosen)),
+        out_specs=vmem(1) + hbm(1),
+        scratch_shapes=[pltpu.SemaphoreType.DMA((len(chosen),))],
+        compiler_params=params(),
+        cost_estimate=pl.CostEstimate(flops=math.prod(shape), bytes_accessed=8 * math.prod(shape), transcendentals=0),
+        name="gather",
+    )(idx, *[pieces[k] for k in chosen])
+
+
+def solve_kernel(fold, groups, cuts, chosen, idx, damping, *refs):
     stage = len(groups) - 1
     count = 1 << len(groups[stage])
     ends, rest = refs[:count], refs[count:]
@@ -467,21 +490,18 @@
         entry, rest = rest[0], rest[1:]
     else:
         entry = None
-    count = sum(len(c) for part in cuts for c in part)
-    pieces, rest = rest[:count], rest[count:]
-    coefficients_out, pressure_out, coefficients, pressure, entered, c_sems, p_sems = rest
+    pieces, rest = rest[: len(chosen)], rest[len(chosen) :]
+    _, _, coefficients, coefficients_out, pressure_out, pressure, entered, c_sems, p_sems = rest
     cells = coefficients.shape[0]
     sub = cells // fold
     half = sub // 2
+    places = place(fold, cuts, idx[0], sub)
     copies = []
-    for h in range(2):
-        for r in range(fold):
-            for low, high in cuts[h][r]:
-                rows = pl.ds(chunk_start(idx[0] ^ r, h, sub) + low, high - low)
-                k = len(copies)
-                coefficients[rows] = pieces[k][...]
-                copies.append(pltpu.make_async_copy(coefficients.at[rows], coefficients_out.at[rows], c_sems.at[k]))
-                copies[k].start()
+    for n, k in enumerate(chosen):
+        rows = pl.ds(*places[k])
+        coefficients[rows] = pieces[n][...]
+        copies.append(pltpu.make_async_copy(coefficients.at[rows], coefficients_out.at[rows], c_sems.at[n]))
+        copies[n].start()
 
     def put(at, union, entry):
         entered[0, :, at], entered[1, :, at] = entry
@@ -514,53 +534,58 @@
         copy.wait()
 
 
-def solve(fold, groups, cuts, idx, damping, ends, entry, pieces, cells):
-    planes, cols = damping.shape
-    shape = (cells, planes, cols)
+def solve(fold, groups, cuts, idx, damping, ends, entry, pieces, chosen, gathered, partly):
     extra = [entry] if len(groups) > 2 else []
+    operands = [idx, damping, *ends, *extra, *[pieces[k] for k in chosen], gathered, partly]
+    shape = jax.ShapeDtypeStruct(gathered.shape, F32)
     return pl.pallas_call(
-        functools.partial(solve_kernel, fold, groups, cuts),
-        out_shape=[jax.ShapeDtypeStruct(shape, F32)] * 2,
-        in_specs=smem(1) + vmem(1 + len(ends) + len(extra) + len(pieces)),
-        out_specs=hbm(2),
+        functools.partial(solve_kernel, fold, groups, cuts, chosen),
+        out_shape=[shape] * 3,
+        in_specs=smem(1) + vmem(len(operands) - 2) + hbm(1),
+        out_specs=vmem(1) + hbm(2),
         scratch_shapes=[
-            pltpu.VMEM(shape, F32),
-            pltpu.VMEM(shape, F32),
-            pltpu.VMEM((2, planes, cols), F32),
-            pltpu.SemaphoreType.DMA((len(pieces),)),
+            pltpu.VMEM(gathered.shape, F32),
+            pltpu.VMEM((2,) + damping.shape, F32),
+            pltpu.SemaphoreType.DMA((len(chosen),)),
             pltpu.SemaphoreType.DMA((2 * fold,)),
         ],
+        input_output_aliases={len(operands) - 2: 0, len(operands) - 1: 1},
         compiler_params=params(),
-        cost_estimate=pl.CostEstimate(flops=5 * cells * planes * cols, bytes_accessed=12 * cells * planes * cols, transcendentals=0),
+        cost_estimate=pl.CostEstimate(flops=5 * gathered.size, bytes_accessed=12 * gathered.size, transcendentals=0),
         name="solve",
-    )(idx, damping, *ends, *extra, *pieces)
+    )(*operands)[1:]
 
 
 def body(velocity_u, wall_strain, damping):
-    cells, _, cols = velocity_u.shape
+    cells, planes, cols = velocity_u.shape
     fold = lax.axis_size("gy")
     sub = cells // fold
     me, row = lax.axis_index("gy"), lax.axis_index("gx")
     idx = jnp.stack([me, row]).astype(jnp.int32)
     order = list(range(fold - 1, 0, -1))
-    *sends, near, far, u, wall, damping = lead(fold, idx, velocity_u, wall_strain, damping)
+    *sends, near, far, u, wall = lead(fold, idx, velocity_u, wall_strain)
     got = {(r, 0): partner(sends[r - 1], "gy", r) for r in order}
     near, far = exchange_edges(near, far)
+    damp = {0: damping}
+    bit = fold // 2
+    while bit:
+        damp |= {r ^ bit: partner(x, "gy", bit) for r, x in damp.items()}
+        bit //= 2
+    damp = [damp[r] for r in range(fold)]
     second, own, *sends = stencil(fold, idx, u, wall, near, far)
     for r in order:
         got[r, 1] = partner(sends[r - 1], "gy", r)
     tables = cosine_tables(fold, idx, cols)
     cuts = pieces_of(fold, sub)
-    first = transform(fold, idx, sub, cuts[0], 0, [own] + [got[r, 0] for r in range(1, fold)], tables, [damping])
-    every_damping, ends_a = first[-2:]
-    extra = [every_damping, ends_a]
+    first = transform(fold, idx, sub, cuts[0], 0, [own] + [got[r, 0] for r in range(1, fold)], tables, damp)
+    extra = [*damp, first[-1]]
     rest = transform(fold, idx, sub, cuts[1], 1, [own] + [got[r, 1] for r in range(1, fold)], tables, extra)
     ends_b = rest[-fold:]
     pieces = []
     for h, outs in enumerate((first, rest)):
         outs = iter(outs)
         for r in range(fold):
-            for _ in range(len(cuts[h][r])):
+            for k in range(len(cuts[h][r])):
                 out = next(outs)
                 pieces.append(out if r == 0 else partner(out, "gy", r))
     groups = stages(fold, lax.axis_size("gx"))
@@ -570,7 +595,14 @@
         mine, *entries = combined(groups, stage - 1, sub, idx, damping, ends, entry)
         entry = entries[0] if entries else None
         ends = [mine] + [partner(mine, "gx", o) for o in peers(groups[stage])[1:]]
-    coefficients, pressure = solve(fold, groups, cuts, idx, damping, ends, entry, pieces, cells)
+    late, k = [], 0
+    for h in range(2):
+        for r in range(fold):
+            late += [k + n for n in range(len(cuts[h][r])) if h == 1 and r > 1]
+            k += len(cuts[h][r])
+    early = [n for n in range(k) if n not in late]
+    gathered, partly = gather(fold, cuts, idx, pieces, early, (cells, planes, cols))
+    coefficients, pressure = solve(fold, groups, cuts, idx, damping, ends, entry, pieces, late, gathered, partly)
     return second, coefficients, pressure
 
 

time: 74.6 us -> 88.6 us (1.19)
  starting transfers between devices: 18.9 us -> 28.7 us
  waiting for transfers between devices: 31 us -> 36.6 us
  local copies, waits for them, and re-layouts: 3.94 us -> 0.01 us
  Pallas kernels: 19.7 us -> 22.3 us
    ppermute x21 -> x24, starting transfers between devices: 18.2 us -> 28.1 us  [partner(): return lax.ppermute(x, axis, [(i, i ^ bit) for i in range(count)])]
    ppermute x21 -> x24, waiting for transfers between devices: 31 us -> 36.6 us  [partner(): return lax.ppermute(x, axis, [(i, i ^ bit) for i in range(count)])]
    unnamed x6 -> x2, local copies, waits for them, and re-layouts: 3.94 us -> 0.01 us
    pallas_call x1 -> x2, Pallas kernels: 2.71 us -> 4.15 us  [the longest x1 2.32 us: solve(): pl.pallas_call(functools.partial(solve_kernel, fold, groups, cuts, chosen...]
    pallas_call x1, Pallas kernels: 1.53 us -> 2.76 us  [lead(): pl.pallas_call(functools.partial(lead_kernel, fold), out_shape=outs, in_s...]
  transfers between devices with their start and end apart: 22 -> 25, of which waited for: 11 -> 10; matrix products, arithmetic and copies ran while one was open for 0% -> 0% of each run, Pallas kernels for 16% -> 15%
where the time goes in v1:
time: 88.6 us; the launch traced here: 88.5 us
  waiting for transfers between devices  36.6 us (41%)
  starting transfers between devices  28.7 us (32%)
  Pallas kernels  22.3 us (25%)
    ppermute x24, waiting for transfers between devices, partner(): return lax.ppermute(x, axis, [(i, i ^ bit) for i in range(count)])  36.6 us
    ppermute x24, starting transfers between devices, partner(): return lax.ppermute(x, axis, [(i, i ^ bit) for i in range(count)])  28.1 us
    pallas_call x2, Pallas kernels, transform(): pl.pallas_call(functools.partial(transform_kernel, fold, at, sizes, cuts,...  7.72 us
    pallas_call x1, Pallas kernels, cosine_tables(): pl.pallas_call(functools.partial(table_kernel, total, cols, fold, 128), o...  3.79 us
    pallas_call x1, Pallas kernels, lead(): pl.pallas_call(functools.partial(lead_kernel, fold), out_shape=outs, in_s...  2.76 us
    pallas_call x1, Pallas kernels, stencil(): pl.pallas_call(functools.partial(stencil_kernel, fold), out_shape=outs, i...  2.72 us
    pallas_call x1, Pallas kernels, solve(): pl.pallas_call(functools.partial(solve_kernel, fold, groups, cuts, chosen...  2.32 us
    pallas_call x1, Pallas kernels, gather(): pl.pallas_call(functools.partial(gather_kernel, fold, cuts, chosen), out_...  1.83 us
  transfers between devices with their start and end apart: 25, of which 10 were waited for; matrix products, arithmetic and copies ran while one was open for 0% of the time, Pallas kernels for 15%

profile of v1, /device:TPU:0, one launch (start us, length us, event | category | flops | bytes accessed | tf_op | source)
XLA Modules:
  0.0 88.5 jit_solution(10619669229577606845)
XLA Ops:
  0.7 2.8 %lead.1 = (f32[11,16,512]{2,1,0:T(8,128)S(1)}, f32[11,16,512]{2,1,0:T(8,128)S(1)}, f32[11,16,512]{2,1,0:T(8,128)S(1)}, f32[3,16,512]{2,1,0:T(8,128)S(1)}, f32[3,...) custom-call(s32[2]{0:T(128)S(1)} %pad_add_fusion.idx, f32[64,16,512]{2,1,0:T(8,128)} %u_in.1, ...), custom_call_target="tpu_custom_call" | custom-call | flops 3145728 | bytes 3145728 | tf_op jit(solution)/shard_map/lead/pallas_call | solution.py:99
  4.0 2.6 %collective-permute-start.9 = (f32[11,16,512]{2,1,0:T(8,128)S(1)}, f32[11,16,512]{2,1,0:T(8,128)S(1)}, u32[]{:S(2)}, u32[]{:S(2)}) collective-permute-start(f32[11,16,512]{2,1,0:T(8,128)S(1)} %get-tuple-element.53), channel_id=1, source_target_pairs={{0,2},{1,3},{2,0},{3,1},{4,6},{5,7},{6,4},{7,5},{8,10},{9,11},{10,... | collective-permute-start | bytes 1081352 | tf_op jit(solution)/shard_map/ppermute | solution.py:37
  6.6 1.7 %collective-permute-start.6 = (f32[16,512]{1,0:T(8,128)S(1)}, f32[16,512]{1,0:T(8,128)S(1)}, u32[]{:S(2)}, u32[]{:S(2)}) collective-permute-start(f32[16,512]{1,0:T(8,128)S(1)} %copy-done), channel_id=1, source_target_pairs={{0,2},{1,3},{2,0},{3,1},{4,6},{5,7},{6,4},{7,5},{8,10},{9,11},{10,... | collective-permute-start | bytes 98312 | tf_op jit(solution)/shard_map/ppermute | solution.py:37
  8.4 1.5 %collective-permute-start = (f32[3,16,512]{2,1,0:T(8,128)S(1)}, f32[3,16,512]{2,1,0:T(8,128)S(1)}, u32[]{:S(2)}, u32[]{:S(2)}) collective-permute-start(f32[3,16,512]{2,1,0:T(8,128)S(1)} %get-tuple-element.41), channel_id=1, source_target_pairs={{0,4},{4,0},{8,12},{12,8},{16,20},{20,16},{24,28},{28,24},{1,5},{5... | collective-permute-start | bytes 294920 | tf_op jit(solution)/shard_map/ppermute | solution.py:37
  9.9 14.1 %collective-permute-done.6.refs_10_ = f32[16,512]{1,0:T(8,128)S(1)} collective-permute-done((f32[16,512]{1,0:T(8,128)S(1)}, f32[16,512]{1,0:T(8,128)S(1)}, u32[]{:S(2)}, u32[]{:S(2)}) %collective-permute-start.6) | collective-permute-done | bytes 32800 | tf_op jit(solution)/shard_map/ppermute | solution.py:37
  25.3 3.8 %table.1 = (bf16[1024,1024]{1,0:T(8,128)(2,1)S(1)}, bf16[1024,1024]{1,0:T(8,128)(2,1)S(1)}, bf16[1024,1024]{1,0:T(8,128)(2,1)S(1)}, bf16[1024,1024]{1,0:T(8,128)(2,1)S(1)}) custom-call(s32[2]{0:T(128)S(1)} %pad_add_fusion.idx), custom_call_target="tpu_custom_call" | custom-call | flops 62914560 | bytes 8388608 | tf_op jit(solution)/shard_map/table/pallas_call | solution.py:223
  29.1 2.7 %stencil.1 = (f32[64,16,512]{2,1,0:T(8,128)}, f32[16,16,512]{2,1,0:T(8,128)S(1)}, f32[5,16,512]{2,1,0:T(8,128)S(1)}, f32[5,16,512]{2,1,0:T(8,128)S(1)}, f32[5,16,512]{2,1,0:T(8,128)S(1)}) custom-call(s32[2]{0:T(128)S(1)} %pad_add_fusion.idx, f32[64,16,512]{2,1,0:T(8,128)S(1)} %get-tuple-element.39.u, f32[64,16,512]{2,1,0:T(8,128)S(1)} %get-tuple-element.40.wall, ...), custom_call_target="tpu_custom_call" | custom-call | flops 10485760 | bytes 8388608 | tf_op jit(solution)/shard_map/stencil/pallas_call | solution.py:150
  32.0 1.7 %collective-permute-start.3 = (f32[5,16,512]{2,1,0:T(8,128)S(1)}, f32[5,16,512]{2,1,0:T(8,128)S(1)}, u32[]{:S(2)}, u32[]{:S(2)}) collective-permute-start(f32[5,16,512]{2,1,0:T(8,128)S(1)} %get-tuple-element.46), channel_id=1, source_target_pairs={{0,2},{1,3},{2,0},{3,1},{4,6},{5,7},{6,4},{7,5},{8,10},{9,11},{10,... | collective-permute-start | bytes 491528 | tf_op jit(solution)/shard_map/ppermute | solution.py:37
  33.8 4.6 %transform_a.1 = (f32[11,16,512]{2,1,0:T(8,128)S(1)}, f32[11,16,512]{2,1,0:T(8,128)S(1)}, f32[11,16,512]{2,1,0:T(8,128)S(1)}, f32[5,16,512]{2,1,0:T(8,128)S(1)},...) custom-call(s32[2]{0:T(128)S(1)} %pad_add_fusion.idx, f32[16,16,512]{2,1,0:T(8,128)S(1)} %get-tuple-element.44.refs_0_, ...), custom_call_target="tpu_custom_call" | custom-call | flops 2214592512 | bytes 8388608 | tf_op jit(solution)/shard_map/transform_a/pallas_call | solution.py:336
  39.0 2.4 %collective-permute-done.4.refs_3_ = f32[5,16,512]{2,1,0:T(8,128)S(1)} collective-permute-done((f32[5,16,512]{2,1,0:T(8,128)S(1)}, f32[5,16,512]{2,1,0:T(8,128)S(1)}, u32[]{:S(2)}, u32[]{:S(2)}) %collective-permute-start.4) | collective-permute-done | bytes 163872 | tf_op jit(solution)/shard_map/ppermute | solution.py:37
  41.5 3.1 %transform_b.1 = (f32[5,16,512]{2,1,0:T(8,128)S(1)}, f32[5,16,512]{2,1,0:T(8,128)S(1)}, f32[5,16,512]{2,1,0:T(8,128)S(1)}, f32[5,16,512]{2,1,0:T(8,128)S(1)}, f3...) custom-call(s32[2]{0:T(128)S(1)} %pad_add_fusion.idx, ...), custom_call_target="tpu_custom_call" | custom-call | flops 1006632960 | bytes 8388608 | tf_op jit(solution)/shard_map/transform_b/pallas_call | solution.py:336
  45.0 1.7 %collective-permute-start.12 = (f32[2,16,512]{2,1,0:T(8,128)S(1)}, f32[2,16,512]{2,1,0:T(8,128)S(1)}, u32[]{:S(2)}, u32[]{:S(2)}) collective-permute-start(f32[2,16,512]{2,1,0:T(8,128)S(1)} %get-tuple-element.58), channel_id=1, source_target_pairs={{0,2},{1,3},{2,0},{3,1},{4,6},{5,7},{6,4},{7,5},{8,10},{9,11},{10,... | collective-permute-start | bytes 196616 | tf_op jit(solution)/shard_map/ppermute | solution.py:37
  46.8 2.5 %collective-permute-done.12.refs_2_ = f32[2,16,512]{2,1,0:T(8,128)S(1)} collective-permute-done((f32[2,16,512]{2,1,0:T(8,128)S(1)}, f32[2,16,512]{2,1,0:T(8,128)S(1)}, u32[]{:S(2)}, u32[]{:S(2)}) %collective-permute-start.12) | collective-permute-done | bytes 65568 | tf_op jit(solution)/shard_map/ppermute | solution.py:37
  49.3 1.8 %collective-permute-done.13.refs_3_ = f32[2,16,512]{2,1,0:T(8,128)S(1)} collective-permute-done((f32[2,16,512]{2,1,0:T(8,128)S(1)}, f32[2,16,512]{2,1,0:T(8,128)S(1)}, u32[]{:S(2)}, u32[]{:S(2)}) %collective-permute-start.13) | collective-permute-done | bytes 65568 | tf_op jit(solution)/shard_map/ppermute | solution.py:37
  51.7 8.8 %collective-permute-start.16 = (f32[2,16,512]{2,1,0:T(8,128)S(1)}, f32[2,16,512]{2,1,0:T(8,128)S(1)}, u32[]{:S(2)}, u32[]{:S(2)}) collective-permute-start(f32[2,16,512]{2,1,0:T(8,128)S(1)} %shard_map.58.refs_0_), channel_id=1, source_target_pairs={{0,12},{4,8},{8,4},{12,0},{16,28},{20,24},{24,20},{28,16},{1,13},{... | collective-permute-start | bytes 196616 | tf_op jit(solution)/shard_map/ppermute | solution.py:37
  62.9 2.1 %collective-permute-start.14 = (f32[2,16,512]{2,1,0:T(8,128)S(1)}, f32[2,16,512]{2,1,0:T(8,128)S(1)}, u32[]{:S(2)}, u32[]{:S(2)}) collective-permute-start(f32[2,16,512]{2,1,0:T(8,128)S(1)} %shard_map.58.refs_0_), channel_id=1, source_target_pairs={{0,4},{4,0},{8,12},{12,8},{16,20},{20,16},{24,28},{28,24},{1,5},{5... | collective-permute-start | bytes 196616 | tf_op jit(solution)/shard_map/ppermute | solution.py:37
  65.0 2.2 %collective-permute-done.14.refs_1_ = f32[2,16,512]{2,1,0:T(8,128)S(1)} collective-permute-done((f32[2,16,512]{2,1,0:T(8,128)S(1)}, f32[2,16,512]{2,1,0:T(8,128)S(1)}, u32[]{:S(2)}, u32[]{:S(2)}) %collective-permute-start.14) | collective-permute-done | bytes 65568 | tf_op jit(solution)/shard_map/ppermute | solution.py:37
  68.2 6.7 %collective-permute-done.22.refs_3_ = f32[5,16,512]{2,1,0:T(8,128)S(1)} collective-permute-done((f32[5,16,512]{2,1,0:T(8,128)S(1)}, f32[5,16,512]{2,1,0:T(8,128)S(1)}, u32[]{:S(2)}, u32[]{:S(2)}) %collective-permute-start.22) | collective-permute-done | bytes 163872 | tf_op jit(solution)/shard_map/ppermute | solution.py:37
  74.9 1.2 %collective-permute-start.19 = (f32[5,16,512]{2,1,0:T(8,128)S(1)}, f32[5,16,512]{2,1,0:T(8,128)S(1)}, u32[]{:S(2)}, u32[]{:S(2)}) collective-permute-start(f32[5,16,512]{2,1,0:T(8,128)S(1)} %get-tuple-element.63), channel_id=1, source_target_pairs={{0,3},{1,2},{2,1},{3,0},{4,7},{5,6},{6,5},{7,4},{8,11},{9,10},{10,... | collective-permute-start | bytes 491528 | tf_op jit(solution)/shard_map/ppermute | solution.py:37
  76.7 2.4 %collective-permute-done.23.refs_4_ = f32[6,16,512]{2,1,0:T(8,128)S(1)} collective-permute-done((f32[6,16,512]{2,1,0:T(8,128)S(1)}, f32[6,16,512]{2,1,0:T(8,128)S(1)}, u32[]{:S(2)}, u32[]{:S(2)}) %collective-permute-start.23) | collective-permute-done | bytes 196640 | tf_op jit(solution)/shard_map/ppermute | solution.py:37
  79.1 2.6 %collective-permute-start.17 = (f32[2,16,512]{2,1,0:T(8,128)S(1)}, f32[2,16,512]{2,1,0:T(8,128)S(1)}, u32[]{:S(2)}, u32[]{:S(2)}) collective-permute-start(f32[2,16,512]{2,1,0:T(8,128)S(1)} %get-tuple-element.60.refs_0_), channel_id=1, source_target_pairs={{0,16},{4,20},{8,24},{12,28},{16,0},{20,4},{24,8},{28,12},{1,17},{... | collective-permute-start | bytes 196616 | tf_op jit(solution)/shard_map/ppermute | solution.py:37
  81.7 1.8 %gather.1 = (f32[64,16,512]{2,1,0:T(8,128)S(1)}, f32[64,16,512]{2,1,0:T(8,128)}) custom-call(s32[2]{0:T(128)S(1)} %pad_add_fusion.idx, f32[11,16,512]{2,1,0:T(8,128)S(1)} %get-tuple-element.64.refs_0_, f32[11,16,512]{2,1,0:T(8,128)S(1)} %collective-permute-done.20.refs_1_, f32[11,16,512]{2,1,0:T(8,128)S(1)} %collective-permute-done.21.refs_2_, ...), custom_call_target="tpu_custom_call" | custom-call | flops 524288 | bytes 4194304 | tf_op jit(solution)/shard_map/gather/pallas_call | solution.py:473
  83.6 2.6 %collective-permute-done.19.refs_4_ = f32[5,16,512]{2,1,0:T(8,128)S(1)} collective-permute-done((f32[5,16,512]{2,1,0:T(8,128)S(1)}, f32[5,16,512]{2,1,0:T(8,128)S(1)}, u32[]{:S(2)}, u32[]{:S(2)}) %collective-permute-start.19) | collective-permute-done | bytes 163872 | tf_op jit(solution)/shard_map/ppermute | solution.py:37
  86.2 2.3 %solve.1 = (f32[64,16,512]{2,1,0:T(8,128)S(1)}, f32[64,16,512]{2,1,0:T(8,128)}, f32[64,16,512]{2,1,0:T(8,128)}) custom-call(s32[2]{0:T(128)S(1)} %pad_add_fusion.idx, f32[16,512]{1,0:T(8,128)S(1)} %copy-done, f32[2,16,512]{2,1,0:T(8,128)S(1)} %get-tuple-element.60.refs_0_, ...), custom_call_target="tpu_custom_call", output_to_operand_aliasing={{0}: (7, {}), {1}: (8, {})} | custom-call | flops 2621440 | bytes 6291456 | tf_op jit(solution)/shard_map/solve/pallas_call | solution.py:541
  (38 shorter events, 7.8 us)
Async XLA Ops:
  3.5 30.2 %collective-permute-start.8 = (f32[11,16,512]{2,1,0:T(8,128)S(1)}, f32[11,16,512]{2,1,0:T(8,128)S(1)}, u32[]{:S(2)}, u32[]{:S(2)}) collective-permute-start(f32[11,16,512]{2,1,0:T(8,128)S(1)} %get-tuple-element.52), channel_id=1, source_target_pairs={{0,1},{1,0},{2,3},{3,2},{4,5},{5,4},{6,7},{7,6},{8,9},{9,8},{10,11... | collective-permute-start | bytes 1081352 | tf_op jit(solution)/shard_map/ppermute | solution.py:37
  4.0 29.8 %collective-permute-start.9 = (f32[11,16,512]{2,1,0:T(8,128)S(1)}, f32[11,16,512]{2,1,0:T(8,128)S(1)}, u32[]{:S(2)}, u32[]{:S(2)}) collective-permute-start(f32[11,16,512]{2,1,0:T(8,128)S(1)} %get-tuple-element.53), channel_id=1, source_target_pairs={{0,2},{1,3},{2,0},{3,1},{4,6},{5,7},{6,4},{7,5},{8,10},{9,11},{10,... | collective-permute-start | bytes 1081352 | tf_op jit(solution)/shard_map/ppermute | solution.py:37
  6.6 27.2 %collective-permute-start.10 = (f32[11,16,512]{2,1,0:T(8,128)S(1)}, f32[11,16,512]{2,1,0:T(8,128)S(1)}, u32[]{:S(2)}, u32[]{:S(2)}) collective-permute-start(f32[11,16,512]{2,1,0:T(8,128)S(1)} %get-tuple-element.54), channel_id=1, source_target_pairs={{0,3},{1,2},{2,1},{3,0},{4,7},{5,6},{6,5},{7,4},{8,11},{9,10},{10,... | collective-permute-start | bytes 1081352 | tf_op jit(solution)/shard_map/ppermute | solution.py:37
  6.6 17.4 %collective-permute-start.6 = (f32[16,512]{1,0:T(8,128)S(1)}, f32[16,512]{1,0:T(8,128)S(1)}, u32[]{:S(2)}, u32[]{:S(2)}) collective-permute-start(f32[16,512]{1,0:T(8,128)S(1)} %copy-done), channel_id=1, source_target_pairs={{0,2},{1,3},{2,0},{3,1},{4,6},{5,7},{6,4},{7,5},{8,10},{9,11},{10,... | collective-permute-start | bytes 98312 | tf_op jit(solution)/shard_map/ppermute | solution.py:37
  8.4 16.3 %collective-permute-start = (f32[3,16,512]{2,1,0:T(8,128)S(1)}, f32[3,16,512]{2,1,0:T(8,128)S(1)}, u32[]{:S(2)}, u32[]{:S(2)}) collective-permute-start(f32[3,16,512]{2,1,0:T(8,128)S(1)} %get-tuple-element.41), channel_id=1, source_target_pairs={{0,4},{4,0},{8,12},{12,8},{16,20},{20,16},{24,28},{28,24},{1,5},{5... | collective-permute-start | bytes 294920 | tf_op jit(solution)/shard_map/ppermute | solution.py:37
  24.7 7.1 %collective-permute-start.5 = (f32[16,512]{1,0:T(8,128)S(1)}, f32[16,512]{1,0:T(8,128)S(1)}, u32[]{:S(2)}, u32[]{:S(2)}) collective-permute-start(f32[16,512]{1,0:T(8,128)S(1)} %copy-done), channel_id=1, source_target_pairs={{0,1},{1,0},{2,3},{3,2},{4,5},{5,4},{6,7},{7,6},{8,9},{9,8},{10,11... | collective-permute-start | bytes 98312 | tf_op jit(solution)/shard_map/ppermute | solution.py:37
  24.8 7.2 %collective-permute-start.7 = (f32[16,512]{1,0:T(8,128)S(1)}, f32[16,512]{1,0:T(8,128)S(1)}, u32[]{:S(2)}, u32[]{:S(2)}) collective-permute-start(f32[16,512]{1,0:T(8,128)S(1)} %collective-permute-done.6.refs_10_), channel_id=1, source_target_pairs={{0,1},{1,0},{2,3},{3,2},{4,5},{5,4},{6,7},{7,6},{8,9},{9,8},{10,11... | collective-permute-start | bytes 98312 | tf_op jit(solution)/shard_map/ppermute | solution.py:37
  31.8 6.6 %collective-permute-start.2 = (f32[5,16,512]{2,1,0:T(8,128)S(1)}, f32[5,16,512]{2,1,0:T(8,128)S(1)}, u32[]{:S(2)}, u32[]{:S(2)}) collective-permute-start(f32[5,16,512]{2,1,0:T(8,128)S(1)} %get-tuple-element.45), channel_id=1, source_target_pairs={{0,1},{1,0},{2,3},{3,2},{4,5},{5,4},{6,7},{7,6},{8,9},{9,8},{10,11... | collective-permute-start | bytes 491528 | tf_op jit(solution)/shard_map/ppermute | solution.py:37
  32.0 7.1 %collective-permute-start.3 = (f32[5,16,512]{2,1,0:T(8,128)S(1)}, f32[5,16,512]{2,1,0:T(8,128)S(1)}, u32[]{:S(2)}, u32[]{:S(2)}) collective-permute-start(f32[5,16,512]{2,1,0:T(8,128)S(1)} %get-tuple-element.46), channel_id=1, source_target_pairs={{0,2},{1,3},{2,0},{3,1},{4,6},{5,7},{6,4},{7,5},{8,10},{9,11},{10,... | collective-permute-start | bytes 491528 | tf_op jit(solution)/shard_map/ppermute | solution.py:37
  33.7 7.7 %collective-permute-start.4 = (f32[5,16,512]{2,1,0:T(8,128)S(1)}, f32[5,16,512]{2,1,0:T(8,128)S(1)}, u32[]{:S(2)}, u32[]{:S(2)}) collective-permute-start(f32[5,16,512]{2,1,0:T(8,128)S(1)} %get-tuple-element.47), channel_id=1, source_target_pairs={{0,3},{1,2},{2,1},{3,0},{4,7},{5,6},{6,5},{7,4},{8,11},{9,10},{10,... | collective-permute-start | bytes 491528 | tf_op jit(solution)/shard_map/ppermute | solution.py:37
  44.6 2.2 %collective-permute-start.11 = (f32[2,16,512]{2,1,0:T(8,128)S(1)}, f32[2,16,512]{2,1,0:T(8,128)S(1)}, u32[]{:S(2)}, u32[]{:S(2)}) collective-permute-start(f32[2,16,512]{2,1,0:T(8,128)S(1)} %get-tuple-element.57), channel_id=1, source_target_pairs={{0,1},{1,0},{2,3},{3,2},{4,5},{5,4},{6,7},{7,6},{8,9},{9,8},{10,11... | collective-permute-start | bytes 196616 | tf_op jit(solution)/shard_map/ppermute | solution.py:37
  45.0 4.3 %collective-permute-start.12 = (f32[2,16,512]{2,1,0:T(8,128)S(1)}, f32[2,16,512]{2,1,0:T(8,128)S(1)}, u32[]{:S(2)}, u32[]{:S(2)}) collective-permute-start(f32[2,16,512]{2,1,0:T(8,128)S(1)} %get-tuple-element.58), channel_id=1, source_target_pairs={{0,2},{1,3},{2,0},{3,1},{4,6},{5,7},{6,4},{7,5},{8,10},{9,11},{10,... | collective-permute-start | bytes 196616 | tf_op jit(solution)/shard_map/ppermute | solution.py:37
  46.8 4.3 %collective-permute-start.13 = (f32[2,16,512]{2,1,0:T(8,128)S(1)}, f32[2,16,512]{2,1,0:T(8,128)S(1)}, u32[]{:S(2)}, u32[]{:S(2)}) collective-permute-start(f32[2,16,512]{2,1,0:T(8,128)S(1)} %get-tuple-element.59), channel_id=1, source_target_pairs={{0,3},{1,2},{2,1},{3,0},{4,7},{5,6},{6,5},{7,4},{8,11},{9,10},{10,... | collective-permute-start | bytes 196616 | tf_op jit(solution)/shard_map/ppermute | solution.py:37
  51.7 11.2 %collective-permute-start.16 = (f32[2,16,512]{2,1,0:T(8,128)S(1)}, f32[2,16,512]{2,1,0:T(8,128)S(1)}, u32[]{:S(2)}, u32[]{:S(2)}) collective-permute-start(f32[2,16,512]{2,1,0:T(8,128)S(1)} %shard_map.58.refs_0_), channel_id=1, source_target_pairs={{0,12},{4,8},{8,4},{12,0},{16,28},{20,24},{24,20},{28,16},{1,13},{... | collective-permute-start | bytes 196616 | tf_op jit(solution)/shard_map/ppermute | solution.py:37
  60.6 4.4 %collective-permute-start.15 = (f32[2,16,512]{2,1,0:T(8,128)S(1)}, f32[2,16,512]{2,1,0:T(8,128)S(1)}, u32[]{:S(2)}, u32[]{:S(2)}) collective-permute-start(f32[2,16,512]{2,1,0:T(8,128)S(1)} %shard_map.58.refs_0_), channel_id=1, source_target_pairs={{0,8},{4,12},{8,0},{12,4},{16,24},{20,28},{24,16},{28,20},{1,9},{5... | collective-permute-start | bytes 196616 | tf_op jit(solution)/shard_map/ppermute | solution.py:37
  61.0 20.7 %collective-permute-start.20 = (f32[11,16,512]{2,1,0:T(8,128)S(1)}, f32[11,16,512]{2,1,0:T(8,128)S(1)}, u32[]{:S(2)}, u32[]{:S(2)}) collective-permute-start(f32[11,16,512]{2,1,0:T(8,128)S(1)} %get-tuple-element.65), channel_id=1, source_target_pairs={{0,1},{1,0},{2,3},{3,2},{4,5},{5,4},{6,7},{7,6},{8,9},{9,8},{10,11... | collective-permute-start | bytes 1081352 | tf_op jit(solution)/shard_map/ppermute | solution.py:37
  61.0 20.7 %collective-permute-start.21 = (f32[11,16,512]{2,1,0:T(8,128)S(1)}, f32[11,16,512]{2,1,0:T(8,128)S(1)}, u32[]{:S(2)}, u32[]{:S(2)}) collective-permute-start(f32[11,16,512]{2,1,0:T(8,128)S(1)} %get-tuple-element.66), channel_id=1, source_target_pairs={{0,2},{1,3},{2,0},{3,1},{4,6},{5,7},{6,4},{7,5},{8,10},{9,11},{10,... | collective-permute-start | bytes 1081352 | tf_op jit(solution)/shard_map/ppermute | solution.py:37
  61.6 5.7 %collective-permute-start.24 = (f32[5,16,512]{2,1,0:T(8,128)S(1)}, f32[5,16,512]{2,1,0:T(8,128)S(1)}, u32[]{:S(2)}, u32[]{:S(2)}) collective-permute-start(f32[5,16,512]{2,1,0:T(8,128)S(1)} %get-tuple-element.70), channel_id=1, source_target_pairs={{0,1},{1,0},{2,3},{3,2},{4,5},{5,4},{6,7},{7,6},{8,9},{9,8},{10,11... | collective-permute-start | bytes 491528 | tf_op jit(solution)/shard_map/ppermute | solution.py:37
  62.9 4.3 %collective-permute-start.14 = (f32[2,16,512]{2,1,0:T(8,128)S(1)}, f32[2,16,512]{2,1,0:T(8,128)S(1)}, u32[]{:S(2)}, u32[]{:S(2)}) collective-permute-start(f32[2,16,512]{2,1,0:T(8,128)S(1)} %shard_map.58.refs_0_), channel_id=1, source_target_pairs={{0,4},{4,0},{8,12},{12,8},{16,20},{20,16},{24,28},{28,24},{1,5},{5... | collective-permute-start | bytes 196616 | tf_op jit(solution)/shard_map/ppermute | solution.py:37
  65.0 9.9 %collective-permute-start.22 = (f32[5,16,512]{2,1,0:T(8,128)S(1)}, f32[5,16,512]{2,1,0:T(8,128)S(1)}, u32[]{:S(2)}, u32[]{:S(2)}) collective-permute-start(f32[5,16,512]{2,1,0:T(8,128)S(1)} %get-tuple-element.67), channel_id=1, source_target_pairs={{0,3},{1,2},{2,1},{3,0},{4,7},{5,6},{6,5},{7,4},{8,11},{9,10},{10,... | collective-permute-start | bytes 491528 | tf_op jit(solution)/shard_map/ppermute | solution.py:37
  67.3 11.9 %collective-permute-start.23 = (f32[6,16,512]{2,1,0:T(8,128)S(1)}, f32[6,16,512]{2,1,0:T(8,128)S(1)}, u32[]{:S(2)}, u32[]{:S(2)}) collective-permute-start(f32[6,16,512]{2,1,0:T(8,128)S(1)} %get-tuple-element.68), channel_id=1, source_target_pairs={{0,3},{1,2},{2,1},{3,0},{4,7},{5,6},{6,5},{7,4},{8,11},{9,10},{10,... | collective-permute-start | bytes 589832 | tf_op jit(solution)/shard_map/ppermute | solution.py:37
  67.3 16.3 %collective-permute-start.18 = (f32[5,16,512]{2,1,0:T(8,128)S(1)}, f32[5,16,512]{2,1,0:T(8,128)S(1)}, u32[]{:S(2)}, u32[]{:S(2)}) collective-permute-start(f32[5,16,512]{2,1,0:T(8,128)S(1)} %get-tuple-element.62), channel_id=1, source_target_pairs={{0,2},{1,3},{2,0},{3,1},{4,6},{5,7},{6,4},{7,5},{8,10},{9,11},{10,... | collective-permute-start | bytes 491528 | tf_op jit(solution)/shard_map/ppermute | solution.py:37
  74.9 11.2 %collective-permute-start.19 = (f32[5,16,512]{2,1,0:T(8,128)S(1)}, f32[5,16,512]{2,1,0:T(8,128)S(1)}, u32[]{:S(2)}, u32[]{:S(2)}) collective-permute-start(f32[5,16,512]{2,1,0:T(8,128)S(1)} %get-tuple-element.63), channel_id=1, source_target_pairs={{0,3},{1,2},{2,1},{3,0},{4,7},{5,6},{6,5},{7,4},{8,11},{9,10},{10,... | collective-permute-start | bytes 491528 | tf_op jit(solution)/shard_map/ppermute | solution.py:37
  79.1 7.0 %collective-permute-start.17 = (f32[2,16,512]{2,1,0:T(8,128)S(1)}, f32[2,16,512]{2,1,0:T(8,128)S(1)}, u32[]{:S(2)}, u32[]{:S(2)}) collective-permute-start(f32[2,16,512]{2,1,0:T(8,128)S(1)} %get-tuple-element.60.refs_0_), channel_id=1, source_target_pairs={{0,16},{4,20},{8,24},{12,28},{16,0},{20,4},{24,8},{28,12},{1,17},{... | collective-permute-start | bytes 196616 | tf_op jit(solution)/shard_map/ppermute | solution.py:37
  (2 other events, 6.7 us)

commit v2 on v1

--- a/solution.py
+++ b/solution.py
@@ -14,6 +14,7 @@
 F32 = jnp.float32
 BF16 = jnp.bfloat16
 MIB = 1024 * 1024
+FIRST_LIMIT = 52 * MIB
 
 
 def params(limit=16 * MIB):
@@ -24,8 +25,8 @@
     return [pl.BlockSpec(memory_space=pltpu.VMEM)] * count
 
 
-def smem(count):
-    return [pl.BlockSpec(memory_space=pltpu.SMEM)] * count
+def at_device(kernel, *static):
+    return lambda *refs: kernel(*static, (lax.axis_index("gy"), lax.axis_index("gx")), *refs)
 
 
 def hbm(count):
@@ -59,53 +60,75 @@
     return first, second
 
 
-def lead_kernel(fold, idx, u_in, wall_in, *refs):
-    sends, (near, far, u, wall, sems) = refs[: fold - 1], refs[fold - 1 :]
+def first_kernel(fold, idx, u_in, wall_in, send, ubuf, wbuf, sems):
+    size = send.shape[0]
+    start = chunk_start(idx[0] ^ (fold - 1), 0, u_in.shape[0] // fold)
+    u_copy = pltpu.make_async_copy(u_in.at[pl.ds(start - REACH, size + 2 * REACH)], ubuf, sems.at[0])
+    w_copy = pltpu.make_async_copy(wall_in.at[pl.ds(start, size)], wbuf, sems.at[1])
+    u_copy.start()
+    w_copy.start()
+    u_copy.wait()
+    w_copy.wait()
+
+    def step(j, _):
+        first, _ = derivatives(lambda k: ubuf[k], j)
+        send[j] = first + wbuf[j]
+        return 0
+
+    lax.fori_loop(0, size, step, 0, unroll=2)
+
+
+def first_cells(fold, u, wall):
+    cells, planes, cols = u.shape
+    size = chunks(cells // fold)[0]
+    return pl.pallas_call(
+        at_device(first_kernel, fold),
+        out_shape=jax.ShapeDtypeStruct((size, planes, cols), F32),
+        in_specs=hbm(2),
+        out_specs=vmem(1)[0],
+        scratch_shapes=[
+            pltpu.VMEM((size + 2 * REACH, planes, cols), F32),
+            pltpu.VMEM((size, planes, cols), F32),
+            pltpu.SemaphoreType.DMA((2,)),
+        ],
+        compiler_params=params(FIRST_LIMIT),
+        cost_estimate=pl.CostEstimate(flops=size * planes * cols * 10, bytes_accessed=size * planes * cols * 12, transcendentals=0),
+        name="first",
+    )(u, wall)
+
+
+def lead_kernel(fold, idx, u, wall, *refs):
+    sends, (near, far) = refs[: fold - 2], refs[fold - 2 :]
     cells = u.shape[0]
     sub = cells // fold
-    size = chunks(sub)[0]
-    me, row = idx[0], idx[1]
-    order = list(range(fold - 1, -1, -1))
-    rows = {r: pl.ds((me ^ r) * sub, sub) for r in order}
-    u_copies = [pltpu.make_async_copy(u_in.at[rows[r]], u.at[rows[r]], sems.at[0, r]) for r in order]
-    w_copies = {r: pltpu.make_async_copy(wall_in.at[rows[r]], wall.at[rows[r]], sems.at[1, r]) for r in order}
-    for copy in u_copies:
-        copy.start()
-    for r in order:
-        w_copies[r].start()
-    for copy in u_copies:
-        copy.wait()
+    me, row = idx
     even = row % 2 == 0
-    for r in order[:-1]:
+    near[...] = u[pl.ds(jnp.where(even, cells - REACH, 0), REACH)]
+    far[...] = u[pl.ds(jnp.where(even, 0, cells - REACH), REACH)]
+    for r in range(fold - 2, 0, -1):
         start = chunk_start(me ^ r, 0, sub)
-        w_copies[r].wait()
 
         def step(j, _, r=r, start=start):
             first, _ = derivatives(lambda k: u[k], start - REACH + j)
             sends[r - 1][j] = first + wall[start + j]
             return 0
 
-        lax.fori_loop(0, size, step, 0, unroll=2)
-    near[...] = u[pl.ds(jnp.where(even, cells - REACH, 0), REACH)]
-    far[...] = u[pl.ds(jnp.where(even, 0, cells - REACH), REACH)]
-    w_copies[0].wait()
-
-
-def lead(fold, idx, u, wall):
+        lax.fori_loop(0, chunks(sub)[0], step, 0, unroll=2)
+
+
+def lead(fold, u, wall):
     cells, planes, cols = u.shape
-    size = chunks(cells // fold)[0]
     shape = lambda n: jax.ShapeDtypeStruct((n, planes, cols), F32)
-    outs = [shape(size)] * (fold - 1) + [shape(REACH)] * 2 + [shape(cells)] * 2
-    return pl.pallas_call(
-        functools.partial(lead_kernel, fold),
+    outs = [shape(chunks(cells // fold)[0])] * (fold - 2) + [shape(REACH)] * 2
+    return pl.pallas_call(
+        at_device(lead_kernel, fold),
         out_shape=outs,
-        in_specs=smem(1) + hbm(2),
+        in_specs=vmem(2),
         out_specs=vmem(len(outs)),
-        scratch_shapes=[pltpu.SemaphoreType.DMA((2, fold))],
-        compiler_params=params(48 * MIB),
+        compiler_params=params(),
         cost_estimate=pl.CostEstimate(flops=cells * planes * cols * 6, bytes_accessed=cells * planes * cols * 6, transcendentals=0),
         name="lead",
-    )(idx, u, wall)
+    )(u, wall)
 
 
 def stencil_kernel(fold, idx, u, wall, near, far, second_out, *refs):
@@ -141,16 +164,16 @@
         copy.wait()
 
 
-def stencil(fold, idx, u, wall, near, far):
+def stencil(fold, u, wall, near, far):
     cells, planes, cols = u.shape
     sub = cells // fold
     later = chunks(sub)[1]
     shape = lambda n: jax.ShapeDtypeStruct((n, planes, cols), F32)
     outs = [shape(cells), shape(sub)] + [shape(later)] * (fold - 1)
     return pl.pallas_call(
-        functools.partial(stencil_kernel, fold),
+        at_device(stencil_kernel, fold),
         out_shape=outs,
-        in_specs=smem(1) + vmem(4),
+        in_specs=vmem(4),
         out_specs=hbm(1) + vmem(len(outs) - 1),
         scratch_shapes=[
             pltpu.VMEM((cells + 2 * REACH, planes, cols), F32),
@@ -160,7 +183,7 @@
         compiler_params=params(),
         cost_estimate=pl.CostEstimate(flops=cells * planes * cols * 20, bytes_accessed=cells * planes * cols * 16, transcendentals=0),
         name="stencil",
-    )(idx, u, wall, near, far)
+    )(u, wall, near, far)
 
 
 def exchange_edges(near, far):
@@ -217,18 +240,17 @@
     lax.fori_loop(0, width // LANES, column, 0)
 
 
-def cosine_tables(fold, idx, cols):
+def cosine_tables(fold, cols):
     total = fold * cols
     side = total // 2
     return pl.pallas_call(
-        functools.partial(table_kernel, total, cols, fold, 128),
+        at_device(table_kernel, total, cols, fold, 128),
         out_shape=[jax.ShapeDtypeStruct((side, side), BF16)] * 4,
-        in_specs=smem(1),
         out_specs=vmem(4),
         compiler_params=params(),
         cost_estimate=pl.CostEstimate(flops=side * side * 60, bytes_accessed=side * side * 8, transcendentals=0),
         name="table",
-    )(idx)
+    )()
 
 
 def weight_of(d):
@@ -320,7 +342,7 @@
                 ends_all[1, r, :, at_lanes] = p
 
 
-def transform(fold, idx, sub, cuts, last, xs, tables, extra):
+def transform(fold, sub, cuts, last, xs, tables, extra):
     planes, cols = xs[0].shape[1:]
     sizes = chunks(sub)
     half = sizes[last]
@@ -334,15 +356,15 @@
         outs += [shape(2, fold, planes, cols)]
     rows = half * planes
     return pl.pallas_call(
-        functools.partial(transform_kernel, fold, at, sizes, cuts, last),
+        at_device(transform_kernel, fold, at, sizes, cuts, last),
         out_shape=outs,
-        in_specs=smem(1) + vmem(len(xs) + 4 + len(extra)),
+        in_specs=vmem(len(xs) + 4 + len(extra)),
         out_specs=vmem(len(outs)),
         scratch_shapes=[pltpu.VMEM((2 * rows, side), BF16)] * 2,
         compiler_params=params(),
         cost_estimate=pl.CostEstimate(flops=12 * rows * side * side, bytes_accessed=8 * side * side, transcendentals=0),
         name="transform_b" if last else "transform_a",
-    )(idx, *xs, *tables, *extra)
+    )(*xs, *tables, *extra)
 
 
 def span(d, cells):
@@ -433,18 +455,18 @@
     combine_tiles(groups, stage, sub, idx, damping, ends, entry, put)
 
 
-def combined(groups, stage, sub, idx, damping, ends, entry):
+def combined(groups, stage, sub, damping, ends, entry):
     pair = jax.ShapeDtypeStruct((2,) + damping.shape, F32)
     extra = [entry] if stage > 1 else []
     outs = [pair, pair] if stage else [pair]
     return pl.pallas_call(
-        functools.partial(combine_kernel, groups, stage, sub),
+        at_device(combine_kernel, groups, stage, sub),
         out_shape=outs,
-        in_specs=smem(1) + vmem(1 + len(ends) + len(extra)),
+        in_specs=vmem(1 + len(ends) + len(extra)),
         out_specs=vmem(len(outs)),
         compiler_params=params(),
         cost_estimate=pl.CostEstimate(flops=100 * damping.size, bytes_accessed=32 * damping.size, transcendentals=0),
-    )(idx, damping, *ends, *extra)
+    )(damping, *ends, *extra)
 
 
 def place(fold, cuts, me, sub):
@@ -469,17 +491,17 @@
         copy.wait()
 
 
-def gather(fold, cuts, idx, pieces, chosen, shape):
-    return pl.pallas_call(
-        functools.partial(gather_kernel, fold, cuts, chosen),
+def gather(fold, cuts, pieces, chosen, shape):
+    return pl.pallas_call(
+        at_device(gather_kernel, fold, cuts, chosen),
         out_shape=[jax.ShapeDtypeStruct(shape, F32)] * 2,
-        in_specs=smem(1) + vmem(len(chosen)),
+        in_specs=vmem(len(chosen)),
         out_specs=vmem(1) + hbm(1),
         scratch_shapes=[pltpu.SemaphoreType.DMA((len(chosen),))],
         compiler_params=params(),
         cost_estimate=pl.CostEstimate(flops=math.prod(shape), bytes_accessed=8 * math.prod(shape), transcendentals=0),
         name="gather",
-    )(idx, *[pieces[k] for k in chosen])
+    )(*[pieces[k] for k in chosen])
 
 
 def solve_kernel(fold, groups, cuts, chosen, idx, damping, *refs):
@@ -510,12 +532,14 @@
     d = damping[...]
     w = weight_of(d)
 
-    def forward(i, f):
-        f = w * coefficients[i] + d * f
+    def forward(i, carry):
+        f, now = carry
+        following = coefficients[jnp.minimum(i + 1, cells - 1)]
+        f = w * now + d * f
         pressure[i] = f
-        return f
-
-    lax.fori_loop(0, cells, forward, entered[0], unroll=4)
+        return f, following
+
+    lax.fori_loop(0, cells, forward, (entered[0], coefficients[0]), unroll=4)
 
     p = entered[1]
     for block in reversed(range(2 * fold)):
@@ -534,14 +558,14 @@
         copy.wait()
 
 
-def solve(fold, groups, cuts, idx, damping, ends, entry, pieces, chosen, gathered, partly):
+def solve(fold, groups, cuts, damping, ends, entry, pieces, chosen, gathered, partly):
     extra = [entry] if len(groups) > 2 else []
-    operands = [idx, damping, *ends, *extra, *[pieces[k] for k in chosen], gathered, partly]
+    operands = [damping, *ends, *extra, *[pieces[k] for k in chosen], gathered, partly]
     shape = jax.ShapeDtypeStruct(gathered.shape, F32)
     return pl.pallas_call(
-        functools.partial(solve_kernel, fold, groups, cuts, chosen),
+        at_device(solve_kernel, fold, groups, cuts, chosen),
         out_shape=[shape] * 3,
-        in_specs=smem(1) + vmem(len(operands) - 2) + hbm(1),
+        in_specs=vmem(len(operands) - 1) + hbm(1),
         out_specs=vmem(1) + hbm(2),
         scratch_shapes=[
             pltpu.VMEM(gathered.shape, F32),
@@ -560,10 +584,10 @@
     cells, planes, cols = velocity_u.shape
     fold = lax.axis_size("gy")
     sub = cells // fold
-    me, row = lax.axis_index("gy"), lax.axis_index("gx")
-    idx = jnp.stack([me, row]).astype(jnp.int32)
     order = list(range(fold - 1, 0, -1))
-    *sends, near, far, u, wall = lead(fold, idx, velocity_u, wall_strain)
+    first_send = first_cells(fold, velocity_u, wall_strain)
+    *sends, near, far = lead(fold, velocity_u, wall_strain)
+    sends.append(first_send)
     got = {(r, 0): partner(sends[r - 1], "gy", r) for r in order}
     near, far = exchange_edges(near, far)
     damp = {0: damping}
@@ -572,14 +596,14 @@
         damp |= {r ^ bit: partner(x, "gy", bit) for r, x in damp.items()}
         bit //= 2
     damp = [damp[r] for r in range(fold)]
-    second, own, *sends = stencil(fold, idx, u, wall, near, far)
+    second, own, *sends = stencil(fold, velocity_u, wall_strain, near, far)
     for r in order:
         got[r, 1] = partner(sends[r - 1], "gy", r)
-    tables = cosine_tables(fold, idx, cols)
+    tables = cosine_tables(fold, cols)
     cuts = pieces_of(fold, sub)
-    first = transform(fold, idx, sub, cuts[0], 0, [own] + [got[r, 0] for r in range(1, fold)], tables, damp)
+    first = transform(fold, sub, cuts[0], 0, [own] + [got[r, 0] for r in range(1, fold)], tables, damp)
     extra = [*damp, first[-1]]
-    rest = transform(fold, idx, sub, cuts[1], 1, [own] + [got[r, 1] for r in range(1, fold)], tables, extra)
+    rest = transform(fold, sub, cuts[1], 1, [own] + [got[r, 1] for r in range(1, fold)], tables, extra)
     ends_b = rest[-fold:]
     pieces = []
     for h, outs in enumerate((first, rest)):
@@ -592,7 +616,7 @@
     ends = [ends_b[r] if r == 0 else partner(ends_b[r], "gy", r) for r in peers(groups[0])]
     entry = None
     for stage in range(1, len(groups)):
-        mine, *entries = combined(groups, stage - 1, sub, idx, damping, ends, entry)
+        mine, *entries = combined(groups, stage - 1, sub, damping, ends, entry)
         entry = entries[0] if entries else None
         ends = [mine] + [partner(mine, "gx", o) for o in peers(groups[stage])[1:]]
     late, k = [], 0
@@ -601,8 +625,8 @@
             late += [k + n for n in range(len(cuts[h][r])) if h == 1 and r > 1]
             k += len(cuts[h][r])
     early = [n for n in range(k) if n not in late]
-    gathered, partly = gather(fold, cuts, idx, pieces, early, (cells, planes, cols))
-    coefficients, pressure = solve(fold, groups, cuts, idx, damping, ends, entry, pieces, late, gathered, partly)
+    gathered, partly = gather(fold, cuts, pieces, early, (cells, planes, cols))
+    coefficients, pressure = solve(fold, groups, cuts, damping, ends, entry, pieces, late, gathered, partly)
     return second, coefficients, pressure
 
 

time: 88.6 us -> 84.6 us (0.955)
  Pallas kernels: 22.3 us -> 16.8 us
    pallas_call x9 -> x10, Pallas kernels: 22.3 us -> 16.8 us  [the longest x2 6.33 us: transform(): pl.pallas_call(at_device(transform_kernel, fold, at, sizes, cuts, last),...]
  transfers between devices with their start and end apart: 25 -> 25, of which waited for: 10 -> 11; matrix products, arithmetic and copies ran while one was open for 0% -> 0% of each run, Pallas kernels for 15% -> 13%
where the time goes in v2:
time: 84.6 us; the launch traced here: 84.4 us
  waiting for transfers between devices  37.4 us (44%)
  starting transfers between devices  29.4 us (35%)
  Pallas kernels  16.8 us (20%)
    ppermute x24, waiting for transfers between devices, partner(): return lax.ppermute(x, axis, [(i, i ^ bit) for i in range(count)])  37.4 us
    ppermute x24, starting transfers between devices, partner(): return lax.ppermute(x, axis, [(i, i ^ bit) for i in range(count)])  28.8 us
    pallas_call x2, Pallas kernels, transform(): pl.pallas_call(at_device(transform_kernel, fold, at, sizes, cuts, last),...  6.33 us
    pallas_call x1, Pallas kernels, cosine_tables(): pl.pallas_call(at_device(table_kernel, total, cols, fold, 128), out_shape...  3.25 us
    pallas_call x1, Pallas kernels, stencil(): pl.pallas_call(at_device(stencil_kernel, fold), out_shape=outs, in_specs=...  2.18 us
    pallas_call x1, Pallas kernels, solve(): pl.pallas_call(at_device(solve_kernel, fold, groups, cuts, chosen), out_s...  1.8 us
  transfers between devices with their start and end apart: 25, of which 11 were waited for; matrix products, arithmetic and copies ran while one was open for 0% of the time, Pallas kernels for 13%

profile of v2, /device:TPU:0, one launch (start us, length us, event | category | flops | bytes accessed | tf_op | source)
XLA Modules:
  0.0 84.4 jit_solution(6994122812235015164)
XLA Ops:
  0.6 1.5 %first.1 = f32[11,16,512]{2,1,0:T(8,128)S(1)} custom-call(f32[64,16,512]{2,1,0:T(8,128)} %refs_0_.8, f32[64,16,512]{2,1,0:T(8,128)} %refs_1_.5), custom_call_target="tpu_custom_call" | custom-call | flops 901120 | bytes 1081344 | tf_op jit(solution)/shard_map/first/pallas_call | solution.py:84
  2.1 2.5 %collective-permute-start.10 = (f32[11,16,512]{2,1,0:T(8,128)S(1)}, f32[11,16,512]{2,1,0:T(8,128)S(1)}, u32[]{:S(2)}, u32[]{:S(2)}) collective-permute-start(f32[11,16,512]{2,1,0:T(8,128)S(1)} %first.1), channel_id=1, source_target_pairs={{0,3},{1,2},{2,1},{3,0},{4,7},{5,6},{6,5},{7,4},{8,11},{9,10},{10,... | collective-permute-start | bytes 1081352 | tf_op jit(solution)/shard_map/ppermute | solution.py:38
  6.6 1.1 %collective-permute-start.6 = (f32[16,512]{1,0:T(8,128)S(1)}, f32[16,512]{1,0:T(8,128)S(1)}, u32[]{:S(2)}, u32[]{:S(2)}) collective-permute-start(f32[16,512]{1,0:T(8,128)S(1)} %copy-done.2), channel_id=1, source_target_pairs={{0,2},{1,3},{2,0},{3,1},{4,6},{5,7},{6,4},{7,5},{8,10},{9,11},{10,... | collective-permute-start | bytes 98312 | tf_op jit(solution)/shard_map/ppermute | solution.py:38
  7.7 1.5 %collective-permute-start = (f32[3,16,512]{2,1,0:T(8,128)S(1)}, f32[3,16,512]{2,1,0:T(8,128)S(1)}, u32[]{:S(2)}, u32[]{:S(2)}) collective-permute-start(f32[3,16,512]{2,1,0:T(8,128)S(1)} %get-tuple-element.36), channel_id=1, source_target_pairs={{0,4},{4,0},{8,12},{12,8},{16,20},{20,16},{24,28},{28,24},{1,5},{5... | collective-permute-start | bytes 294920 | tf_op jit(solution)/shard_map/ppermute | solution.py:38
  9.2 12.8 %collective-permute-done.6.refs_10_ = f32[16,512]{1,0:T(8,128)S(1)} collective-permute-done((f32[16,512]{1,0:T(8,128)S(1)}, f32[16,512]{1,0:T(8,128)S(1)}, u32[]{:S(2)}, u32[]{:S(2)}) %collective-permute-start.6) | collective-permute-done | bytes 32800 | tf_op jit(solution)/shard_map/ppermute | solution.py:38
  23.3 3.3 %table.1 = (bf16[1024,1024]{1,0:T(8,128)(2,1)S(1)}, bf16[1024,1024]{1,0:T(8,128)(2,1)S(1)}, bf16[1024,1024]{1,0:T(8,128)(2,1)S(1)}, bf16[1024,1024]{1,0:T(8,128)(2,1)S(1)}) custom-call(), custom_call_target="tpu_custom_call" | custom-call | flops 62914560 | bytes 8388608 | tf_op jit(solution)/shard_map/table/pallas_call | solution.py:246
  26.5 2.2 %stencil.1 = (f32[64,16,512]{2,1,0:T(8,128)}, f32[16,16,512]{2,1,0:T(8,128)S(1)}, f32[5,16,512]{2,1,0:T(8,128)S(1)}, f32[5,16,512]{2,1,0:T(8,128)S(1)}, f32[5,16,512]{2,1,0:T(8,128)S(1)}) custom-call(f32[64,16,512]{2,1,0:T(8,128)S(1)} %copy-done, f32[64,16,512]{2,1,0:T(8,128)S(1)} %copy-done.1, f32[3,16,512]{2,1,0:T(8,128)S(1)} %collective-permute-done.refs_2_, ...), custom_call_target="tpu_custom_call" | custom-call | flops 10485760 | bytes 8388608 | tf_op jit(solution)/shard_map/stencil/pallas_call | solution.py:173
  28.9 2.3 %collective-permute-start.3 = (f32[5,16,512]{2,1,0:T(8,128)S(1)}, f32[5,16,512]{2,1,0:T(8,128)S(1)}, u32[]{:S(2)}, u32[]{:S(2)}) collective-permute-start(f32[5,16,512]{2,1,0:T(8,128)S(1)} %get-tuple-element.41), channel_id=1, source_target_pairs={{0,2},{1,3},{2,0},{3,1},{4,6},{5,7},{6,4},{7,5},{8,10},{9,11},{10,... | collective-permute-start | bytes 491528 | tf_op jit(solution)/shard_map/ppermute | solution.py:38
  31.3 3.9 %transform_a.1 = (f32[11,16,512]{2,1,0:T(8,128)S(1)}, f32[11,16,512]{2,1,0:T(8,128)S(1)}, f32[11,16,512]{2,1,0:T(8,128)S(1)}, f32[5,16,512]{2,1,0:T(8,128)S(1)},...) custom-call(f32[16,16,512]{2,1,0:T(8,128)S(1)} %get-tuple-element.39.refs_0_, ...), custom_call_target="tpu_custom_call" | custom-call | flops 2214592512 | bytes 8388608 | tf_op jit(solution)/shard_map/transform_a/pallas_call | solution.py:358
  36.2 3.0 %collective-permute-done.4.refs_3_ = f32[5,16,512]{2,1,0:T(8,128)S(1)} collective-permute-done((f32[5,16,512]{2,1,0:T(8,128)S(1)}, f32[5,16,512]{2,1,0:T(8,128)S(1)}, u32[]{:S(2)}, u32[]{:S(2)}) %collective-permute-start.4) | collective-permute-done | bytes 163872 | tf_op jit(solution)/shard_map/ppermute | solution.py:38
  39.2 2.5 %transform_b.1 = (f32[5,16,512]{2,1,0:T(8,128)S(1)}, f32[5,16,512]{2,1,0:T(8,128)S(1)}, f32[5,16,512]{2,1,0:T(8,128)S(1)}, f32[5,16,512]{2,1,0:T(8,128)S(1)}, f3...) custom-call(f32[16,16,512]{2,1,0:T(8,128)S(1)} %get-tuple-element.39, ...), custom_call_target="tpu_custom_call" | custom-call | flops 1006632960 | bytes 8388608 | tf_op jit(solution)/shard_map/transform_b/pallas_call | solution.py:358
  41.8 1.7 %collective-permute-start.12 = (f32[2,16,512]{2,1,0:T(8,128)S(1)}, f32[2,16,512]{2,1,0:T(8,128)S(1)}, u32[]{:S(2)}, u32[]{:S(2)}) collective-permute-start(f32[2,16,512]{2,1,0:T(8,128)S(1)} %get-tuple-element.52), channel_id=1, source_target_pairs={{0,2},{1,3},{2,0},{3,1},{4,6},{5,7},{6,4},{7,5},{8,10},{9,11},{10,... | collective-permute-start | bytes 196616 | tf_op jit(solution)/shard_map/ppermute | solution.py:38
  43.6 2.6 %collective-permute-done.12.refs_3_ = f32[2,16,512]{2,1,0:T(8,128)S(1)} collective-permute-done((f32[2,16,512]{2,1,0:T(8,128)S(1)}, f32[2,16,512]{2,1,0:T(8,128)S(1)}, u32[]{:S(2)}, u32[]{:S(2)}) %collective-permute-start.12) | collective-permute-done | bytes 65568 | tf_op jit(solution)/shard_map/ppermute | solution.py:38
  46.2 1.7 %collective-permute-done.13.refs_4_ = f32[2,16,512]{2,1,0:T(8,128)S(1)} collective-permute-done((f32[2,16,512]{2,1,0:T(8,128)S(1)}, f32[2,16,512]{2,1,0:T(8,128)S(1)}, u32[]{:S(2)}, u32[]{:S(2)}) %collective-permute-start.13) | collective-permute-done | bytes 65568 | tf_op jit(solution)/shard_map/ppermute | solution.py:38
  48.0 9.0 %collective-permute-start.16 = (f32[2,16,512]{2,1,0:T(8,128)S(1)}, f32[2,16,512]{2,1,0:T(8,128)S(1)}, u32[]{:S(2)}, u32[]{:S(2)}) collective-permute-start(f32[2,16,512]{2,1,0:T(8,128)S(1)} %shard_map.58.refs_1_), channel_id=1, source_target_pairs={{0,12},{4,8},{8,4},{12,0},{16,28},{20,24},{24,20},{28,16},{1,13},{... | collective-permute-start | bytes 196616 | tf_op jit(solution)/shard_map/ppermute | solution.py:38
  59.4 2.1 %collective-permute-start.14 = (f32[2,16,512]{2,1,0:T(8,128)S(1)}, f32[2,16,512]{2,1,0:T(8,128)S(1)}, u32[]{:S(2)}, u32[]{:S(2)}) collective-permute-start(f32[2,16,512]{2,1,0:T(8,128)S(1)} %shard_map.58.refs_1_), channel_id=1, source_target_pairs={{0,4},{4,0},{8,12},{12,8},{16,20},{20,16},{24,28},{28,24},{1,5},{5... | collective-permute-start | bytes 196616 | tf_op jit(solution)/shard_map/ppermute | solution.py:38
  61.5 2.2 %collective-permute-done.14.refs_2_ = f32[2,16,512]{2,1,0:T(8,128)S(1)} collective-permute-done((f32[2,16,512]{2,1,0:T(8,128)S(1)}, f32[2,16,512]{2,1,0:T(8,128)S(1)}, u32[]{:S(2)}, u32[]{:S(2)}) %collective-permute-start.14) | collective-permute-done | bytes 65568 | tf_op jit(solution)/shard_map/ppermute | solution.py:38
  64.6 6.7 %collective-permute-done.22.refs_3_ = f32[5,16,512]{2,1,0:T(8,128)S(1)} collective-permute-done((f32[5,16,512]{2,1,0:T(8,128)S(1)}, f32[5,16,512]{2,1,0:T(8,128)S(1)}, u32[]{:S(2)}, u32[]{:S(2)}) %collective-permute-start.22) | collective-permute-done | bytes 163872 | tf_op jit(solution)/shard_map/ppermute | solution.py:38
  71.3 1.2 %collective-permute-start.19 = (f32[5,16,512]{2,1,0:T(8,128)S(1)}, f32[5,16,512]{2,1,0:T(8,128)S(1)}, u32[]{:S(2)}, u32[]{:S(2)}) collective-permute-start(f32[5,16,512]{2,1,0:T(8,128)S(1)} %get-tuple-element.57), channel_id=1, source_target_pairs={{0,3},{1,2},{2,1},{3,0},{4,7},{5,6},{6,5},{7,4},{8,11},{9,10},{10,... | collective-permute-start | bytes 491528 | tf_op jit(solution)/shard_map/ppermute | solution.py:38
  72.6 3.0 %collective-permute-done.23.refs_4_ = f32[6,16,512]{2,1,0:T(8,128)S(1)} collective-permute-done((f32[6,16,512]{2,1,0:T(8,128)S(1)}, f32[6,16,512]{2,1,0:T(8,128)S(1)}, u32[]{:S(2)}, u32[]{:S(2)}) %collective-permute-start.23) | collective-permute-done | bytes 196640 | tf_op jit(solution)/shard_map/ppermute | solution.py:38
  75.5 2.6 %collective-permute-start.17 = (f32[2,16,512]{2,1,0:T(8,128)S(1)}, f32[2,16,512]{2,1,0:T(8,128)S(1)}, u32[]{:S(2)}, u32[]{:S(2)}) collective-permute-start(f32[2,16,512]{2,1,0:T(8,128)S(1)} %get-tuple-element.54.refs_1_), channel_id=1, source_target_pairs={{0,16},{4,20},{8,24},{12,28},{16,0},{20,4},{24,8},{28,12},{1,17},{... | collective-permute-start | bytes 196616 | tf_op jit(solution)/shard_map/ppermute | solution.py:38
  78.1 1.3 %gather.1 = (f32[64,16,512]{2,1,0:T(8,128)S(1)}, f32[64,16,512]{2,1,0:T(8,128)}) custom-call(f32[11,16,512]{2,1,0:T(8,128)S(1)} %get-tuple-element.58.refs_0_, f32[11,16,512]{2,1,0:T(8,128)S(1)} %collective-permute-done.20.refs_1_, f32[11,16,512]{2,1,0:T(8,128)S(1)} %collective-permute-done.21.refs_2_, f32[5,16,512]{2,1,0:T(8,128)S(1)} %collective-permute-done.22.refs_3_, ...), custom_call_target="tpu_custom_call" | custom-call | flops 524288 | bytes 4194304 | tf_op jit(solution)/shard_map/gather/pallas_call | solution.py:495
  80.0 2.6 %collective-permute-done.19.refs_5_ = f32[5,16,512]{2,1,0:T(8,128)S(1)} collective-permute-done((f32[5,16,512]{2,1,0:T(8,128)S(1)}, f32[5,16,512]{2,1,0:T(8,128)S(1)}, u32[]{:S(2)}, u32[]{:S(2)}) %collective-permute-start.19) | collective-permute-done | bytes 163872 | tf_op jit(solution)/shard_map/ppermute | solution.py:38
  82.6 1.8 %solve.1 = (f32[64,16,512]{2,1,0:T(8,128)S(1)}, f32[64,16,512]{2,1,0:T(8,128)}, f32[64,16,512]{2,1,0:T(8,128)}) custom-call(f32[16,512]{1,0:T(8,128)S(1)} %copy-done.2, f32[2,16,512]{2,1,0:T(8,128)S(1)} %get-tuple-element.54.refs_1_, f32[2,16,512]{2,1,0:T(8,128)S(1)} %collective-permute-done.17.refs_2_, ...), custom_call_target="tpu_custom_call", output_to_operand_aliasing={{0}: (6, {}), {1}: (7, {})} | custom-call | flops 2621440 | bytes 6291456 | tf_op jit(solution)/shard_map/solve/pallas_call | solution.py:565
  (42 shorter events, 8.7 us)
Async XLA Ops:
  2.1 29.1 %collective-permute-start.10 = (f32[11,16,512]{2,1,0:T(8,128)S(1)}, f32[11,16,512]{2,1,0:T(8,128)S(1)}, u32[]{:S(2)}, u32[]{:S(2)}) collective-permute-start(f32[11,16,512]{2,1,0:T(8,128)S(1)} %first.1), channel_id=1, source_target_pairs={{0,3},{1,2},{2,1},{3,0},{4,7},{5,6},{6,5},{7,4},{8,11},{9,10},{10,... | collective-permute-start | bytes 1081352 | tf_op jit(solution)/shard_map/ppermute | solution.py:38
  4.9 26.4 %collective-permute-start.8 = (f32[11,16,512]{2,1,0:T(8,128)S(1)}, f32[11,16,512]{2,1,0:T(8,128)S(1)}, u32[]{:S(2)}, u32[]{:S(2)}) collective-permute-start(f32[11,16,512]{2,1,0:T(8,128)S(1)} %get-tuple-element.47), channel_id=1, source_target_pairs={{0,1},{1,0},{2,3},{3,2},{4,5},{5,4},{6,7},{7,6},{8,9},{9,8},{10,11... | collective-permute-start | bytes 1081352 | tf_op jit(solution)/shard_map/ppermute | solution.py:38
  5.7 25.6 %collective-permute-start.9 = (f32[11,16,512]{2,1,0:T(8,128)S(1)}, f32[11,16,512]{2,1,0:T(8,128)S(1)}, u32[]{:S(2)}, u32[]{:S(2)}) collective-permute-start(f32[11,16,512]{2,1,0:T(8,128)S(1)} %get-tuple-element.48), channel_id=1, source_target_pairs={{0,2},{1,3},{2,0},{3,1},{4,6},{5,7},{6,4},{7,5},{8,10},{9,11},{10,... | collective-permute-start | bytes 1081352 | tf_op jit(solution)/shard_map/ppermute | solution.py:38
  6.6 15.5 %collective-permute-start.6 = (f32[16,512]{1,0:T(8,128)S(1)}, f32[16,512]{1,0:T(8,128)S(1)}, u32[]{:S(2)}, u32[]{:S(2)}) collective-permute-start(f32[16,512]{1,0:T(8,128)S(1)} %copy-done.2), channel_id=1, source_target_pairs={{0,2},{1,3},{2,0},{3,1},{4,6},{5,7},{6,4},{7,5},{8,10},{9,11},{10,... | collective-permute-start | bytes 98312 | tf_op jit(solution)/shard_map/ppermute | solution.py:38
  7.7 15.0 %collective-permute-start = (f32[3,16,512]{2,1,0:T(8,128)S(1)}, f32[3,16,512]{2,1,0:T(8,128)S(1)}, u32[]{:S(2)}, u32[]{:S(2)}) collective-permute-start(f32[3,16,512]{2,1,0:T(8,128)S(1)} %get-tuple-element.36), channel_id=1, source_target_pairs={{0,4},{4,0},{8,12},{12,8},{16,20},{20,16},{24,28},{28,24},{1,5},{5... | collective-permute-start | bytes 294920 | tf_op jit(solution)/shard_map/ppermute | solution.py:38
  22.7 6.0 %collective-permute-start.5 = (f32[16,512]{1,0:T(8,128)S(1)}, f32[16,512]{1,0:T(8,128)S(1)}, u32[]{:S(2)}, u32[]{:S(2)}) collective-permute-start(f32[16,512]{1,0:T(8,128)S(1)} %copy-done.2), channel_id=1, source_target_pairs={{0,1},{1,0},{2,3},{3,2},{4,5},{5,4},{6,7},{7,6},{8,9},{9,8},{10,11... | collective-permute-start | bytes 98312 | tf_op jit(solution)/shard_map/ppermute | solution.py:38
  22.8 6.1 %collective-permute-start.7 = (f32[16,512]{1,0:T(8,128)S(1)}, f32[16,512]{1,0:T(8,128)S(1)}, u32[]{:S(2)}, u32[]{:S(2)}) collective-permute-start(f32[16,512]{1,0:T(8,128)S(1)} %collective-permute-done.6.refs_10_), channel_id=1, source_target_pairs={{0,1},{1,0},{2,3},{3,2},{4,5},{5,4},{6,7},{7,6},{8,9},{9,8},{10,11... | collective-permute-start | bytes 98312 | tf_op jit(solution)/shard_map/ppermute | solution.py:38
  28.7 6.4 %collective-permute-start.2 = (f32[5,16,512]{2,1,0:T(8,128)S(1)}, f32[5,16,512]{2,1,0:T(8,128)S(1)}, u32[]{:S(2)}, u32[]{:S(2)}) collective-permute-start(f32[5,16,512]{2,1,0:T(8,128)S(1)} %get-tuple-element.40), channel_id=1, source_target_pairs={{0,1},{1,0},{2,3},{3,2},{4,5},{5,4},{6,7},{7,6},{8,9},{9,8},{10,11... | collective-permute-start | bytes 491528 | tf_op jit(solution)/shard_map/ppermute | solution.py:38
  28.9 7.4 %collective-permute-start.3 = (f32[5,16,512]{2,1,0:T(8,128)S(1)}, f32[5,16,512]{2,1,0:T(8,128)S(1)}, u32[]{:S(2)}, u32[]{:S(2)}) collective-permute-start(f32[5,16,512]{2,1,0:T(8,128)S(1)} %get-tuple-element.41), channel_id=1, source_target_pairs={{0,2},{1,3},{2,0},{3,1},{4,6},{5,7},{6,4},{7,5},{8,10},{9,11},{10,... | collective-permute-start | bytes 491528 | tf_op jit(solution)/shard_map/ppermute | solution.py:38
  31.2 8.0 %collective-permute-start.4 = (f32[5,16,512]{2,1,0:T(8,128)S(1)}, f32[5,16,512]{2,1,0:T(8,128)S(1)}, u32[]{:S(2)}, u32[]{:S(2)}) collective-permute-start(f32[5,16,512]{2,1,0:T(8,128)S(1)} %get-tuple-element.42), channel_id=1, source_target_pairs={{0,3},{1,2},{2,1},{3,0},{4,7},{5,6},{6,5},{7,4},{8,11},{9,10},{10,... | collective-permute-start | bytes 491528 | tf_op jit(solution)/shard_map/ppermute | solution.py:38
  41.7 1.9 %collective-permute-start.11 = (f32[2,16,512]{2,1,0:T(8,128)S(1)}, f32[2,16,512]{2,1,0:T(8,128)S(1)}, u32[]{:S(2)}, u32[]{:S(2)}) collective-permute-start(f32[2,16,512]{2,1,0:T(8,128)S(1)} %get-tuple-element.51), channel_id=1, source_target_pairs={{0,1},{1,0},{2,3},{3,2},{4,5},{5,4},{6,7},{7,6},{8,9},{9,8},{10,11... | collective-permute-start | bytes 196616 | tf_op jit(solution)/shard_map/ppermute | solution.py:38
  41.8 4.4 %collective-permute-start.12 = (f32[2,16,512]{2,1,0:T(8,128)S(1)}, f32[2,16,512]{2,1,0:T(8,128)S(1)}, u32[]{:S(2)}, u32[]{:S(2)}) collective-permute-start(f32[2,16,512]{2,1,0:T(8,128)S(1)} %get-tuple-element.52), channel_id=1, source_target_pairs={{0,2},{1,3},{2,0},{3,1},{4,6},{5,7},{6,4},{7,5},{8,10},{9,11},{10,... | collective-permute-start | bytes 196616 | tf_op jit(solution)/shard_map/ppermute | solution.py:38
  43.6 4.4 %collective-permute-start.13 = (f32[2,16,512]{2,1,0:T(8,128)S(1)}, f32[2,16,512]{2,1,0:T(8,128)S(1)}, u32[]{:S(2)}, u32[]{:S(2)}) collective-permute-start(f32[2,16,512]{2,1,0:T(8,128)S(1)} %get-tuple-element.53), channel_id=1, source_target_pairs={{0,3},{1,2},{2,1},{3,0},{4,7},{5,6},{6,5},{7,4},{8,11},{9,10},{10,... | collective-permute-start | bytes 196616 | tf_op jit(solution)/shard_map/ppermute | solution.py:38
  48.0 11.4 %collective-permute-start.16 = (f32[2,16,512]{2,1,0:T(8,128)S(1)}, f32[2,16,512]{2,1,0:T(8,128)S(1)}, u32[]{:S(2)}, u32[]{:S(2)}) collective-permute-start(f32[2,16,512]{2,1,0:T(8,128)S(1)} %shard_map.58.refs_1_), channel_id=1, source_target_pairs={{0,12},{4,8},{8,4},{12,0},{16,28},{20,24},{24,20},{28,16},{1,13},{... | collective-permute-start | bytes 196616 | tf_op jit(solution)/shard_map/ppermute | solution.py:38
  57.0 4.4 %collective-permute-start.15 = (f32[2,16,512]{2,1,0:T(8,128)S(1)}, f32[2,16,512]{2,1,0:T(8,128)S(1)}, u32[]{:S(2)}, u32[]{:S(2)}) collective-permute-start(f32[2,16,512]{2,1,0:T(8,128)S(1)} %shard_map.58.refs_1_), channel_id=1, source_target_pairs={{0,8},{4,12},{8,0},{12,4},{16,24},{20,28},{24,16},{28,20},{1,9},{5... | collective-permute-start | bytes 196616 | tf_op jit(solution)/shard_map/ppermute | solution.py:38
  57.5 20.7 %collective-permute-start.20 = (f32[11,16,512]{2,1,0:T(8,128)S(1)}, f32[11,16,512]{2,1,0:T(8,128)S(1)}, u32[]{:S(2)}, u32[]{:S(2)}) collective-permute-start(f32[11,16,512]{2,1,0:T(8,128)S(1)} %get-tuple-element.59), channel_id=1, source_target_pairs={{0,1},{1,0},{2,3},{3,2},{4,5},{5,4},{6,7},{7,6},{8,9},{9,8},{10,11... | collective-permute-start | bytes 1081352 | tf_op jit(solution)/shard_map/ppermute | solution.py:38
  57.5 20.7 %collective-permute-start.21 = (f32[11,16,512]{2,1,0:T(8,128)S(1)}, f32[11,16,512]{2,1,0:T(8,128)S(1)}, u32[]{:S(2)}, u32[]{:S(2)}) collective-permute-start(f32[11,16,512]{2,1,0:T(8,128)S(1)} %get-tuple-element.60), channel_id=1, source_target_pairs={{0,2},{1,3},{2,0},{3,1},{4,6},{5,7},{6,4},{7,5},{8,10},{9,11},{10,... | collective-permute-start | bytes 1081352 | tf_op jit(solution)/shard_map/ppermute | solution.py:38
  58.0 5.7 %collective-permute-start.24 = (f32[5,16,512]{2,1,0:T(8,128)S(1)}, f32[5,16,512]{2,1,0:T(8,128)S(1)}, u32[]{:S(2)}, u32[]{:S(2)}) collective-permute-start(f32[5,16,512]{2,1,0:T(8,128)S(1)} %get-tuple-element.64), channel_id=1, source_target_pairs={{0,1},{1,0},{2,3},{3,2},{4,5},{5,4},{6,7},{7,6},{8,9},{9,8},{10,11... | collective-permute-start | bytes 491528 | tf_op jit(solution)/shard_map/ppermute | solution.py:38
  59.4 4.3 %collective-permute-start.14 = (f32[2,16,512]{2,1,0:T(8,128)S(1)}, f32[2,16,512]{2,1,0:T(8,128)S(1)}, u32[]{:S(2)}, u32[]{:S(2)}) collective-permute-start(f32[2,16,512]{2,1,0:T(8,128)S(1)} %shard_map.58.refs_1_), channel_id=1, source_target_pairs={{0,4},{4,0},{8,12},{12,8},{16,20},{20,16},{24,28},{28,24},{1,5},{5... | collective-permute-start | bytes 196616 | tf_op jit(solution)/shard_map/ppermute | solution.py:38
  61.4 9.9 %collective-permute-start.22 = (f32[5,16,512]{2,1,0:T(8,128)S(1)}, f32[5,16,512]{2,1,0:T(8,128)S(1)}, u32[]{:S(2)}, u32[]{:S(2)}) collective-permute-start(f32[5,16,512]{2,1,0:T(8,128)S(1)} %get-tuple-element.61), channel_id=1, source_target_pairs={{0,3},{1,2},{2,1},{3,0},{4,7},{5,6},{6,5},{7,4},{8,11},{9,10},{10,... | collective-permute-start | bytes 491528 | tf_op jit(solution)/shard_map/ppermute | solution.py:38
  63.7 11.9 %collective-permute-start.23 = (f32[6,16,512]{2,1,0:T(8,128)S(1)}, f32[6,16,512]{2,1,0:T(8,128)S(1)}, u32[]{:S(2)}, u32[]{:S(2)}) collective-permute-start(f32[6,16,512]{2,1,0:T(8,128)S(1)} %get-tuple-element.62), channel_id=1, source_target_pairs={{0,3},{1,2},{2,1},{3,0},{4,7},{5,6},{6,5},{7,4},{8,11},{9,10},{10,... | collective-permute-start | bytes 589832 | tf_op jit(solution)/shard_map/ppermute | solution.py:38
  63.7 16.3 %collective-permute-start.18 = (f32[5,16,512]{2,1,0:T(8,128)S(1)}, f32[5,16,512]{2,1,0:T(8,128)S(1)}, u32[]{:S(2)}, u32[]{:S(2)}) collective-permute-start(f32[5,16,512]{2,1,0:T(8,128)S(1)} %get-tuple-element.56), channel_id=1, source_target_pairs={{0,2},{1,3},{2,0},{3,1},{4,6},{5,7},{6,4},{7,5},{8,10},{9,11},{10,... | collective-permute-start | bytes 491528 | tf_op jit(solution)/shard_map/ppermute | solution.py:38
  71.3 11.2 %collective-permute-start.19 = (f32[5,16,512]{2,1,0:T(8,128)S(1)}, f32[5,16,512]{2,1,0:T(8,128)S(1)}, u32[]{:S(2)}, u32[]{:S(2)}) collective-permute-start(f32[5,16,512]{2,1,0:T(8,128)S(1)} %get-tuple-element.57), channel_id=1, source_target_pairs={{0,3},{1,2},{2,1},{3,0},{4,7},{5,6},{6,5},{7,4},{8,11},{9,10},{10,... | collective-permute-start | bytes 491528 | tf_op jit(solution)/shard_map/ppermute | solution.py:38
  75.5 7.0 %collective-permute-start.17 = (f32[2,16,512]{2,1,0:T(8,128)S(1)}, f32[2,16,512]{2,1,0:T(8,128)S(1)}, u32[]{:S(2)}, u32[]{:S(2)}) collective-permute-start(f32[2,16,512]{2,1,0:T(8,128)S(1)} %get-tuple-element.54.refs_1_), channel_id=1, source_target_pairs={{0,16},{4,20},{8,24},{12,28},{16,0},{20,4},{24,8},{28,12},{1,17},{... | collective-permute-start | bytes 196616 | tf_op jit(solution)/shard_map/ppermute | solution.py:38
  (4 other events, 13.1 us)

commit v3 on v2

--- a/solution.py
+++ b/solution.py
@@ -271,7 +271,7 @@
         earlier = next(take)
     outs = [[next(take) for _ in pieces] for pieces in cuts]
     if last:
-        ends = [next(take) for _ in range(fold)]
+        ends = [next(take) for _ in range(2)]
     else:
         ends_all = next(take)
     parts = [next(take) for _ in range(2)]
@@ -335,8 +335,8 @@
             if last:
                 f0, p0 = earlier[0, r, :, at_lanes], earlier[1, r, :, at_lanes]
                 f, p = merge((f, p), (f0, p0), idx[0] != 0, span(d, half), span(d, sizes[0]))
-                ends[r][0, :, at_lanes] = f
-                ends[r][1, :, at_lanes] = p
+                ends[r % 2][r // 2, 0, :, at_lanes] = f
+                ends[r % 2][r // 2, 1, :, at_lanes] = p
             else:
                 ends_all[0, r, :, at_lanes] = f
                 ends_all[1, r, :, at_lanes] = p
@@ -351,7 +351,7 @@
     shape = lambda *n: jax.ShapeDtypeStruct(n, F32)
     outs = [shape(high - low, planes, cols) for pieces in cuts for low, high in pieces]
     if last:
-        outs += [shape(2, planes, cols)] * fold
+        outs += [shape(fold // 2, 2, planes, cols)] * 2
     else:
         outs += [shape(2, fold, planes, cols)]
     rows = half * planes
@@ -393,10 +393,9 @@
     return power * power, gain * (1.0 + power * power)
 
 
-def stages(fold, count):
+def stages(count):
     bits = [1 << k for k in range(count.bit_length() - 1)]
-    groups = [[1 << k for k in range(fold.bit_length() - 1)]]
-    return groups + [bits[k : k + 2] for k in range(0, len(bits), 2)]
+    return [bits[k : k + 2] for k in range(0, len(bits), 2)]
 
 
 def peers(bits):
@@ -406,67 +405,96 @@
     return offsets
 
 
-def combine(groups, stage, d, sub, me, row, ends, entry):
-    power, gain = span(d, sub)
-    start, stop, turn = None, None, None
+def combine(groups, stage, d, block, row, ends, entry):
+    power, gain = span(d, block)
+    start, stop, turn = jnp.ones_like(d), jnp.ones_like(d), jnp.zeros_like(d)
+    if entry is None:
+        entry = (jnp.zeros_like(d), jnp.zeros_like(d))
     for k, bits in enumerate(groups[: stage + 1]):
-        position = row if k else me
-        if k == 1:
-            start, stop, turn = jnp.ones_like(d), jnp.ones_like(d), jnp.zeros_like(d)
-            if entry is None:
-                entry = (jnp.zeros_like(d), jnp.zeros_like(d))
         for bit in bits:
-            upper = position & bit != 0
-            if k:
-                if k == stage:
-                    mine, other = ends[0], ends[1]
-                    below, above = entry
-                    below = below + jnp.where(upper, start * other[0], 0.0)
-                    above = above + jnp.where(upper, turn * other[0], stop * (other[1] + gain * mine[0]))
-                    entry = (below, above)
-                turn = jnp.where(upper, power * turn, turn + stop * gain * power)
-                start = jnp.where(upper, power * start, start)
-                stop = jnp.where(upper, stop, power * stop)
+            upper = row & bit != 0
             if k == stage:
+                mine, other = ends[0], ends[1]
+                below, above = entry
+                below = below + jnp.where(upper, start * other[0], 0.0)
+                above = above + jnp.where(upper, turn * other[0], stop * (other[1] + gain * mine[0]))
+                entry = (below, above)
                 ends = [merge(ends[i], ends[i + 1], upper, (power, gain), (power, gain)) for i in range(0, len(ends), 2)]
+            turn = jnp.where(upper, power * turn, turn + stop * gain * power)
+            start = jnp.where(upper, power * start, start)
+            stop = jnp.where(upper, stop, power * stop)
             power, gain = doubled(power, gain)
     return ends[0], entry
 
 
-def combine_tiles(groups, stage, sub, idx, damping, ends, entry, put):
+def combine_tiles(groups, stage, block, idx, damping, ends, entry, put):
     for t in range(damping.shape[1] // LANES):
         at = pl.ds(t * LANES, LANES)
         pairs = [(e[0, :, at], e[1, :, at]) for e in ends]
         entered = None if entry is None else (entry[0, :, at], entry[1, :, at])
-        put(at, *combine(groups, stage, damping[:, at], sub, idx[0], idx[1], pairs, entered))
-
-
-def combine_kernel(groups, stage, sub, idx, damping, *refs):
+        put(at, *combine(groups, stage, damping[:, at], block, idx[1], pairs, entered))
+
+
+def combine_kernel(groups, stage, block, idx, damping, *refs):
     count = 1 << len(groups[stage])
     ends, rest = refs[:count], refs[count:]
-    entry = rest[0] if stage > 1 else None
-    outs = rest[-2:] if stage else rest[-1:]
+    entry = rest[0] if stage else None
+    outs = rest[-2:]
 
     def put(at, union, entered):
         outs[0][0, :, at], outs[0][1, :, at] = union
-        if stage:
-            outs[1][0, :, at], outs[1][1, :, at] = entered
-
-    combine_tiles(groups, stage, sub, idx, damping, ends, entry, put)
-
-
-def combined(groups, stage, sub, damping, ends, entry):
+        outs[1][0, :, at], outs[1][1, :, at] = entered
+
+    combine_tiles(groups, stage, block, idx, damping, ends, entry, put)
+
+
+def combined(groups, stage, block, damping, ends, entry):
     pair = jax.ShapeDtypeStruct((2,) + damping.shape, F32)
-    extra = [entry] if stage > 1 else []
-    outs = [pair, pair] if stage else [pair]
-    return pl.pallas_call(
-        at_device(combine_kernel, groups, stage, sub),
-        out_shape=outs,
+    extra = [entry] if stage else []
+    return pl.pallas_call(
+        at_device(combine_kernel, groups, stage, block),
+        out_shape=[pair, pair],
         in_specs=vmem(1 + len(ends) + len(extra)),
-        out_specs=vmem(len(outs)),
+        out_specs=vmem(2),
         compiler_params=params(),
         cost_estimate=pl.CostEstimate(flops=100 * damping.size, bytes_accessed=32 * damping.size, transcendentals=0),
     )(damping, *ends, *extra)
+
+
+def pairs_kernel(bit, sub, idx, keep, got, *refs):
+    count = keep.shape[0]
+    damp, outs = refs[:count], refs[count:]
+    for i in range(count):
+        for t in range(damp[i].shape[1] // LANES):
+            at = pl.ds(t * LANES, LANES)
+            both = span(damp[i][:, at], sub * bit)
+            mine, other = ((e[i, 0, :, at], e[i, 1, :, at]) for e in (keep, got))
+            out = outs[i % 2] if count > 1 else outs[0]
+            place = (i // 2,) if count > 1 else ()
+            f, p = merge(mine, other, idx[0] & bit != 0, both, both)
+            out[(*place, 0, slice(None), at)] = f
+            out[(*place, 1, slice(None), at)] = p
+
+
+def block_ends(fold, sub, damp, keep, send):
+    bit = 1
+    while bit < fold:
+        got = partner(send, "gy", bit)
+        kept = [damp[r] for r in range(0, fold, 2 * bit)]
+        count = len(kept)
+        shape = keep.shape[1:] if count == 1 else (count // 2,) + keep.shape[1:]
+        outs = [jax.ShapeDtypeStruct(shape, F32)] * (1 if count == 1 else 2)
+        keep, *rest = pl.pallas_call(
+            at_device(pairs_kernel, bit, sub),
+            out_shape=outs,
+            in_specs=vmem(2 + count),
+            out_specs=vmem(len(outs)),
+            compiler_params=params(),
+            cost_estimate=pl.CostEstimate(flops=50 * keep.size, bytes_accessed=16 * keep.size, transcendentals=0),
+        )(keep, got, *kept)
+        send = rest[0] if rest else None
+        bit *= 2
+    return keep
 
 
 def place(fold, cuts, me, sub):
@@ -508,7 +536,7 @@
     stage = len(groups) - 1
     count = 1 << len(groups[stage])
     ends, rest = refs[:count], refs[count:]
-    if stage > 1:
+    if stage:
         entry, rest = rest[0], rest[1:]
     else:
         entry = None
@@ -516,7 +544,6 @@
     _, _, coefficients, coefficients_out, pressure_out, pressure, entered, c_sems, p_sems = rest
     cells = coefficients.shape[0]
     sub = cells // fold
-    half = sub // 2
     places = place(fold, cuts, idx[0], sub)
     copies = []
     for n, k in enumerate(chosen):
@@ -528,38 +555,42 @@
     def put(at, union, entry):
         entered[0, :, at], entered[1, :, at] = entry
 
-    combine_tiles(groups, stage, sub, idx, damping, ends, entry, put)
-    d = damping[...]
-    w = weight_of(d)
-
-    def forward(i, carry):
-        f, now = carry
-        following = coefficients[jnp.minimum(i + 1, cells - 1)]
-        f = w * now + d * f
-        pressure[i] = f
-        return f, following
-
-    lax.fori_loop(0, cells, forward, (entered[0], coefficients[0]), unroll=4)
-
-    p = entered[1]
-    for block in reversed(range(2 * fold)):
-
-        def backward(i, p, block=block):
-            at = (block + 1) * half - 1 - i
-            p = pressure[at] + d * p
-            pressure[at] = p
-            return p
-
-        p = lax.fori_loop(0, half, backward, p, unroll=4)
-        rows = pl.ds(block * half, half)
-        copies.append(pltpu.make_async_copy(pressure.at[rows], pressure_out.at[rows], p_sems.at[block]))
-        copies[-1].start()
+    combine_tiles(groups, stage, cells, idx, damping, ends, entry, put)
+    width = max(coefficients.shape[2] // 2, LANES)
+    for low in range(0, coefficients.shape[2], width):
+        lanes = pl.ds(low, width)
+        d = damping[:, lanes]
+        w = weight_of(d)
+
+        def forward(i, carry, w=w, d=d, lanes=lanes):
+            f, now = carry
+            following = coefficients[jnp.minimum(i + 1, cells - 1), :, lanes]
+            f = w * now + d * f
+            pressure[i, :, lanes] = f
+            return f, following
+
+        lax.fori_loop(0, cells, forward, (entered[0, :, lanes], coefficients[0, :, lanes]), unroll=8)
+
+        p = entered[1, :, lanes]
+        for block in reversed(range(fold)):
+
+            def backward(i, p, d=d, lanes=lanes, block=block):
+                at = (block + 1) * sub - 1 - i
+                p = pressure[at, :, lanes] + d * p
+                pressure[at, :, lanes] = p
+                return p
+
+            p = lax.fori_loop(0, sub, backward, p, unroll=8)
+            part = (pl.ds(block * sub, sub), slice(None), lanes)
+            k = len(copies) - len(chosen)
+            copies.append(pltpu.make_async_copy(pressure.at[part], pressure_out.at[part], p_sems.at[k]))
+            copies[-1].start()
     for copy in copies:
         copy.wait()
 
 
 def solve(fold, groups, cuts, damping, ends, entry, pieces, chosen, gathered, partly):
-    extra = [entry] if len(groups) > 2 else []
+    extra = [entry] if len(groups) > 1 else []
     operands = [damping, *ends, *extra, *[pieces[k] for k in chosen], gathered, partly]
     shape = jax.ShapeDtypeStruct(gathered.shape, F32)
     return pl.pallas_call(
@@ -604,7 +635,6 @@
     first = transform(fold, sub, cuts[0], 0, [own] + [got[r, 0] for r in range(1, fold)], tables, damp)
     extra = [*damp, first[-1]]
     rest = transform(fold, sub, cuts[1], 1, [own] + [got[r, 1] for r in range(1, fold)], tables, extra)
-    ends_b = rest[-fold:]
     pieces = []
     for h, outs in enumerate((first, rest)):
         outs = iter(outs)
@@ -612,13 +642,12 @@
             for k in range(len(cuts[h][r])):
                 out = next(outs)
                 pieces.append(out if r == 0 else partner(out, "gy", r))
-    groups = stages(fold, lax.axis_size("gx"))
-    ends = [ends_b[r] if r == 0 else partner(ends_b[r], "gy", r) for r in peers(groups[0])]
-    entry = None
-    for stage in range(1, len(groups)):
-        mine, *entries = combined(groups, stage - 1, sub, damping, ends, entry)
-        entry = entries[0] if entries else None
-        ends = [mine] + [partner(mine, "gx", o) for o in peers(groups[stage])[1:]]
+    groups = stages(lax.axis_size("gx"))
+    mine, entry = block_ends(fold, sub, damp, *rest[-2:]), None
+    for stage, bits in enumerate(groups):
+        if stage:
+            mine, entry = combined(groups, stage - 1, cells, damping, ends, entry)
+        ends = [mine] + [partner(mine, "gx", o) for o in peers(bits)[1:]]
     late, k = [], 0
     for h in range(2):
         for r in range(fold):
@@ -631,11 +660,7 @@
 
 
 def pieces_of(fold, sub):
-    first, later = chunks(sub)
-    cut = first // 2
-    whole = [[(0, first)] for _ in range(fold)]
-    whole[fold - 1] = [(0, cut), (cut, first)]
-    return whole, [[(0, later)] for _ in range(fold)]
+    return [[[(0, size)] for _ in range(fold)] for size in chunks(sub)]
 
 
 def solution(mesh):

time: 84.6 us -> 79.8 us (0.943)
  waiting for transfers between devices: 37.4 us -> 31.1 us
  starting transfers between devices: 29.4 us -> 30.4 us
    ppermute x24 -> x22, waiting for transfers between devices: 37.4 us -> 31.1 us  [partner(): return lax.ppermute(x, axis, [(i, i ^ bit) for i in range(count)])]
    ppermute x24 -> x22, starting transfers between devices: 28.8 us -> 29.7 us  [partner(): return lax.ppermute(x, axis, [(i, i ^ bit) for i in range(count)])]
  transfers between devices with their start and end apart: 25 -> 23, of which waited for: 11 -> 8; matrix products, arithmetic and copies ran while one was open for 0% -> 0% of each run, Pallas kernels for 13% -> 14%
where the time goes in v3:
time: 79.8 us; the launch traced here: 79.1 us
  waiting for transfers between devices  31.1 us (39%)
  starting transfers between devices  30.4 us (38%)
  Pallas kernels  16.8 us (21%)
  between operations  0.8 us (1%)
    ppermute x22, waiting for transfers between devices, partner(): return lax.ppermute(x, axis, [(i, i ^ bit) for i in range(count)])  31.1 us
    ppermute x22, starting transfers between devices, partner(): return lax.ppermute(x, axis, [(i, i ^ bit) for i in range(count)])  29.7 us
    pallas_call x2, Pallas kernels, transform(): pl.pallas_call(at_device(transform_kernel, fold, at, sizes, cuts, last),...  6.33 us
    pallas_call x1, Pallas kernels, cosine_tables(): pl.pallas_call(at_device(table_kernel, total, cols, fold, 128), out_shape...  3.25 us
    pallas_call x1, Pallas kernels, stencil(): pl.pallas_call(at_device(stencil_kernel, fold), out_shape=outs, in_specs=...  2.18 us
    pallas_call x1, Pallas kernels, solve(): pl.pallas_call(at_device(solve_kernel, fold, groups, cuts, chosen), out_s...  1.77 us
  transfers between devices with their start and end apart: 23, of which 8 were waited for; matrix products, arithmetic and copies ran while one was open for 0% of the time, Pallas kernels for 14%

profile of v3, /device:TPU:0, one launch (start us, length us, event | category | flops | bytes accessed | tf_op | source)
XLA Modules:
  0.0 79.1 jit_solution(5676899449292988732)
XLA Ops:
  0.6 1.5 %first.1 = f32[11,16,512]{2,1,0:T(8,128)S(1)} custom-call(f32[64,16,512]{2,1,0:T(8,128)} %refs_0_.7, f32[64,16,512]{2,1,0:T(8,128)} %refs_1_.5), custom_call_target="tpu_custom_call" | custom-call | flops 901120 | bytes 1081344 | tf_op jit(solution)/shard_map/first/pallas_call | solution.py:84
  2.1 2.5 %collective-permute-start.10 = (f32[11,16,512]{2,1,0:T(8,128)S(1)}, f32[11,16,512]{2,1,0:T(8,128)S(1)}, u32[]{:S(2)}, u32[]{:S(2)}) collective-permute-start(f32[11,16,512]{2,1,0:T(8,128)S(1)} %first.1), channel_id=1, source_target_pairs={{0,3},{1,2},{2,1},{3,0},{4,7},{5,6},{6,5},{7,4},{8,11},{9,10},{10,... | collective-permute-start | bytes 1081352 | tf_op jit(solution)/shard_map/ppermute | solution.py:38
  4.9 0.7 collective-permute-start.8
  5.7 0.9 %collective-permute-start.9 = (f32[11,16,512]{2,1,0:T(8,128)S(1)}, f32[11,16,512]{2,1,0:T(8,128)S(1)}, u32[]{:S(2)}, u32[]{:S(2)}) collective-permute-start(f32[11,16,512]{2,1,0:T(8,128)S(1)} %get-tuple-element.47), channel_id=1, source_target_pairs={{0,2},{1,3},{2,0},{3,1},{4,6},{5,7},{6,4},{7,5},{8,10},{9,11},{10,... | collective-permute-start | bytes 1081352 | tf_op jit(solution)/shard_map/ppermute | solution.py:38
  6.6 1.1 %collective-permute-start.6 = (f32[16,512]{1,0:T(8,128)S(1)}, f32[16,512]{1,0:T(8,128)S(1)}, u32[]{:S(2)}, u32[]{:S(2)}) collective-permute-start(f32[16,512]{1,0:T(8,128)S(1)} %copy-done.2), channel_id=1, source_target_pairs={{0,2},{1,3},{2,0},{3,1},{4,6},{5,7},{6,4},{7,5},{8,10},{9,11},{10,... | collective-permute-start | bytes 98312 | tf_op jit(solution)/shard_map/ppermute | solution.py:38
  7.7 1.5 %collective-permute-start = (f32[3,16,512]{2,1,0:T(8,128)S(1)}, f32[3,16,512]{2,1,0:T(8,128)S(1)}, u32[]{:S(2)}, u32[]{:S(2)}) collective-permute-start(f32[3,16,512]{2,1,0:T(8,128)S(1)} %get-tuple-element.35), channel_id=1, source_target_pairs={{0,4},{4,0},{8,12},{12,8},{16,20},{20,16},{24,28},{28,24},{1,5},{5... | collective-permute-start | bytes 294920 | tf_op jit(solution)/shard_map/ppermute | solution.py:38
  9.2 12.8 %collective-permute-done.6.refs_10_.refs_3_ = f32[16,512]{1,0:T(8,128)S(1)} collective-permute-done((f32[16,512]{1,0:T(8,128)S(1)}, f32[16,512]{1,0:T(8,128)S(1)}, u32[]{:S(2)}, u32[]{:S(2)}) %collective-permute-start.6) | collective-permute-done | bytes 32800 | tf_op jit(solution)/shard_map/ppermute | solution.py:38
  23.3 3.3 %table.1 = (bf16[1024,1024]{1,0:T(8,128)(2,1)S(1)}, bf16[1024,1024]{1,0:T(8,128)(2,1)S(1)}, bf16[1024,1024]{1,0:T(8,128)(2,1)S(1)}, bf16[1024,1024]{1,0:T(8,128)(2,1)S(1)}) custom-call(), custom_call_target="tpu_custom_call" | custom-call | flops 62914560 | bytes 8388608 | tf_op jit(solution)/shard_map/table/pallas_call | solution.py:246
  26.5 2.2 %stencil.1 = (f32[64,16,512]{2,1,0:T(8,128)}, f32[16,16,512]{2,1,0:T(8,128)S(1)}, f32[5,16,512]{2,1,0:T(8,128)S(1)}, f32[5,16,512]{2,1,0:T(8,128)S(1)}, f32[5,16,512]{2,1,0:T(8,128)S(1)}) custom-call(f32[64,16,512]{2,1,0:T(8,128)S(1)} %copy-done, f32[64,16,512]{2,1,0:T(8,128)S(1)} %copy-done.1, f32[3,16,512]{2,1,0:T(8,128)S(1)} %collective-permute-done.refs_2_, ...), custom_call_target="tpu_custom_call" | custom-call | flops 10485760 | bytes 8388608 | tf_op jit(solution)/shard_map/stencil/pallas_call | solution.py:173
  28.9 2.3 %collective-permute-start.3 = (f32[5,16,512]{2,1,0:T(8,128)S(1)}, f32[5,16,512]{2,1,0:T(8,128)S(1)}, u32[]{:S(2)}, u32[]{:S(2)}) collective-permute-start(f32[5,16,512]{2,1,0:T(8,128)S(1)} %get-tuple-element.40), channel_id=1, source_target_pairs={{0,2},{1,3},{2,0},{3,1},{4,6},{5,7},{6,4},{7,5},{8,10},{9,11},{10,... | collective-permute-start | bytes 491528 | tf_op jit(solution)/shard_map/ppermute | solution.py:38
  31.3 3.9 %transform_a.1 = (f32[11,16,512]{2,1,0:T(8,128)S(1)}, f32[11,16,512]{2,1,0:T(8,128)S(1)}, f32[11,16,512]{2,1,0:T(8,128)S(1)}, f32[11,16,512]{2,1,0:T(8,128)S(1)}, f32[2,4,16,512]{3,2,1,0:T(8,128)S(1)}) custom-call(f32[16,16,512]{2,1,0:T(8,128)S(1)} %get-tuple-element.38.refs_0_, f32[11,16,512]{2,1,0:T(8,128)S(1)} %collective-permute-done.8.refs_1_, ...), custom_call_target="tpu_custom_call" | custom-call | flops 2214592512 | bytes 8388608 | tf_op jit(solution)/shard_map/transform_a/pallas_call | solution.py:358
  35.2 1.1 %collective-permute-done.3.refs_2_ = f32[5,16,512]{2,1,0:T(8,128)S(1)} collective-permute-done((f32[5,16,512]{2,1,0:T(8,128)S(1)}, f32[5,16,512]{2,1,0:T(8,128)S(1)}, u32[]{:S(2)}, u32[]{:S(2)}) %collective-permute-start.3) | collective-permute-done | bytes 163872 | tf_op jit(solution)/shard_map/ppermute | solution.py:38
  36.2 3.0 %collective-permute-done.4.refs_3_ = f32[5,16,512]{2,1,0:T(8,128)S(1)} collective-permute-done((f32[5,16,512]{2,1,0:T(8,128)S(1)}, f32[5,16,512]{2,1,0:T(8,128)S(1)}, u32[]{:S(2)}, u32[]{:S(2)}) %collective-permute-start.4) | collective-permute-done | bytes 163872 | tf_op jit(solution)/shard_map/ppermute | solution.py:38
  39.2 2.5 %transform_b.1 = (f32[5,16,512]{2,1,0:T(8,128)S(1)}, f32[5,16,512]{2,1,0:T(8,128)S(1)}, f32[5,16,512]{2,1,0:T(8,128)S(1)}, f32[5,16,512]{2,1,0:T(8,128)S(1)}, f3...) custom-call(f32[16,16,512]{2,1,0:T(8,128)S(1)} %get-tuple-element.38.refs_0_, ...), custom_call_target="tpu_custom_call" | custom-call | flops 1006632960 | bytes 8388608 | tf_op jit(solution)/shard_map/transform_b/pallas_call | solution.py:358
  42.4 1.7 %collective-permute-start.20 = (f32[11,16,512]{2,1,0:T(8,128)S(1)}, f32[11,16,512]{2,1,0:T(8,128)S(1)}, u32[]{:S(2)}, u32[]{:S(2)}) collective-permute-start(f32[11,16,512]{2,1,0:T(8,128)S(1)} %get-tuple-element.59), channel_id=1, source_target_pairs={{0,2},{1,3},{2,0},{3,1},{4,6},{5,7},{6,4},{7,5},{8,10},{9,11},{10,... | collective-permute-start | bytes 1081352 | tf_op jit(solution)/shard_map/ppermute | solution.py:38
  45.4 9.6 %collective-permute-done.12.refs_1_ = f32[1,2,16,512]{3,2,1,0:T(8,128)S(1)} collective-permute-done((f32[1,2,16,512]{3,2,1,0:T(8,128)S(1)}, f32[1,2,16,512]{3,2,1,0:T(8,128)S(1)}, u32[]{:S(2)}, u32[]{:S(2)}) %collective-permute-start.12) | collective-permute-done | bytes 65568 | tf_op jit(solution)/shard_map/ppermute | solution.py:38
  55.1 9.2 %collective-permute-start.15 = (f32[2,16,512]{2,1,0:T(8,128)S(1)}, f32[2,16,512]{2,1,0:T(8,128)S(1)}, u32[]{:S(2)}, u32[]{:S(2)}) collective-permute-start(f32[2,16,512]{2,1,0:T(8,128)S(1)} %shard_map.59.refs_1_), channel_id=1, source_target_pairs={{0,12},{4,8},{8,4},{12,0},{16,28},{20,24},{24,20},{28,16},{1,13},{... | collective-permute-start | bytes 196616 | tf_op jit(solution)/shard_map/ppermute | solution.py:38
  64.7 1.8 %collective-permute-done.15.refs_4_ = f32[2,16,512]{2,1,0:T(8,128)S(1)} collective-permute-done((f32[2,16,512]{2,1,0:T(8,128)S(1)}, f32[2,16,512]{2,1,0:T(8,128)S(1)}, u32[]{:S(2)}, u32[]{:S(2)}) %collective-permute-start.15) | collective-permute-done | bytes 65568 | tf_op jit(solution)/shard_map/ppermute | solution.py:38
  66.5 1.9 %collective-permute-start.13 = (f32[2,16,512]{2,1,0:T(8,128)S(1)}, f32[2,16,512]{2,1,0:T(8,128)S(1)}, u32[]{:S(2)}, u32[]{:S(2)}) collective-permute-start(f32[2,16,512]{2,1,0:T(8,128)S(1)} %shard_map.59.refs_1_), channel_id=1, source_target_pairs={{0,4},{4,0},{8,12},{12,8},{16,20},{20,16},{24,28},{28,24},{1,5},{5... | collective-permute-start | bytes 196616 | tf_op jit(solution)/shard_map/ppermute | solution.py:38
  68.6 1.5 %collective-permute-start.17 = (f32[5,16,512]{2,1,0:T(8,128)S(1)}, f32[5,16,512]{2,1,0:T(8,128)S(1)}, u32[]{:S(2)}, u32[]{:S(2)}) collective-permute-start(f32[5,16,512]{2,1,0:T(8,128)S(1)} %get-tuple-element.55), channel_id=1, source_target_pairs={{0,2},{1,3},{2,0},{3,1},{4,6},{5,7},{6,4},{7,5},{8,10},{9,11},{10,... | collective-permute-start | bytes 491528 | tf_op jit(solution)/shard_map/ppermute | solution.py:38
  70.9 3.1 %collective-permute-start.16 = (f32[2,16,512]{2,1,0:T(8,128)S(1)}, f32[2,16,512]{2,1,0:T(8,128)S(1)}, u32[]{:S(2)}, u32[]{:S(2)}) collective-permute-start(f32[2,16,512]{2,1,0:T(8,128)S(1)} %get-tuple-element.53.refs_1_), channel_id=1, source_target_pairs={{0,16},{4,20},{8,24},{12,28},{16,0},{20,4},{24,8},{28,12},{1,17},{... | collective-permute-start | bytes 196616 | tf_op jit(solution)/shard_map/ppermute | solution.py:38
  74.0 1.3 %gather.1 = (f32[64,16,512]{2,1,0:T(8,128)S(1)}, f32[64,16,512]{2,1,0:T(8,128)}) custom-call(f32[11,16,512]{2,1,0:T(8,128)S(1)} %get-tuple-element.57.refs_0_, f32[11,16,512]{2,1,0:T(8,128)S(1)} %collective-permute-done.19.refs_1_, f32[11,16,512]{2,1,0:T(8,128)S(1)} %collective-permute-done.20.refs_2_, f32[11,16,512]{2,1,0:T(8,128)S(1)} %collective-permute-done.21.refs_3_, ...), custom_call_target="tpu_custom_call" | custom-call | flops 524288 | bytes 4194304 | tf_op jit(solution)/shard_map/gather/pallas_call | solution.py:523
  75.3 2.0 %collective-permute-done.18.refs_5_ = f32[5,16,512]{2,1,0:T(8,128)S(1)} collective-permute-done((f32[5,16,512]{2,1,0:T(8,128)S(1)}, f32[5,16,512]{2,1,0:T(8,128)S(1)}, u32[]{:S(2)}, u32[]{:S(2)}) %collective-permute-start.18) | collective-permute-done | bytes 163872 | tf_op jit(solution)/shard_map/ppermute | solution.py:38
  77.3 1.8 %solve.1 = (f32[64,16,512]{2,1,0:T(8,128)S(1)}, f32[64,16,512]{2,1,0:T(8,128)}, f32[64,16,512]{2,1,0:T(8,128)}) custom-call(f32[16,512]{1,0:T(8,128)S(1)} %copy-done.2, f32[2,16,512]{2,1,0:T(8,128)S(1)} %get-tuple-element.53.refs_1_, f32[2,16,512]{2,1,0:T(8,128)S(1)} %collective-permute-done.16.refs_2_, ...), custom_call_target="tpu_custom_call", output_to_operand_aliasing={{0}: (6, {}), {1}: (7, {})} | custom-call | flops 2621440 | bytes 6291456 | tf_op jit(solution)/shard_map/solve/pallas_call | solution.py:596
  (39 shorter events, 5.2 us)
Async XLA Ops:
  2.1 4.4 %copy-start.2 = (f32[16,512]{1,0:T(8,128)S(1)}, f32[16,512]{1,0:T(8,128)}, u32[]{:S(2)}) copy-start(f32[16,512]{1,0:T(8,128)} %refs_0_.9) | copy-start | bytes 98308
  2.1 29.1 %collective-permute-start.10 = (f32[11,16,512]{2,1,0:T(8,128)S(1)}, f32[11,16,512]{2,1,0:T(8,128)S(1)}, u32[]{:S(2)}, u32[]{:S(2)}) collective-permute-start(f32[11,16,512]{2,1,0:T(8,128)S(1)} %first.1), channel_id=1, source_target_pairs={{0,3},{1,2},{2,1},{3,0},{4,7},{5,6},{6,5},{7,4},{8,11},{9,10},{10,... | collective-permute-start | bytes 1081352 | tf_op jit(solution)/shard_map/ppermute | solution.py:38
  4.9 26.4 %collective-permute-start.8 = (f32[11,16,512]{2,1,0:T(8,128)S(1)}, f32[11,16,512]{2,1,0:T(8,128)S(1)}, u32[]{:S(2)}, u32[]{:S(2)}) collective-permute-start(f32[11,16,512]{2,1,0:T(8,128)S(1)} %get-tuple-element.46), channel_id=1, source_target_pairs={{0,1},{1,0},{2,3},{3,2},{4,5},{5,4},{6,7},{7,6},{8,9},{9,8},{10,11... | collective-permute-start | bytes 1081352 | tf_op jit(solution)/shard_map/ppermute | solution.py:38
  5.7 25.6 %collective-permute-start.9 = (f32[11,16,512]{2,1,0:T(8,128)S(1)}, f32[11,16,512]{2,1,0:T(8,128)S(1)}, u32[]{:S(2)}, u32[]{:S(2)}) collective-permute-start(f32[11,16,512]{2,1,0:T(8,128)S(1)} %get-tuple-element.47), channel_id=1, source_target_pairs={{0,2},{1,3},{2,0},{3,1},{4,6},{5,7},{6,4},{7,5},{8,10},{9,11},{10,... | collective-permute-start | bytes 1081352 | tf_op jit(solution)/shard_map/ppermute | solution.py:38
  6.6 15.5 %collective-permute-start.6 = (f32[16,512]{1,0:T(8,128)S(1)}, f32[16,512]{1,0:T(8,128)S(1)}, u32[]{:S(2)}, u32[]{:S(2)}) collective-permute-start(f32[16,512]{1,0:T(8,128)S(1)} %copy-done.2), channel_id=1, source_target_pairs={{0,2},{1,3},{2,0},{3,1},{4,6},{5,7},{6,4},{7,5},{8,10},{9,11},{10,... | collective-permute-start | bytes 98312 | tf_op jit(solution)/shard_map/ppermute | solution.py:38
  7.7 15.0 %collective-permute-start = (f32[3,16,512]{2,1,0:T(8,128)S(1)}, f32[3,16,512]{2,1,0:T(8,128)S(1)}, u32[]{:S(2)}, u32[]{:S(2)}) collective-permute-start(f32[3,16,512]{2,1,0:T(8,128)S(1)} %get-tuple-element.35), channel_id=1, source_target_pairs={{0,4},{4,0},{8,12},{12,8},{16,20},{20,16},{24,28},{28,24},{1,5},{5... | collective-permute-start | bytes 294920 | tf_op jit(solution)/shard_map/ppermute | solution.py:38
  22.0 0.8 collective-permute-start.1
  22.7 6.0 %collective-permute-start.5 = (f32[16,512]{1,0:T(8,128)S(1)}, f32[16,512]{1,0:T(8,128)S(1)}, u32[]{:S(2)}, u32[]{:S(2)}) collective-permute-start(f32[16,512]{1,0:T(8,128)S(1)} %copy-done.2), channel_id=1, source_target_pairs={{0,1},{1,0},{2,3},{3,2},{4,5},{5,4},{6,7},{7,6},{8,9},{9,8},{10,11... | collective-permute-start | bytes 98312 | tf_op jit(solution)/shard_map/ppermute | solution.py:38
  22.8 6.1 %collective-permute-start.7 = (f32[16,512]{1,0:T(8,128)S(1)}, f32[16,512]{1,0:T(8,128)S(1)}, u32[]{:S(2)}, u32[]{:S(2)}) collective-permute-start(f32[16,512]{1,0:T(8,128)S(1)} %collective-permute-done.6.refs_10_.refs_3_), channel_id=1, source_target_pairs={{0,1},{1,0},{2,3},{3,2},{4,5},{5,4},{6,7},{7,6},{8,9},{9,8},{10,11... | collective-permute-start | bytes 98312 | tf_op jit(solution)/shard_map/ppermute | solution.py:38
  28.7 6.4 %collective-permute-start.2 = (f32[5,16,512]{2,1,0:T(8,128)S(1)}, f32[5,16,512]{2,1,0:T(8,128)S(1)}, u32[]{:S(2)}, u32[]{:S(2)}) collective-permute-start(f32[5,16,512]{2,1,0:T(8,128)S(1)} %get-tuple-element.39), channel_id=1, source_target_pairs={{0,1},{1,0},{2,3},{3,2},{4,5},{5,4},{6,7},{7,6},{8,9},{9,8},{10,11... | collective-permute-start | bytes 491528 | tf_op jit(solution)/shard_map/ppermute | solution.py:38
  28.9 7.4 %collective-permute-start.3 = (f32[5,16,512]{2,1,0:T(8,128)S(1)}, f32[5,16,512]{2,1,0:T(8,128)S(1)}, u32[]{:S(2)}, u32[]{:S(2)}) collective-permute-start(f32[5,16,512]{2,1,0:T(8,128)S(1)} %get-tuple-element.40), channel_id=1, source_target_pairs={{0,2},{1,3},{2,0},{3,1},{4,6},{5,7},{6,4},{7,5},{8,10},{9,11},{10,... | collective-permute-start | bytes 491528 | tf_op jit(solution)/shard_map/ppermute | solution.py:38
  31.2 8.0 %collective-permute-start.4 = (f32[5,16,512]{2,1,0:T(8,128)S(1)}, f32[5,16,512]{2,1,0:T(8,128)S(1)}, u32[]{:S(2)}, u32[]{:S(2)}) collective-permute-start(f32[5,16,512]{2,1,0:T(8,128)S(1)} %get-tuple-element.41), channel_id=1, source_target_pairs={{0,3},{1,2},{2,1},{3,0},{4,7},{5,6},{6,5},{7,4},{8,11},{9,10},{10,... | collective-permute-start | bytes 491528 | tf_op jit(solution)/shard_map/ppermute | solution.py:38
  41.7 2.4 %collective-permute-start.11 = (f32[2,2,16,512]{3,2,1,0:T(8,128)S(1)}, f32[2,2,16,512]{3,2,1,0:T(8,128)S(1)}, u32[]{:S(2)}, u32[]{:S(2)}) collective-permute-start(f32[2,2,16,512]{3,2,1,0:T(8,128)S(1)} %get-tuple-element.50), channel_id=1, source_target_pairs={{0,1},{1,0},{2,3},{3,2},{4,5},{5,4},{6,7},{7,6},{8,9},{9,8},{10,11... | collective-permute-start | bytes 393224 | tf_op jit(solution)/shard_map/ppermute | solution.py:38
  41.8 29.1 %collective-permute-start.19 = (f32[11,16,512]{2,1,0:T(8,128)S(1)}, f32[11,16,512]{2,1,0:T(8,128)S(1)}, u32[]{:S(2)}, u32[]{:S(2)}) collective-permute-start(f32[11,16,512]{2,1,0:T(8,128)S(1)} %get-tuple-element.58), channel_id=1, source_target_pairs={{0,1},{1,0},{2,3},{3,2},{4,5},{5,4},{6,7},{7,6},{8,9},{9,8},{10,11... | collective-permute-start | bytes 1081352 | tf_op jit(solution)/shard_map/ppermute | solution.py:38
  42.2 22.1 %collective-permute-start.22 = (f32[5,16,512]{2,1,0:T(8,128)S(1)}, f32[5,16,512]{2,1,0:T(8,128)S(1)}, u32[]{:S(2)}, u32[]{:S(2)}) collective-permute-start(f32[5,16,512]{2,1,0:T(8,128)S(1)} %get-tuple-element.62), channel_id=1, source_target_pairs={{0,1},{1,0},{2,3},{3,2},{4,5},{5,4},{6,7},{7,6},{8,9},{9,8},{10,11... | collective-permute-start | bytes 491528 | tf_op jit(solution)/shard_map/ppermute | solution.py:38
  42.4 31.6 %collective-permute-start.20 = (f32[11,16,512]{2,1,0:T(8,128)S(1)}, f32[11,16,512]{2,1,0:T(8,128)S(1)}, u32[]{:S(2)}, u32[]{:S(2)}) collective-permute-start(f32[11,16,512]{2,1,0:T(8,128)S(1)} %get-tuple-element.59), channel_id=1, source_target_pairs={{0,2},{1,3},{2,0},{3,1},{4,6},{5,7},{6,4},{7,5},{8,10},{9,11},{10,... | collective-permute-start | bytes 1081352 | tf_op jit(solution)/shard_map/ppermute | solution.py:38
  44.1 10.9 %collective-permute-start.12 = (f32[1,2,16,512]{3,2,1,0:T(8,128)S(1)}, f32[1,2,16,512]{3,2,1,0:T(8,128)S(1)}, u32[]{:S(2)}, u32[]{:S(2)}) collective-permute-start(f32[1,2,16,512]{3,2,1,0:T(8,128)S(1)} %get-tuple-element.52), channel_id=1, source_target_pairs={{0,2},{1,3},{2,0},{3,1},{4,6},{5,7},{6,4},{7,5},{8,10},{9,11},{10,... | collective-permute-start | bytes 196616 | tf_op jit(solution)/shard_map/ppermute | solution.py:38
  44.7 29.3 %collective-permute-start.21 = (f32[11,16,512]{2,1,0:T(8,128)S(1)}, f32[11,16,512]{2,1,0:T(8,128)S(1)}, u32[]{:S(2)}, u32[]{:S(2)}) collective-permute-start(f32[11,16,512]{2,1,0:T(8,128)S(1)} %get-tuple-element.60), channel_id=1, source_target_pairs={{0,3},{1,2},{2,1},{3,0},{4,7},{5,6},{6,5},{7,4},{8,11},{9,10},{10,... | collective-permute-start | bytes 1081352 | tf_op jit(solution)/shard_map/ppermute | solution.py:38
  55.1 11.5 %collective-permute-start.15 = (f32[2,16,512]{2,1,0:T(8,128)S(1)}, f32[2,16,512]{2,1,0:T(8,128)S(1)}, u32[]{:S(2)}, u32[]{:S(2)}) collective-permute-start(f32[2,16,512]{2,1,0:T(8,128)S(1)} %shard_map.59.refs_1_), channel_id=1, source_target_pairs={{0,12},{4,8},{8,4},{12,0},{16,28},{20,24},{24,20},{28,16},{1,13},{... | collective-permute-start | bytes 196616 | tf_op jit(solution)/shard_map/ppermute | solution.py:38
  64.3 4.3 %collective-permute-start.14 = (f32[2,16,512]{2,1,0:T(8,128)S(1)}, f32[2,16,512]{2,1,0:T(8,128)S(1)}, u32[]{:S(2)}, u32[]{:S(2)}) collective-permute-start(f32[2,16,512]{2,1,0:T(8,128)S(1)} %shard_map.59.refs_1_), channel_id=1, source_target_pairs={{0,8},{4,12},{8,0},{12,4},{16,24},{20,28},{24,16},{28,20},{1,9},{5... | collective-permute-start | bytes 196616 | tf_op jit(solution)/shard_map/ppermute | solution.py:38
  66.5 4.3 %collective-permute-start.13 = (f32[2,16,512]{2,1,0:T(8,128)S(1)}, f32[2,16,512]{2,1,0:T(8,128)S(1)}, u32[]{:S(2)}, u32[]{:S(2)}) collective-permute-start(f32[2,16,512]{2,1,0:T(8,128)S(1)} %shard_map.59.refs_1_), channel_id=1, source_target_pairs={{0,4},{4,0},{8,12},{12,8},{16,20},{20,16},{24,28},{28,24},{1,5},{5... | collective-permute-start | bytes 196616 | tf_op jit(solution)/shard_map/ppermute | solution.py:38
  68.6 6.7 %collective-permute-start.17 = (f32[5,16,512]{2,1,0:T(8,128)S(1)}, f32[5,16,512]{2,1,0:T(8,128)S(1)}, u32[]{:S(2)}, u32[]{:S(2)}) collective-permute-start(f32[5,16,512]{2,1,0:T(8,128)S(1)} %get-tuple-element.55), channel_id=1, source_target_pairs={{0,2},{1,3},{2,0},{3,1},{4,6},{5,7},{6,4},{7,5},{8,10},{9,11},{10,... | collective-permute-start | bytes 491528 | tf_op jit(solution)/shard_map/ppermute | solution.py:38
  70.8 6.5 %collective-permute-start.18 = (f32[5,16,512]{2,1,0:T(8,128)S(1)}, f32[5,16,512]{2,1,0:T(8,128)S(1)}, u32[]{:S(2)}, u32[]{:S(2)}) collective-permute-start(f32[5,16,512]{2,1,0:T(8,128)S(1)} %get-tuple-element.56), channel_id=1, source_target_pairs={{0,3},{1,2},{2,1},{3,0},{4,7},{5,6},{6,5},{7,4},{8,11},{9,10},{10,... | collective-permute-start | bytes 491528 | tf_op jit(solution)/shard_map/ppermute | solution.py:38
  70.9 6.4 %collective-permute-start.16 = (f32[2,16,512]{2,1,0:T(8,128)S(1)}, f32[2,16,512]{2,1,0:T(8,128)S(1)}, u32[]{:S(2)}, u32[]{:S(2)}) collective-permute-start(f32[2,16,512]{2,1,0:T(8,128)S(1)} %get-tuple-element.53.refs_1_), channel_id=1, source_target_pairs={{0,16},{4,20},{8,24},{12,28},{16,0},{20,4},{24,8},{28,12},{1,17},{... | collective-permute-start | bytes 196616 | tf_op jit(solution)/shard_map/ppermute | solution.py:38
  (2 other events, 8.0 us)

commit v4 on v3

--- a/solution.py
+++ b/solution.py
@@ -439,11 +439,13 @@
     count = 1 << len(groups[stage])
     ends, rest = refs[:count], refs[count:]
     entry = rest[0] if stage else None
-    outs = rest[-2:]
+    final = stage == len(groups) - 1
+    outs = rest[-1:] if final else rest[-2:]
 
     def put(at, union, entered):
-        outs[0][0, :, at], outs[0][1, :, at] = union
-        outs[1][0, :, at], outs[1][1, :, at] = entered
+        if not final:
+            outs[1][0, :, at], outs[1][1, :, at] = union
+        outs[0][0, :, at], outs[0][1, :, at] = entered
 
     combine_tiles(groups, stage, block, idx, damping, ends, entry, put)
 
@@ -451,11 +453,12 @@
 def combined(groups, stage, block, damping, ends, entry):
     pair = jax.ShapeDtypeStruct((2,) + damping.shape, F32)
     extra = [entry] if stage else []
+    outs = [pair] if stage == len(groups) - 1 else [pair, pair]
     return pl.pallas_call(
         at_device(combine_kernel, groups, stage, block),
-        out_shape=[pair, pair],
+        out_shape=outs,
         in_specs=vmem(1 + len(ends) + len(extra)),
-        out_specs=vmem(2),
+        out_specs=vmem(len(outs)),
         compiler_params=params(),
         cost_estimate=pl.CostEstimate(flops=100 * damping.size, bytes_accessed=32 * damping.size, transcendentals=0),
     )(damping, *ends, *extra)
@@ -532,16 +535,9 @@
     )(*[pieces[k] for k in chosen])
 
 
-def solve_kernel(fold, groups, cuts, chosen, idx, damping, *refs):
-    stage = len(groups) - 1
-    count = 1 << len(groups[stage])
-    ends, rest = refs[:count], refs[count:]
-    if stage:
-        entry, rest = rest[0], rest[1:]
-    else:
-        entry = None
-    pieces, rest = rest[: len(chosen)], rest[len(chosen) :]
-    _, _, coefficients, coefficients_out, pressure_out, pressure, entered, c_sems, p_sems = rest
+def solve_kernel(fold, cuts, chosen, idx, damping, entered, *refs):
+    pieces, rest = refs[: len(chosen)], refs[len(chosen) :]
+    _, _, coefficients, coefficients_out, pressure_out, pressure, c_sems, p_sems = rest
     cells = coefficients.shape[0]
     sub = cells // fold
     places = place(fold, cuts, idx[0], sub)
@@ -552,10 +548,6 @@
         copies.append(pltpu.make_async_copy(coefficients.at[rows], coefficients_out.at[rows], c_sems.at[n]))
         copies[n].start()
 
-    def put(at, union, entry):
-        entered[0, :, at], entered[1, :, at] = entry
-
-    combine_tiles(groups, stage, cells, idx, damping, ends, entry, put)
     width = max(coefficients.shape[2] // 2, LANES)
     for low in range(0, coefficients.shape[2], width):
         lanes = pl.ds(low, width)
@@ -589,18 +581,16 @@
         copy.wait()
 
 
-def solve(fold, groups, cuts, damping, ends, entry, pieces, chosen, gathered, partly):
-    extra = [entry] if len(groups) > 1 else []
-    operands = [damping, *ends, *extra, *[pieces[k] for k in chosen], gathered, partly]
+def solve(fold, cuts, damping, entered, pieces, chosen, gathered, partly):
+    operands = [damping, entered, *[pieces[k] for k in chosen], gathered, partly]
     shape = jax.ShapeDtypeStruct(gathered.shape, F32)
     return pl.pallas_call(
-        at_device(solve_kernel, fold, groups, cuts, chosen),
+        at_device(solve_kernel, fold, cuts, chosen),
         out_shape=[shape] * 3,
         in_specs=vmem(len(operands) - 1) + hbm(1),
         out_specs=vmem(1) + hbm(2),
         scratch_shapes=[
             pltpu.VMEM(gathered.shape, F32),
-            pltpu.VMEM((2,) + damping.shape, F32),
             pltpu.SemaphoreType.DMA((len(chosen),)),
             pltpu.SemaphoreType.DMA((2 * fold,)),
         ],
@@ -646,8 +636,9 @@
     mine, entry = block_ends(fold, sub, damp, *rest[-2:]), None
     for stage, bits in enumerate(groups):
         if stage:
-            mine, entry = combined(groups, stage - 1, cells, damping, ends, entry)
+            entry, mine = combined(groups, stage - 1, cells, damping, ends, entry)
         ends = [mine] + [partner(mine, "gx", o) for o in peers(bits)[1:]]
+    (entered,) = combined(groups, len(groups) - 1, cells, damping, ends, entry)
     late, k = [], 0
     for h in range(2):
         for r in range(fold):
@@ -655,7 +646,7 @@
             k += len(cuts[h][r])
     early = [n for n in range(k) if n not in late]
     gathered, partly = gather(fold, cuts, pieces, early, (cells, planes, cols))
-    coefficients, pressure = solve(fold, groups, cuts, damping, ends, entry, pieces, late, gathered, partly)
+    coefficients, pressure = solve(fold, cuts, damping, entered, pieces, late, gathered, partly)
     return second, coefficients, pressure
 
 

time: 79.8 us -> 83.5 us (1.046)
  waiting for transfers between devices: 31.1 us -> 39.2 us
  starting transfers between devices: 30.4 us -> 26.7 us
    ppermute x22, waiting for transfers between devices: 31.1 us -> 39.2 us  [partner(): return lax.ppermute(x, axis, [(i, i ^ bit) for i in range(count)])]
    ppermute x22, starting transfers between devices: 29.7 us -> 26 us  [partner(): return lax.ppermute(x, axis, [(i, i ^ bit) for i in range(count)])]
  transfers between devices with their start and end apart: 23 -> 23, of which waited for: 8 -> 12; matrix products, arithmetic and copies ran while one was open for 0% -> 0% of each run, Pallas kernels for 14% -> 13%
where the time goes in v4:
time: 83.5 us; the launch traced here: 83.4 us
  waiting for transfers between devices  39.2 us (47%)
  starting transfers between devices  26.7 us (32%)
  Pallas kernels  16.8 us (20%)
    ppermute x22, waiting for transfers between devices, partner(): return lax.ppermute(x, axis, [(i, i ^ bit) for i in range(count)])  39.2 us
    ppermute x22, starting transfers between devices, partner(): return lax.ppermute(x, axis, [(i, i ^ bit) for i in range(count)])  26 us
    pallas_call x2, Pallas kernels, transform(): pl.pallas_call(at_device(transform_kernel, fold, at, sizes, cuts, last),...  6.33 us
    pallas_call x1, Pallas kernels, cosine_tables(): pl.pallas_call(at_device(table_kernel, total, cols, fold, 128), out_shape...  3.25 us
    pallas_call x1, Pallas kernels, stencil(): pl.pallas_call(at_device(stencil_kernel, fold), out_shape=outs, in_specs=...  2.18 us
    pallas_call x1, Pallas kernels, solve(): pl.pallas_call(at_device(solve_kernel, fold, cuts, chosen), out_shape=[sh...  1.71 us
  transfers between devices with their start and end apart: 23, of which 12 were waited for; matrix products, arithmetic and copies ran while one was open for 0% of the time, Pallas kernels for 13%

profile of v4, /device:TPU:0, one launch (start us, length us, event | category | flops | bytes accessed | tf_op | source)
XLA Modules:
  0.0 83.4 jit_solution(12716617869160986969)
XLA Ops:
  0.6 1.5 %first.1 = f32[11,16,512]{2,1,0:T(8,128)S(1)} custom-call(f32[64,16,512]{2,1,0:T(8,128)} %refs_0_.8, f32[64,16,512]{2,1,0:T(8,128)} %refs_1_.5), custom_call_target="tpu_custom_call" | custom-call | flops 901120 | bytes 1081344 | tf_op jit(solution)/shard_map/first/pallas_call | solution.py:84
  2.1 2.5 %collective-permute-start.10 = (f32[11,16,512]{2,1,0:T(8,128)S(1)}, f32[11,16,512]{2,1,0:T(8,128)S(1)}, u32[]{:S(2)}, u32[]{:S(2)}) collective-permute-start(f32[11,16,512]{2,1,0:T(8,128)S(1)} %first.1), channel_id=1, source_target_pairs={{0,3},{1,2},{2,1},{3,0},{4,7},{5,6},{6,5},{7,4},{8,11},{9,10},{10,... | collective-permute-start | bytes 1081352 | tf_op jit(solution)/shard_map/ppermute | solution.py:38
  7.7 1.5 %collective-permute-start = (f32[3,16,512]{2,1,0:T(8,128)S(1)}, f32[3,16,512]{2,1,0:T(8,128)S(1)}, u32[]{:S(2)}, u32[]{:S(2)}) collective-permute-start(f32[3,16,512]{2,1,0:T(8,128)S(1)} %get-tuple-element.35), channel_id=1, source_target_pairs={{0,4},{4,0},{8,12},{12,8},{16,20},{20,16},{24,28},{28,24},{1,5},{5... | collective-permute-start | bytes 294920 | tf_op jit(solution)/shard_map/ppermute | solution.py:38
  9.2 12.8 %collective-permute-done.6.refs_10_.refs_3_ = f32[16,512]{1,0:T(8,128)S(1)} collective-permute-done((f32[16,512]{1,0:T(8,128)S(1)}, f32[16,512]{1,0:T(8,128)S(1)}, u32[]{:S(2)}, u32[]{:S(2)}) %collective-permute-start.6) | collective-permute-done | bytes 32800 | tf_op jit(solution)/shard_map/ppermute | solution.py:38
  23.3 3.3 %table.1 = (bf16[1024,1024]{1,0:T(8,128)(2,1)S(1)}, bf16[1024,1024]{1,0:T(8,128)(2,1)S(1)}, bf16[1024,1024]{1,0:T(8,128)(2,1)S(1)}, bf16[1024,1024]{1,0:T(8,128)(2,1)S(1)}) custom-call(), custom_call_target="tpu_custom_call" | custom-call | flops 62914560 | bytes 8388608 | tf_op jit(solution)/shard_map/table/pallas_call | solution.py:246
  26.5 2.2 %stencil.1 = (f32[64,16,512]{2,1,0:T(8,128)}, f32[16,16,512]{2,1,0:T(8,128)S(1)}, f32[5,16,512]{2,1,0:T(8,128)S(1)}, f32[5,16,512]{2,1,0:T(8,128)S(1)}, f32[5,16,512]{2,1,0:T(8,128)S(1)}) custom-call(f32[64,16,512]{2,1,0:T(8,128)S(1)} %copy-done, f32[64,16,512]{2,1,0:T(8,128)S(1)} %copy-done.1, f32[3,16,512]{2,1,0:T(8,128)S(1)} %collective-permute-done.refs_2_, ...), custom_call_target="tpu_custom_call" | custom-call | flops 10485760 | bytes 8388608 | tf_op jit(solution)/shard_map/stencil/pallas_call | solution.py:173
  28.9 2.3 %collective-permute-start.3 = (f32[5,16,512]{2,1,0:T(8,128)S(1)}, f32[5,16,512]{2,1,0:T(8,128)S(1)}, u32[]{:S(2)}, u32[]{:S(2)}) collective-permute-start(f32[5,16,512]{2,1,0:T(8,128)S(1)} %get-tuple-element.40), channel_id=1, source_target_pairs={{0,2},{1,3},{2,0},{3,1},{4,6},{5,7},{6,4},{7,5},{8,10},{9,11},{10,... | collective-permute-start | bytes 491528 | tf_op jit(solution)/shard_map/ppermute | solution.py:38
  31.3 3.9 %transform_a.1 = (f32[11,16,512]{2,1,0:T(8,128)S(1)}, f32[11,16,512]{2,1,0:T(8,128)S(1)}, f32[11,16,512]{2,1,0:T(8,128)S(1)}, f32[11,16,512]{2,1,0:T(8,128)S(1)}, f32[2,4,16,512]{3,2,1,0:T(8,128)S(1)}) custom-call(f32[16,16,512]{2,1,0:T(8,128)S(1)} %get-tuple-element.38.refs_0_, f32[11,16,512]{2,1,0:T(8,128)S(1)} %collective-permute-done.8.refs_1_, ...), custom_call_target="tpu_custom_call" | custom-call | flops 2214592512 | bytes 8388608 | tf_op jit(solution)/shard_map/transform_a/pallas_call | solution.py:358
  36.2 3.0 %collective-permute-done.4.refs_3_ = f32[5,16,512]{2,1,0:T(8,128)S(1)} collective-permute-done((f32[5,16,512]{2,1,0:T(8,128)S(1)}, f32[5,16,512]{2,1,0:T(8,128)S(1)}, u32[]{:S(2)}, u32[]{:S(2)}) %collective-permute-start.4) | collective-permute-done | bytes 163872 | tf_op jit(solution)/shard_map/ppermute | solution.py:38
  39.2 2.5 %transform_b.1 = (f32[5,16,512]{2,1,0:T(8,128)S(1)}, f32[5,16,512]{2,1,0:T(8,128)S(1)}, f32[5,16,512]{2,1,0:T(8,128)S(1)}, f32[5,16,512]{2,1,0:T(8,128)S(1)}, f3...) custom-call(f32[16,16,512]{2,1,0:T(8,128)S(1)} %get-tuple-element.38.refs_0_, ...), custom_call_target="tpu_custom_call" | custom-call | flops 1006632960 | bytes 8388608 | tf_op jit(solution)/shard_map/transform_b/pallas_call | solution.py:358
  41.8 1.2 %collective-permute-done.11.refs_1_ = f32[2,2,16,512]{3,2,1,0:T(8,128)S(1)} collective-permute-done((f32[2,2,16,512]{3,2,1,0:T(8,128)S(1)}, f32[2,2,16,512]{3,2,1,0:T(8,128)S(1)}, u32[]{:S(2)}, u32[]{:S(2)}) %collective-permute-start.11) | collective-permute-done | bytes 131104 | tf_op jit(solution)/shard_map/ppermute | solution.py:38
  43.1 1.5 %collective-permute-start.12 = (f32[1,2,16,512]{3,2,1,0:T(8,128)S(1)}, f32[1,2,16,512]{3,2,1,0:T(8,128)S(1)}, u32[]{:S(2)}, u32[]{:S(2)}) collective-permute-start(f32[1,2,16,512]{3,2,1,0:T(8,128)S(1)} %get-tuple-element.52), channel_id=1, source_target_pairs={{0,2},{1,3},{2,0},{3,1},{4,6},{5,7},{6,4},{7,5},{8,10},{9,11},{10,... | collective-permute-start | bytes 196616 | tf_op jit(solution)/shard_map/ppermute | solution.py:38
  44.7 2.8 %collective-permute-done.12.refs_1_ = f32[1,2,16,512]{3,2,1,0:T(8,128)S(1)} collective-permute-done((f32[1,2,16,512]{3,2,1,0:T(8,128)S(1)}, f32[1,2,16,512]{3,2,1,0:T(8,128)S(1)}, u32[]{:S(2)}, u32[]{:S(2)}) %collective-permute-start.12) | collective-permute-done | bytes 65568 | tf_op jit(solution)/shard_map/ppermute | solution.py:38
  47.5 9.1 %collective-permute-start.15 = (f32[2,16,512]{2,1,0:T(8,128)S(1)}, f32[2,16,512]{2,1,0:T(8,128)S(1)}, u32[]{:S(2)}, u32[]{:S(2)}) collective-permute-start(f32[2,16,512]{2,1,0:T(8,128)S(1)} %shard_map.59.refs_1_), channel_id=1, source_target_pairs={{0,12},{4,8},{8,4},{12,0},{16,28},{20,24},{24,20},{28,16},{1,13},{... | collective-permute-start | bytes 196616 | tf_op jit(solution)/shard_map/ppermute | solution.py:38
  56.6 1.5 %collective-permute-start.20 = (f32[11,16,512]{2,1,0:T(8,128)S(1)}, f32[11,16,512]{2,1,0:T(8,128)S(1)}, u32[]{:S(2)}, u32[]{:S(2)}) collective-permute-start(f32[11,16,512]{2,1,0:T(8,128)S(1)} %get-tuple-element.59), channel_id=1, source_target_pairs={{0,2},{1,3},{2,0},{3,1},{4,6},{5,7},{6,4},{7,5},{8,10},{9,11},{10,... | collective-permute-start | bytes 1081352 | tf_op jit(solution)/shard_map/ppermute | solution.py:38
  59.2 3.2 %collective-permute-done.14.refs_3_ = f32[2,16,512]{2,1,0:T(8,128)S(1)} collective-permute-done((f32[2,16,512]{2,1,0:T(8,128)S(1)}, f32[2,16,512]{2,1,0:T(8,128)S(1)}, u32[]{:S(2)}, u32[]{:S(2)}) %collective-permute-start.14) | collective-permute-done | bytes 65568 | tf_op jit(solution)/shard_map/ppermute | solution.py:38
  62.9 3.8 %collective-permute-done.13.refs_2_ = f32[2,16,512]{2,1,0:T(8,128)S(1)} collective-permute-done((f32[2,16,512]{2,1,0:T(8,128)S(1)}, f32[2,16,512]{2,1,0:T(8,128)S(1)}, u32[]{:S(2)}, u32[]{:S(2)}) %collective-permute-start.13) | collective-permute-done | bytes 65568 | tf_op jit(solution)/shard_map/ppermute | solution.py:38
  66.7 1.3 %collective-permute-start.16 = (f32[2,16,512]{2,1,0:T(8,128)S(1)}, f32[2,16,512]{2,1,0:T(8,128)S(1)}, u32[]{:S(2)}, u32[]{:S(2)}) collective-permute-start(f32[2,16,512]{2,1,0:T(8,128)S(1)} %get-tuple-element.53.refs_1_), channel_id=1, source_target_pairs={{0,16},{4,20},{8,24},{12,28},{16,0},{20,4},{24,8},{28,12},{1,17},{... | collective-permute-start | bytes 196616 | tf_op jit(solution)/shard_map/ppermute | solution.py:38
  69.2 3.3 %collective-permute-done.16.refs_2_ = f32[2,16,512]{2,1,0:T(8,128)S(1)} collective-permute-done((f32[2,16,512]{2,1,0:T(8,128)S(1)}, f32[2,16,512]{2,1,0:T(8,128)S(1)}, u32[]{:S(2)}, u32[]{:S(2)}) %collective-permute-start.16) | collective-permute-done | bytes 65568 | tf_op jit(solution)/shard_map/ppermute | solution.py:38
  72.6 2.0 %collective-permute-done.21.refs_3_ = f32[11,16,512]{2,1,0:T(8,128)S(1)} collective-permute-done((f32[11,16,512]{2,1,0:T(8,128)S(1)}, f32[11,16,512]{2,1,0:T(8,128)S(1)}, u32[]{:S(2)}, u32[]{:S(2)}) %collective-permute-start.21) | collective-permute-done | bytes 360480 | tf_op jit(solution)/shard_map/ppermute | solution.py:38
  74.7 1.3 %gather.1 = (f32[64,16,512]{2,1,0:T(8,128)S(1)}, f32[64,16,512]{2,1,0:T(8,128)}) custom-call(f32[11,16,512]{2,1,0:T(8,128)S(1)} %get-tuple-element.57.refs_0_, f32[11,16,512]{2,1,0:T(8,128)S(1)} %collective-permute-done.19.refs_1_, f32[11,16,512]{2,1,0:T(8,128)S(1)} %collective-permute-done.20.refs_2_, f32[11,16,512]{2,1,0:T(8,128)S(1)} %collective-permute-done.21.refs_3_, ...), custom_call_target="tpu_custom_call" | custom-call | flops 524288 | bytes 4194304 | tf_op jit(solution)/shard_map/gather/pallas_call | solution.py:526
  75.9 3.1 %collective-permute-done.17.refs_2_ = f32[5,16,512]{2,1,0:T(8,128)S(1)} collective-permute-done((f32[5,16,512]{2,1,0:T(8,128)S(1)}, f32[5,16,512]{2,1,0:T(8,128)S(1)}, u32[]{:S(2)}, u32[]{:S(2)}) %collective-permute-start.17) | collective-permute-done | bytes 163872 | tf_op jit(solution)/shard_map/ppermute | solution.py:38
  79.1 2.6 %collective-permute-done.18.refs_3_ = f32[5,16,512]{2,1,0:T(8,128)S(1)} collective-permute-done((f32[5,16,512]{2,1,0:T(8,128)S(1)}, f32[5,16,512]{2,1,0:T(8,128)S(1)}, u32[]{:S(2)}, u32[]{:S(2)}) %collective-permute-start.18) | collective-permute-done | bytes 163872 | tf_op jit(solution)/shard_map/ppermute | solution.py:38
  81.7 1.7 %solve.1 = (f32[64,16,512]{2,1,0:T(8,128)S(1)}, f32[64,16,512]{2,1,0:T(8,128)}, f32[64,16,512]{2,1,0:T(8,128)}) custom-call(f32[16,512]{1,0:T(8,128)S(1)} %copy-done.2, f32[2,16,512]{2,1,0:T(8,128)S(1)} %shard_map.61.refs_1_, f32[5,16,512]{2,1,0:T(8,128)S(1)} %collective-permute-done.17.refs_2_, ...), custom_call_target="tpu_custom_call", output_to_operand_aliasing={{0}: (4, {}), {1}: (5, {})} | custom-call | flops 2621440 | bytes 6291456 | tf_op jit(solution)/shard_map/solve/pallas_call | solution.py:587
  (40 shorter events, 8.8 us)
Async XLA Ops:
  2.1 4.4 %copy-start.2 = (f32[16,512]{1,0:T(8,128)S(1)}, f32[16,512]{1,0:T(8,128)}, u32[]{:S(2)}) copy-start(f32[16,512]{1,0:T(8,128)} %refs_0_.11) | copy-start | bytes 98308
  2.1 29.1 %collective-permute-start.10 = (f32[11,16,512]{2,1,0:T(8,128)S(1)}, f32[11,16,512]{2,1,0:T(8,128)S(1)}, u32[]{:S(2)}, u32[]{:S(2)}) collective-permute-start(f32[11,16,512]{2,1,0:T(8,128)S(1)} %first.1), channel_id=1, source_target_pairs={{0,3},{1,2},{2,1},{3,0},{4,7},{5,6},{6,5},{7,4},{8,11},{9,10},{10,... | collective-permute-start | bytes 1081352 | tf_op jit(solution)/shard_map/ppermute | solution.py:38
  4.9 26.4 %collective-permute-start.8 = (f32[11,16,512]{2,1,0:T(8,128)S(1)}, f32[11,16,512]{2,1,0:T(8,128)S(1)}, u32[]{:S(2)}, u32[]{:S(2)}) collective-permute-start(f32[11,16,512]{2,1,0:T(8,128)S(1)} %get-tuple-element.46), channel_id=1, source_target_pairs={{0,1},{1,0},{2,3},{3,2},{4,5},{5,4},{6,7},{7,6},{8,9},{9,8},{10,11... | collective-permute-start | bytes 1081352 | tf_op jit(solution)/shard_map/ppermute | solution.py:38
  5.7 25.6 %collective-permute-start.9 = (f32[11,16,512]{2,1,0:T(8,128)S(1)}, f32[11,16,512]{2,1,0:T(8,128)S(1)}, u32[]{:S(2)}, u32[]{:S(2)}) collective-permute-start(f32[11,16,512]{2,1,0:T(8,128)S(1)} %get-tuple-element.47), channel_id=1, source_target_pairs={{0,2},{1,3},{2,0},{3,1},{4,6},{5,7},{6,4},{7,5},{8,10},{9,11},{10,... | collective-permute-start | bytes 1081352 | tf_op jit(solution)/shard_map/ppermute | solution.py:38
  6.6 15.5 %collective-permute-start.6 = (f32[16,512]{1,0:T(8,128)S(1)}, f32[16,512]{1,0:T(8,128)S(1)}, u32[]{:S(2)}, u32[]{:S(2)}) collective-permute-start(f32[16,512]{1,0:T(8,128)S(1)} %copy-done.2), channel_id=1, source_target_pairs={{0,2},{1,3},{2,0},{3,1},{4,6},{5,7},{6,4},{7,5},{8,10},{9,11},{10,... | collective-permute-start | bytes 98312 | tf_op jit(solution)/shard_map/ppermute | solution.py:38
  7.7 15.0 %collective-permute-start = (f32[3,16,512]{2,1,0:T(8,128)S(1)}, f32[3,16,512]{2,1,0:T(8,128)S(1)}, u32[]{:S(2)}, u32[]{:S(2)}) collective-permute-start(f32[3,16,512]{2,1,0:T(8,128)S(1)} %get-tuple-element.35), channel_id=1, source_target_pairs={{0,4},{4,0},{8,12},{12,8},{16,20},{20,16},{24,28},{28,24},{1,5},{5... | collective-permute-start | bytes 294920 | tf_op jit(solution)/shard_map/ppermute | solution.py:38
  22.0 0.8 collective-permute-start.1
  22.7 6.0 %collective-permute-start.5 = (f32[16,512]{1,0:T(8,128)S(1)}, f32[16,512]{1,0:T(8,128)S(1)}, u32[]{:S(2)}, u32[]{:S(2)}) collective-permute-start(f32[16,512]{1,0:T(8,128)S(1)} %copy-done.2), channel_id=1, source_target_pairs={{0,1},{1,0},{2,3},{3,2},{4,5},{5,4},{6,7},{7,6},{8,9},{9,8},{10,11... | collective-permute-start | bytes 98312 | tf_op jit(solution)/shard_map/ppermute | solution.py:38
  22.8 6.1 %collective-permute-start.7 = (f32[16,512]{1,0:T(8,128)S(1)}, f32[16,512]{1,0:T(8,128)S(1)}, u32[]{:S(2)}, u32[]{:S(2)}) collective-permute-start(f32[16,512]{1,0:T(8,128)S(1)} %collective-permute-done.6.refs_10_.refs_3_), channel_id=1, source_target_pairs={{0,1},{1,0},{2,3},{3,2},{4,5},{5,4},{6,7},{7,6},{8,9},{9,8},{10,11... | collective-permute-start | bytes 98312 | tf_op jit(solution)/shard_map/ppermute | solution.py:38
  28.7 6.4 %collective-permute-start.2 = (f32[5,16,512]{2,1,0:T(8,128)S(1)}, f32[5,16,512]{2,1,0:T(8,128)S(1)}, u32[]{:S(2)}, u32[]{:S(2)}) collective-permute-start(f32[5,16,512]{2,1,0:T(8,128)S(1)} %get-tuple-element.39), channel_id=1, source_target_pairs={{0,1},{1,0},{2,3},{3,2},{4,5},{5,4},{6,7},{7,6},{8,9},{9,8},{10,11... | collective-permute-start | bytes 491528 | tf_op jit(solution)/shard_map/ppermute | solution.py:38
  28.9 7.4 %collective-permute-start.3 = (f32[5,16,512]{2,1,0:T(8,128)S(1)}, f32[5,16,512]{2,1,0:T(8,128)S(1)}, u32[]{:S(2)}, u32[]{:S(2)}) collective-permute-start(f32[5,16,512]{2,1,0:T(8,128)S(1)} %get-tuple-element.40), channel_id=1, source_target_pairs={{0,2},{1,3},{2,0},{3,1},{4,6},{5,7},{6,4},{7,5},{8,10},{9,11},{10,... | collective-permute-start | bytes 491528 | tf_op jit(solution)/shard_map/ppermute | solution.py:38
  31.2 8.0 %collective-permute-start.4 = (f32[5,16,512]{2,1,0:T(8,128)S(1)}, f32[5,16,512]{2,1,0:T(8,128)S(1)}, u32[]{:S(2)}, u32[]{:S(2)}) collective-permute-start(f32[5,16,512]{2,1,0:T(8,128)S(1)} %get-tuple-element.41), channel_id=1, source_target_pairs={{0,3},{1,2},{2,1},{3,0},{4,7},{5,6},{6,5},{7,4},{8,11},{9,10},{10,... | collective-permute-start | bytes 491528 | tf_op jit(solution)/shard_map/ppermute | solution.py:38
  41.7 1.4 %collective-permute-start.11 = (f32[2,2,16,512]{3,2,1,0:T(8,128)S(1)}, f32[2,2,16,512]{3,2,1,0:T(8,128)S(1)}, u32[]{:S(2)}, u32[]{:S(2)}) collective-permute-start(f32[2,2,16,512]{3,2,1,0:T(8,128)S(1)} %get-tuple-element.50), channel_id=1, source_target_pairs={{0,1},{1,0},{2,3},{3,2},{4,5},{5,4},{6,7},{7,6},{8,9},{9,8},{10,11... | collective-permute-start | bytes 393224 | tf_op jit(solution)/shard_map/ppermute | solution.py:38
  43.1 4.3 %collective-permute-start.12 = (f32[1,2,16,512]{3,2,1,0:T(8,128)S(1)}, f32[1,2,16,512]{3,2,1,0:T(8,128)S(1)}, u32[]{:S(2)}, u32[]{:S(2)}) collective-permute-start(f32[1,2,16,512]{3,2,1,0:T(8,128)S(1)} %get-tuple-element.52), channel_id=1, source_target_pairs={{0,2},{1,3},{2,0},{3,1},{4,6},{5,7},{6,4},{7,5},{8,10},{9,11},{10,... | collective-permute-start | bytes 196616 | tf_op jit(solution)/shard_map/ppermute | solution.py:38
  47.5 11.3 %collective-permute-start.15 = (f32[2,16,512]{2,1,0:T(8,128)S(1)}, f32[2,16,512]{2,1,0:T(8,128)S(1)}, u32[]{:S(2)}, u32[]{:S(2)}) collective-permute-start(f32[2,16,512]{2,1,0:T(8,128)S(1)} %shard_map.59.refs_1_), channel_id=1, source_target_pairs={{0,12},{4,8},{8,4},{12,0},{16,28},{20,24},{24,20},{28,16},{1,13},{... | collective-permute-start | bytes 196616 | tf_op jit(solution)/shard_map/ppermute | solution.py:38
  56.6 16.0 %collective-permute-start.19 = (f32[11,16,512]{2,1,0:T(8,128)S(1)}, f32[11,16,512]{2,1,0:T(8,128)S(1)}, u32[]{:S(2)}, u32[]{:S(2)}) collective-permute-start(f32[11,16,512]{2,1,0:T(8,128)S(1)} %get-tuple-element.58), channel_id=1, source_target_pairs={{0,1},{1,0},{2,3},{3,2},{4,5},{5,4},{6,7},{7,6},{8,9},{9,8},{10,11... | collective-permute-start | bytes 1081352 | tf_op jit(solution)/shard_map/ppermute | solution.py:38
  56.6 16.0 %collective-permute-start.20 = (f32[11,16,512]{2,1,0:T(8,128)S(1)}, f32[11,16,512]{2,1,0:T(8,128)S(1)}, u32[]{:S(2)}, u32[]{:S(2)}) collective-permute-start(f32[11,16,512]{2,1,0:T(8,128)S(1)} %get-tuple-element.59), channel_id=1, source_target_pairs={{0,2},{1,3},{2,0},{3,1},{4,6},{5,7},{6,4},{7,5},{8,10},{9,11},{10,... | collective-permute-start | bytes 1081352 | tf_op jit(solution)/shard_map/ppermute | solution.py:38
  58.1 4.3 %collective-permute-start.14 = (f32[2,16,512]{2,1,0:T(8,128)S(1)}, f32[2,16,512]{2,1,0:T(8,128)S(1)}, u32[]{:S(2)}, u32[]{:S(2)}) collective-permute-start(f32[2,16,512]{2,1,0:T(8,128)S(1)} %shard_map.59.refs_1_), channel_id=1, source_target_pairs={{0,8},{4,12},{8,0},{12,4},{16,24},{20,28},{24,16},{28,20},{1,9},{5... | collective-permute-start | bytes 196616 | tf_op jit(solution)/shard_map/ppermute | solution.py:38
  58.5 16.1 %collective-permute-start.21 = (f32[11,16,512]{2,1,0:T(8,128)S(1)}, f32[11,16,512]{2,1,0:T(8,128)S(1)}, u32[]{:S(2)}, u32[]{:S(2)}) collective-permute-start(f32[11,16,512]{2,1,0:T(8,128)S(1)} %get-tuple-element.60), channel_id=1, source_target_pairs={{0,3},{1,2},{2,1},{3,0},{4,7},{5,6},{6,5},{7,4},{8,11},{9,10},{10,... | collective-permute-start | bytes 1081352 | tf_op jit(solution)/shard_map/ppermute | solution.py:38
  58.8 9.2 %collective-permute-start.22 = (f32[5,16,512]{2,1,0:T(8,128)S(1)}, f32[5,16,512]{2,1,0:T(8,128)S(1)}, u32[]{:S(2)}, u32[]{:S(2)}) collective-permute-start(f32[5,16,512]{2,1,0:T(8,128)S(1)} %get-tuple-element.62), channel_id=1, source_target_pairs={{0,1},{1,0},{2,3},{3,2},{4,5},{5,4},{6,7},{7,6},{8,9},{9,8},{10,11... | collective-permute-start | bytes 491528 | tf_op jit(solution)/shard_map/ppermute | solution.py:38
  62.4 4.3 %collective-permute-start.13 = (f32[2,16,512]{2,1,0:T(8,128)S(1)}, f32[2,16,512]{2,1,0:T(8,128)S(1)}, u32[]{:S(2)}, u32[]{:S(2)}) collective-permute-start(f32[2,16,512]{2,1,0:T(8,128)S(1)} %shard_map.59.refs_1_), channel_id=1, source_target_pairs={{0,4},{4,0},{8,12},{12,8},{16,20},{20,16},{24,28},{28,24},{1,5},{5... | collective-permute-start | bytes 196616 | tf_op jit(solution)/shard_map/ppermute | solution.py:38
  66.7 5.8 %collective-permute-start.16 = (f32[2,16,512]{2,1,0:T(8,128)S(1)}, f32[2,16,512]{2,1,0:T(8,128)S(1)}, u32[]{:S(2)}, u32[]{:S(2)}) collective-permute-start(f32[2,16,512]{2,1,0:T(8,128)S(1)} %get-tuple-element.53.refs_1_), channel_id=1, source_target_pairs={{0,16},{4,20},{8,24},{12,28},{16,0},{20,4},{24,8},{28,12},{1,17},{... | collective-permute-start | bytes 196616 | tf_op jit(solution)/shard_map/ppermute | solution.py:38
  68.0 11.1 %collective-permute-start.17 = (f32[5,16,512]{2,1,0:T(8,128)S(1)}, f32[5,16,512]{2,1,0:T(8,128)S(1)}, u32[]{:S(2)}, u32[]{:S(2)}) collective-permute-start(f32[5,16,512]{2,1,0:T(8,128)S(1)} %get-tuple-element.55), channel_id=1, source_target_pairs={{0,2},{1,3},{2,0},{3,1},{4,6},{5,7},{6,4},{7,5},{8,10},{9,11},{10,... | collective-permute-start | bytes 491528 | tf_op jit(solution)/shard_map/ppermute | solution.py:38
  72.5 9.2 %collective-permute-start.18 = (f32[5,16,512]{2,1,0:T(8,128)S(1)}, f32[5,16,512]{2,1,0:T(8,128)S(1)}, u32[]{:S(2)}, u32[]{:S(2)}) collective-permute-start(f32[5,16,512]{2,1,0:T(8,128)S(1)} %get-tuple-element.56), channel_id=1, source_target_pairs={{0,3},{1,2},{2,1},{3,0},{4,7},{5,6},{6,5},{7,4},{8,11},{9,10},{10,... | collective-permute-start | bytes 491528 | tf_op jit(solution)/shard_map/ppermute | solution.py:38
  (2 other events, 8.0 us)
